TPU v7x, 16 devices: a 4x2x1 block of a 4x4x8 slice. The times are simulated.
16 devices in a mesh: dp: 2 (over y, z), tp: 8 (over x, core).
Axes of the slice: x: 4, y: 2, z: 1, core: 2. Of those that a mesh axis runs over, the one named last changes fastest.
The devices are a block of a 4x4x8 slice.
Arguments:
- y_one: float32 [16, 256, 1408], P('dp'), parts along dimension 0
- y_two: float32 [16, 256, 1408], P('dp'), parts along dimension 0
- dy_one: float32 [16, 256, 1408], P('dp'), parts along dimension 0
- dy_two: float32 [16, 256, 1408], P('dp'), parts along dimension 0
- saved_one: float32 [1, 16, 256, 1408], P(None, 'dp'), parts along dimension 1
- saved_two: float32 [1, 16, 256, 1408], P(None, 'dp'), parts along dimension 1
- w_qkv: bfloat16 [3, 1408, 3, 16, 88], P(None, None, None, 'tp')
- w_o: bfloat16 [3, 16, 88, 1408], P(None, 'tp')
- w_in: bfloat16 [3, 1408, 6144], P(None, None, 'tp')
- w_out: bfloat16 [3, 6144, 1408], P(None, 'tp')
Outputs:
- output 1: float32 [16, 256, 1408], P('dp'), parts along dimension 0
- output 2: float32 [16, 256, 1408], P('dp'), parts along dimension 0
- output 3: float32 [16, 256, 1408], P('dp'), parts along dimension 0
- output 4: float32 [16, 256, 1408], P('dp'), parts along dimension 0
- output 5: float32 [6, 1408, 3, 16, 88], P('dp', None, None, 'tp'), parts along dimension 0
- output 6: float32 [6, 16, 88, 1408], P('dp', 'tp'), parts along dimension 0
- output 7: float32 [6, 1408, 6144], P('dp', None, 'tp'), parts along dimension 0
- output 8: float32 [6, 6144, 1408], P('dp', 'tp'), parts along dimension 0
There are 2 independent parts. A program takes and returns all parts, laid end to end along the dimension named above; an argument that names none is the same for every part.
All inputs are finite; a program needn't handle non-finite values.
Results may differ from a plain program's by a relative error of at most 0.012256.
Values are sent between devices in bfloat16 or wider.
A program may use at most 768 MiB of HBM per device.

v0:
```python
import jax
import jax.numpy as jnp
from jax import lax
from jax.sharding import PartitionSpec as P

EPS = 1e-6


def rms_norm(state):
    return state * lax.rsqrt(jnp.mean(state * state, axis=-1, keepdims=True) + EPS)


def gelu_tanh(hidden):
    return jax.nn.gelu(hidden, approximate=True)


def attn_forward(normed, w_qkv):
    head_dim = w_qkv.shape[-1]
    qkv_all = jnp.einsum("bsh,hkne->kbsne", normed, w_qkv, preferred_element_type=jnp.float32).astype(jnp.bfloat16)
    scores = jnp.einsum("bqne,bkne->bnqk", qkv_all[0], qkv_all[1], preferred_element_type=jnp.float32) * head_dim ** -0.5
    attn_probs = jax.nn.softmax(scores, axis=-1)
    probs_bf = attn_probs.astype(jnp.bfloat16)
    heads_out = jnp.einsum("bnqk,bkne->bqne", probs_bf, qkv_all[2], preferred_element_type=jnp.float32).astype(jnp.bfloat16)
    return qkv_all, attn_probs, probs_bf, heads_out


def attn_backward(normed, w_qkv, w_o, attn_cache, d_out):
    qkv_all, attn_probs, probs_bf, heads_out = attn_cache
    head_dim = w_qkv.shape[-1]
    d_bf = d_out.astype(jnp.bfloat16)
    d_wo = jnp.einsum("bqne,bqh->neh", heads_out, d_bf, preferred_element_type=jnp.float32)
    d_heads = jnp.einsum("bqh,neh->bqne", d_bf, w_o, preferred_element_type=jnp.float32).astype(jnp.bfloat16)
    d_v = jnp.einsum("bnqk,bqne->bkne", probs_bf, d_heads, preferred_element_type=jnp.float32)
    d_probs = jnp.einsum("bqne,bkne->bnqk", d_heads, qkv_all[2], preferred_element_type=jnp.float32)
    d_scores = attn_probs * (d_probs - jnp.sum(d_probs * attn_probs, axis=-1, keepdims=True)) * head_dim ** -0.5
    ds_bf = d_scores.astype(jnp.bfloat16)
    d_q = jnp.einsum("bnqk,bkne->bqne", ds_bf, qkv_all[1], preferred_element_type=jnp.float32)
    d_k = jnp.einsum("bnqk,bqne->bkne", ds_bf, qkv_all[0], preferred_element_type=jnp.float32)
    d_qkv = jnp.stack([d_q.astype(jnp.bfloat16), d_k.astype(jnp.bfloat16), d_v.astype(jnp.bfloat16)], axis=2)
    d_wqkv = jnp.einsum("bsh,bskne->hkne", normed, d_qkv, preferred_element_type=jnp.float32)
    d_normed = jnp.einsum("bskne,hkne->bsh", d_qkv, w_qkv, preferred_element_type=jnp.float32)
    return d_normed, d_wqkv, d_wo


def mlp_forward(normed, w_in):
    hidden = jnp.einsum("bsh,hf->bsf", normed, w_in, preferred_element_type=jnp.float32)
    gelu_out, gelu_pull = jax.vjp(gelu_tanh, hidden)
    return gelu_out.astype(jnp.bfloat16), gelu_pull


def mlp_backward(normed, w_in, w_out, act_bf, gelu_pull, d_out):
    d_bf = d_out.astype(jnp.bfloat16)
    d_wout = jnp.einsum("bsf,bsh->fh", act_bf, d_bf, preferred_element_type=jnp.float32)
    d_act = jnp.einsum("bsh,fh->bsf", d_bf, w_out, preferred_element_type=jnp.float32)
    d_hidden = gelu_pull(d_act)[0].astype(jnp.bfloat16)
    d_win = jnp.einsum("bsh,bsf->hf", normed, d_hidden, preferred_element_type=jnp.float32)
    d_normed = jnp.einsum("bsf,hf->bsh", d_hidden, w_in, preferred_element_type=jnp.float32)
    return d_normed, d_win, d_wout


def reversible_block(block_w, y_one, y_two, d_one, d_two, want_x_one):
    w_qkv, w_o, w_in, w_out = block_w
    g_norm, g_norm_pull = jax.vjp(rms_norm, y_one)
    g_in = g_norm.astype(jnp.bfloat16)
    act_bf, gelu_pull = mlp_forward(g_in, w_in)
    g_part = jnp.einsum("bsf,fh->bsh", act_bf, w_out, preferred_element_type=jnp.float32)
    x_two = y_two - lax.psum(g_part, "tp")
    g_back, d_win, d_wout = mlp_backward(g_in, w_in, w_out, act_bf, gelu_pull, d_two)
    d_one = d_one + g_norm_pull(lax.psum(g_back, "tp"))[0]
    f_norm, f_norm_pull = jax.vjp(rms_norm, x_two)
    f_in = f_norm.astype(jnp.bfloat16)
    attn_cache = attn_forward(f_in, w_qkv)
    x_one = None
    if want_x_one:
        f_part = jnp.einsum("bqne,neh->bqh", attn_cache[3], w_o, preferred_element_type=jnp.float32)
        x_one = y_one - lax.psum(f_part, "tp")
    f_back, d_wqkv, d_wo = attn_backward(f_in, w_qkv, w_o, attn_cache, d_one)
    d_two = d_two + f_norm_pull(lax.psum(f_back, "tp"))[0]
    return x_one, x_two, d_one, d_two, (d_wqkv, d_wo, d_win, d_wout)


def plain_block(block_w, x_one, x_two, d_one, d_two):
    w_qkv, w_o, w_in, w_out = block_w
    f_norm, f_norm_pull = jax.vjp(rms_norm, x_two)
    f_in = f_norm.astype(jnp.bfloat16)
    attn_cache = attn_forward(f_in, w_qkv)
    f_back, d_wqkv, d_wo = attn_backward(f_in, w_qkv, w_o, attn_cache, d_one)
    g_norm, g_norm_pull = jax.vjp(rms_norm, x_one)
    g_in = g_norm.astype(jnp.bfloat16)
    act_bf, gelu_pull = mlp_forward(g_in, w_in)
    g_back, d_win, d_wout = mlp_backward(g_in, w_in, w_out, act_bf, gelu_pull, d_two)
    new_one = d_one + g_norm_pull(lax.psum(g_back, "tp"))[0]
    new_two = d_two + f_norm_pull(lax.psum(f_back, "tp"))[0]
    return new_one, new_two, (d_wqkv, d_wo, d_win, d_wout)


def solution(mesh):
    act_spec = P("dp", None, None)
    saved_spec = P(None, "dp", None, None)
    weight_specs = (P(None, None, None, "tp", None), P(None, "tp", None, None), P(None, None, "tp"), P(None, "tp", None))
    grad_specs = (P("dp", None, None, "tp", None), P("dp", "tp", None, None), P("dp", None, "tp"), P("dp", "tp", None))

    def per_device(y_one, y_two, dy_one, dy_two, saved_one, saved_two, w_qkv, w_o, w_in, w_out):
        all_w = (w_qkv, w_o, w_in, w_out)
        n_layers = w_qkv.shape[0]
        n_pairs = saved_one.shape[0]
        grad_list = [None] * n_layers
        top_w = tuple(weight[n_layers - 1] for weight in all_w)
        x_one, x_two, d_one, d_two, top_grads = reversible_block(top_w, y_one, y_two, dy_one, dy_two, n_pairs == 0)
        grad_list[n_layers - 1] = top_grads
        for pair_idx in reversed(range(n_pairs)):
            plain_w = tuple(weight[2 * pair_idx + 1] for weight in all_w)
            d_one, d_two, plain_grads = plain_block(plain_w, saved_one[pair_idx], saved_two[pair_idx], d_one, d_two)
            grad_list[2 * pair_idx + 1] = plain_grads
            rev_w = tuple(weight[2 * pair_idx] for weight in all_w)
            x_one, x_two, d_one, d_two, rev_grads = reversible_block(rev_w, saved_one[pair_idx], saved_two[pair_idx], d_one, d_two, pair_idx == 0)
            grad_list[2 * pair_idx] = rev_grads
        stacked = tuple(jnp.stack([entry[slot_idx] for entry in grad_list]) for slot_idx in range(4))
        return (x_one, x_two, d_one, d_two) + stacked

    return jax.shard_map(
        per_device,
        mesh=mesh,
        in_specs=(act_spec,) * 4 + (saved_spec,) * 2 + weight_specs,
        out_specs=(act_spec,) * 4 + grad_specs,
        check_vma=False,
    )
```

profile of v0, /device:TPU:113, one launch (start us, length us, event | category | flops | bytes accessed | tf_op | source)
XLA Modules:
  0.0 1446.5 jit_solution(10674390841938683390)
XLA Ops:
  24.6 10.5 fusion.149
  35.1 10.7 fusion.32
  47.5 9.4 fusion.146
  77.1 216.4 %all-reduce.15.cloned.1.call-done = (f32[8,256,1408]{2,1,0:T(8,128)}, f32[8,256,1408]{2,1,0:T(8,128)}) async-done(((f32[8,256,1408]{2,1,0:T(8,128)}, f32[8,256,1408]{2,1,0:T(8,128)}), (f32[8,256,1408]{2,1,0:T(8,128)}, f32[8,256,1408]{2,1,0:T(8,128)})) %all-reduce.15.cloned.1.call-update) | async-done | bytes 23068688 | tf_op jit(solution)/shard_map/psum | solution.py:69
  293.5 20.2 %multiply_reduce_fusion.2 = (f32[8,256]{1,0:T(8,128)S(1)}, f32[8,256,1408]{2,1,0:T(8,128)}, f32[8,256]{1,0:T(8,128)S(1)}) fusion(f32[8,256,1408]{2,1,0:T(8,128)} %param.11, f32[8,256,1408]{2,1,0:T(8,128)} %get-tuple-element.18, f32[8,256,1408]{2,1,0:T(8,128)} %param.10, f32[8,256,1408]{2,1,0:T(8,128)} %get-tuple-element.17), kind=kLoop, calls=%fused_computation.43 | loop fusion | flops 14413824 | bytes 57688064 | tf_op jit(solution)/shard_map/jvp()/reduce_sum | solution.py:10
  315.2 13.2 fusion.318
  350.9 8.7 fusion.240
  359.6 8.7 fusion.237
  392.4 9.4 convolution_bitcast_fusion.1
  401.8 9.6 convolution_bitcast_fusion.2
  417.3 8.8 fusion.137
  426.1 11.5 fusion.153
  437.7 8.6 fusion.135
  446.3 198.9 %all-reduce.13.cloned.1.call-done = (f32[8,256,1408]{2,1,0:T(8,128)}, f32[8,256,1408]{2,1,0:T(8,128)}) async-done(((f32[8,256,1408]{2,1,0:T(8,128)}, f32[8,256,1408]{2,1,0:T(8,128)}), (f32[8,256,1408]{2,1,0:T(8,128)}, f32[8,256,1408]{2,1,0:T(8,128)})) %all-reduce.13.cloned.1.call-update) | async-done | bytes 23068688 | tf_op jit(solution)/shard_map/psum | solution.py:78
  662.6 18.9 %fusion.10 = (f32[8,256,1408]{2,1,0:T(8,128)S(1)}, bf16[8,256,1408]{2,1,0:T(8,128)(2,1)S(1)}) fusion(f32[1,8,256,1408]{3,2,1,0:T(8,128)} %param.15, f32[8,256,1408]{2,1,0:T(8,128)} %get-tuple-element.16, f32[8,256]{1,0:T(8,128)S(1)} %multiply_multiply_fusion.8, f32[8,256]{1,0:T(8,128)S(1)} %copy-done.37, f32[8,256,1408]{2,1,0:T(8,128)} %param.13, ...), kind=kLoop, calls=%fused_computation.18 | loop fusion | flops 31719424 | bytes 75005952 | tf_op jit(solution)/shard_map/add | solution.py:93
  681.5 14.8 %fusion.25 = bf16[8,256,768]{2,1,0:T(8,128)(2,1)S(1)} fusion(f32[8,256,768]{2,1,0:T(8,128)} %copy-done.38, f32[8,256,1408]{2,1,0:T(8,128)S(1)} %get-tuple-element.21, bf16[3,768,1408]{2,1,0:T(8,128)(2,1)} %param.19), kind=kOutput, calls=%fused_computation.67 | convolution fusion | flops 4463525888 | bytes 23134208 | tf_op jit(solution)/shard_map/bsh,fh->bsf/dot_general | solution.py:54
  696.4 11.8 fusion.39
  708.2 10.6 fusion.142
  718.8 9.4 fusion.155
  728.9 12.2 convolution_bitcast_fusion.7
  741.2 12.7 convolution_bitcast_fusion.4
  764.9 305.3 %all-reduce.11.cloned.1.call-done = (f32[8,256,1408]{2,1,0:T(8,128)}, f32[8,256,1408]{2,1,0:T(8,128)}, f32[8,256,1408]{2,1,0:T(8,128)}) async-done(((f32[8,256,1408]{2,1,0:T(8,128)}, f32[8,256,1408]{2,1,0:T(8,128)}, f32[8,256,1408]{2,1,0:T(8,128)}), (f32[8,256,1408]{2,1,0:T(8,128)}, f32[8,256,1408]{2,1,0:T(8,128)}, f32[8,256,1408]{2,1,0:T(8,128)})) %all-reduce.11.cloned.1.call-update) | async-done | bytes 34603024 | tf_op jit(solution)/shard_map/psum | solution.py:67
  1070.3 12.4 multiply_reduce_fusion.5
  1094.9 12.4 fusion.9
  1158.6 9.4 convolution_bitcast_fusion
  1181.2 10.0 convolution_bitcast_fusion.9
  1204.9 8.9 convolution_bitcast_fusion.5
  1213.8 12.3 convolution_bitcast_fusion.6
  1226.1 10.9 pad_maximum_fusion.1
  1249.2 152.5 %all-reduce.9.cloned.1.call-done = (f32[8,256,1408]{2,1,0:T(8,128)}, f32[8,256,1408]{2,1,0:T(8,128)}) async-done(((f32[8,256,1408]{2,1,0:T(8,128)}, f32[8,256,1408]{2,1,0:T(8,128)}), (f32[8,256,1408]{2,1,0:T(8,128)}, f32[8,256,1408]{2,1,0:T(8,128)})) %all-reduce.9.cloned.1.call-update) | async-done | bytes 23068688 | tf_op jit(solution)/shard_map/psum | solution.py:76
  1401.8 12.9 bitcast_subtract_fusion.1
  1423.3 16.4 %fusion.11 = f32[8,256,1408]{2,1,0:T(8,128)} fusion(f32[8,256,1408]{2,1,0:T(8,128)} %copy-done.4, f32[8,256,1408]{2,1,0:T(8,128)} %get-tuple-element.20, f32[8,256,1408]{2,1,0:T(8,128)} %get-tuple-element.11, f32[8,256]{1,0:T(8,128)S(1)} %multiply_multiply_fusion.6, f32[8,256]{1,0:T(8,128)S(1)} %fusion.284), kind=kLoop, calls=%fused_computation.19 | loop fusion | flops 14417920 | bytes 46153728 | tf_op jit(solution)/shard_map/add | solution.py:78
  (263 shorter events, 232.7 us)
Async XLA Ops:
  7.2 286.3 %all-reduce.15.cloned.1.call-start = ((), (), s32[]{:S(2)}) async-start(), calls=%async_computation.3 | async-start | bytes 46137344 | tf_op jit(solution)/shard_map/psum | solution.py:69
  14.8 298.9 %copy-start.32 = (f32[8,256]{1,0:T(8,128)}, f32[8,256]{1,0:T(8,128)S(1)}, u32[]{:S(2)}) copy-start(f32[8,256]{1,0:T(8,128)S(1)} %fusion.285) | copy-start | bytes 24580
  14.8 20.3 %slice-start.27 = ((s8[11534336]{0:T(1024)(128)(4,1)}), s8[3145728]{0:T(1024)(128)(4,1)S(1)}, s32[]{:S(2)}) async-start(s8[11534336]{0:T(1024)(128)(4,1)} %bitcast.386), calls=%async_computation.31 | async-start | bytes 6291456
  14.8 20.3 %slice-start.28 = ((s8[11534336]{0:T(1024)(128)(4,1)}), s8[4194304]{0:T(1024)(128)(4,1)S(1)}, s32[]{:S(2)}) async-start(s8[11534336]{0:T(1024)(128)(4,1)} %bitcast.386), calls=%async_computation.32 | async-start | bytes 8388608
  57.0 588.3 %all-reduce.13.cloned.1.call-start = ((), (), s32[]{:S(2)}) async-start(), calls=%async_computation.2 | async-start | bytes 46137344 | tf_op jit(solution)/shard_map/psum | solution.py:78
  77.1 311.8 %copy-start.7 = (bf16[8,2,256,256]{2,3,1,0:T(8,128)(2,1)}, bf16[8,2,256,256]{2,3,1,0:T(8,128)(2,1)S(1)}, u32[]{:S(2)}) copy-start(bf16[8,2,256,256]{2,3,1,0:T(8,128)(2,1)S(1)} %fusion.316) | copy-start | bytes 6291460
  293.5 20.2 %slice-start.18 = ((s8[11534336]{0:T(1024)(128)(4,1)}), s8[4194304]{0:T(1024)(128)(4,1)S(1)}, s32[]{:S(2)}) async-start(s8[11534336]{0:T(1024)(128)(4,1)} %bitcast.380), calls=%async_computation.22 | async-start | bytes 8388608
  293.5 20.2 %slice-start.19 = ((s8[11534336]{0:T(1024)(128)(4,1)}), s8[4194304]{0:T(1024)(128)(4,1)S(1)}, s32[]{:S(2)}) async-start(s8[11534336]{0:T(1024)(128)(4,1)} %bitcast.380), calls=%async_computation.23 | async-start | bytes 8388608
  293.5 21.7 %slice-start.20 = ((s8[11534336]{0:T(1024)(128)(4,1)}), s8[3145728]{0:T(1024)(128)(4,1)S(1)}, s32[]{:S(2)}) async-start(s8[11534336]{0:T(1024)(128)(4,1)} %bitcast.380), calls=%async_computation.24 | async-start | bytes 6291456
  411.5 658.7 %all-reduce.11.cloned.1.call-start = ((), (), s32[]{:S(2)}) async-start(), calls=%async_computation.1 | async-start | bytes 69206016 | tf_op jit(solution)/shard_map/psum | solution.py:67
  417.3 20.4 %copy-start.34 = (f32[8,256]{1,0:T(8,128)}, f32[8,256]{1,0:T(8,128)S(1)}, u32[]{:S(2)}) copy-start(f32[8,256]{1,0:T(8,128)S(1)} %fusion.283) | copy-start | bytes 24580
  417.3 20.4 %slice-start.3 = ((s8[11534336]{0:T(1024)(128)(4,1)}), s8[4194304]{0:T(1024)(128)(4,1)S(1)}, s32[]{:S(2)}) async-start(s8[11534336]{0:T(1024)(128)(4,1)} %bitcast.370), calls=%async_computation.7 | async-start | bytes 8388608
  417.3 20.4 %slice-start.4 = ((s8[11534336]{0:T(1024)(128)(4,1)}), s8[4194304]{0:T(1024)(128)(4,1)S(1)}, s32[]{:S(2)}) async-start(s8[11534336]{0:T(1024)(128)(4,1)} %bitcast.370), calls=%async_computation.8 | async-start | bytes 8388608
  681.5 14.8 %copy-start.4 = (f32[8,256,1408]{2,1,0:T(8,128)}, f32[8,256,1408]{2,1,0:T(8,128)S(1)}, u32[]{:S(2)}) copy-start(f32[8,256,1408]{2,1,0:T(8,128)S(1)} %get-tuple-element.21) | copy-start | bytes 34603012
  681.5 14.9 %copy-start.10 = (bf16[8,256,1408]{2,1,0:T(8,128)(2,1)}, bf16[8,256,1408]{2,1,0:T(8,128)(2,1)S(1)}, u32[]{:S(2)}) copy-start(bf16[8,256,1408]{2,1,0:T(8,128)(2,1)S(1)} %get-tuple-element.22) | copy-start | bytes 17301508
  696.4 22.4 %copy-start.43 = (bf16[8,256,768]{2,1,0:T(8,128)(2,1)}, bf16[8,256,768]{2,1,0:T(8,128)(2,1)S(1)}, u32[]{:S(2)}) copy-start(bf16[8,256,768]{2,1,0:T(8,128)(2,1)S(1)} %fusion.25) | copy-start | bytes 9437188
  728.3 673.5 %all-reduce.9.cloned.1.call-start = ((), (), s32[]{:S(2)}) async-start(), calls=%async_computation | async-start | bytes 46137344 | tf_op jit(solution)/shard_map/psum | solution.py:76
  728.9 25.0 %slice-start.21 = ((s8[11534336]{0:T(1024)(128)(4,1)}), s8[4194304]{0:T(1024)(128)(4,1)S(1)}, s32[]{:S(2)}) async-start(s8[11534336]{0:T(1024)(128)(4,1)} %bitcast.382), calls=%async_computation.25 | async-start | bytes 8388608
  728.9 25.0 %slice-start.22 = ((s8[11534336]{0:T(1024)(128)(4,1)}), s8[4194304]{0:T(1024)(128)(4,1)S(1)}, s32[]{:S(2)}) async-start(s8[11534336]{0:T(1024)(128)(4,1)} %bitcast.382), calls=%async_computation.26 | async-start | bytes 8388608
  741.2 18.3 %slice-start = ((s8[11534336]{0:T(1024)(128)(4,1)}), s8[3145728]{0:T(1024)(128)(4,1)S(1)}, s32[]{:S(2)}) async-start(s8[11534336]{0:T(1024)(128)(4,1)} %bitcast.368), calls=%async_computation.4 | async-start | bytes 6291456
  1070.2 14.4 slice-start.24
  1070.2 15.6 %slice-start.7 = ((s8[11534336]{0:T(1024)(128)(4,1)}), s8[4194304]{0:T(1024)(128)(4,1)S(1)}, s32[]{:S(2)}) async-start(s8[11534336]{0:T(1024)(128)(4,1)} %bitcast.372), calls=%async_computation.11 | async-start | bytes 8388608
  1070.2 16.4 %slice-start.8 = ((s8[11534336]{0:T(1024)(128)(4,1)}), s8[3145728]{0:T(1024)(128)(4,1)S(1)}, s32[]{:S(2)}) async-start(s8[11534336]{0:T(1024)(128)(4,1)} %bitcast.372), calls=%async_computation.12 | async-start | bytes 6291456
  1070.2 17.6 %slice-start.25 = ((s8[11534336]{0:T(1024)(128)(4,1)}), s8[4194304]{0:T(1024)(128)(4,1)S(1)}, s32[]{:S(2)}) async-start(s8[11534336]{0:T(1024)(128)(4,1)} %bitcast.384), calls=%async_computation.29 | async-start | bytes 8388608
  1070.2 18.5 %slice-start.26 = ((s8[11534336]{0:T(1024)(128)(4,1)}), s8[3145728]{0:T(1024)(128)(4,1)S(1)}, s32[]{:S(2)}) async-start(s8[11534336]{0:T(1024)(128)(4,1)} %bitcast.384), calls=%async_computation.30 | async-start | bytes 6291456
  1130.7 27.9 %copy-start.44 = (bf16[8,256,1,2,88]{1,4,3,0,2:T(8,128)(2,1)}, bf16[8,256,1,2,88]{1,4,3,0,2:T(8,128)(2,1)S(1)}, u32[]{:S(2)}) copy-start(bf16[8,256,1,2,88]{1,4,3,0,2:T(8,128)(2,1)S(1)} %fusion.236) | copy-start | bytes 2162692
  1175.0 16.2 %slice-start.9 = ((s8[11534336]{0:T(1024)(128)(4,1)}), s8[3145728]{0:T(1024)(128)(4,1)S(1)}, s32[]{:S(2)}) async-start(s8[11534336]{0:T(1024)(128)(4,1)} %bitcast.374), calls=%async_computation.13 | async-start | bytes 6291456
  1181.2 17.1 %slice-start.34 = ((s8[4325376]{0:T(1024)(128)(4,1)}), s8[4194304]{0:T(1024)(128)(4,1)S(1)}, s32[]{:S(2)}) async-start(s8[4325376]{0:T(1024)(128)(4,1)} %bitcast.392), calls=%async_computation.38 | async-start | bytes 8388608
  1181.2 23.6 %slice-start.30 = ((s8[5767168]{0:T(1024)(128)(4,1)}), s8[4194304]{0:T(1024)(128)(4,1)S(1)}, s32[]{:S(2)}) async-start(s8[5767168]{0:T(1024)(128)(4,1)} %bitcast.388), calls=%async_computation.34 | async-start | bytes 8388608
  1204.9 21.2 %slice-start.32 = ((s8[4325376]{0:T(1024)(128)(4,1)}), s8[4194304]{0:T(1024)(128)(4,1)S(1)}, s32[]{:S(2)}) async-start(s8[4325376]{0:T(1024)(128)(4,1)} %bitcast.390), calls=%async_computation.36 | async-start | bytes 8388608
  1213.8 23.3 %slice-start.12 = ((s8[11534336]{0:T(1024)(128)(4,1)}), s8[4194304]{0:T(1024)(128)(4,1)S(1)}, s32[]{:S(2)}) async-start(s8[11534336]{0:T(1024)(128)(4,1)} %bitcast.376), calls=%async_computation.16 | async-start | bytes 8388608
  1213.8 23.3 %slice-start.13 = ((s8[11534336]{0:T(1024)(128)(4,1)}), s8[3145728]{0:T(1024)(128)(4,1)S(1)}, s32[]{:S(2)}) async-start(s8[11534336]{0:T(1024)(128)(4,1)} %bitcast.376), calls=%async_computation.17 | async-start | bytes 6291456
  (66 other events, 465.0 us)
Sparse Core Ops, SparseCore 0:
  57.1 236.3 all-reduce.14
  411.6 233.5 all-reduce.12
  728.4 341.7 all-reduce.10
  1168.2 233.5 all-reduce.8
where the time goes:
time: 1450 us
  waiting for transfers between devices  873 us (60%)
  matrix products  340 us (23%)
  other arithmetic  189 us (13%)
  local copies, waits for them, and re-layouts  27.9 us (2%)
  between operations  15 us (1%)
    psum x1, waiting for transfers between devices, reversible_block(): x_two = y_two - lax.psum(g_part, 'tp')  305 us
    psum x1, waiting for transfers between devices, reversible_block(): d_one = d_one + g_norm_pull(lax.psum(g_back, 'tp'))[0]  216 us
    psum x1, waiting for transfers between devices, reversible_block(): d_two = d_two + f_norm_pull(lax.psum(f_back, 'tp'))[0]  199 us
    psum x1, waiting for transfers between devices, reversible_block(): x_one = y_one - lax.psum(f_part, 'tp')  153 us
    reduce_sum x5, other arithmetic, rms_norm(): jnp.mean(state * state, axis=-1, keepdims=True) + EPS  48.1 us
    dot_general x3, matrix products, mlp_backward(): jnp.einsum('bsh,fh->bsf', d_bf, w_out, preferred_element_type=jnp.float32)  37.3 us
    dot_general x3, matrix products, mlp_backward(): jnp.einsum('bsf,bsh->fh', act_bf, d_bf, preferred_element_type=jnp.float32)  33.9 us
    reduce_sum x4, other arithmetic, rms_norm(): state * lax.rsqrt(jnp.mean(state * state, axis=-1, keepdims=True) + EPS)  31.9 us
  transfers between devices with their start and end apart: 4, of which 4 were waited for; matrix products, arithmetic and copies ran while one was open for 11% of the time, Pallas kernels for 0%

commit v1 on v0

v1 whole, which is shorter than its diff:
```python
import jax
import jax.numpy as jnp
from jax import lax
from jax.sharding import PartitionSpec as P

EPS = 1e-6
F32, BF16 = jnp.float32, jnp.bfloat16


def rms_scale(state):
    return lax.rsqrt(jnp.mean(state * state, axis=-1, keepdims=True) + EPS)


def rms_bf(state):
    return (state * rms_scale(state)).astype(BF16)


def rms_pull(state, cot):
    scale = rms_scale(state)
    normed = state * scale
    return scale * (cot - normed * jnp.mean(normed * cot, axis=-1, keepdims=True))


def gelu_tanh(hidden):
    return jax.nn.gelu(hidden, approximate=True)


def attn_forward(normed, w_qkv):
    head_dim = w_qkv.shape[-1]
    qkv_all = jnp.einsum("bsh,hkne->kbsne", normed, w_qkv, preferred_element_type=F32).astype(BF16)
    scores = jnp.einsum("bqne,bkne->bnqk", qkv_all[0], qkv_all[1], preferred_element_type=F32) * head_dim ** -0.5
    attn_probs = jax.nn.softmax(scores, axis=-1)
    probs_bf = attn_probs.astype(BF16)
    heads_out = jnp.einsum("bnqk,bkne->bqne", probs_bf, qkv_all[2], preferred_element_type=F32).astype(BF16)
    return qkv_all, attn_probs, probs_bf, heads_out


def attn_backward(normed, w_qkv, w_o, attn_cache, d_bf):
    qkv_all, attn_probs, probs_bf, heads_out = attn_cache
    head_dim = w_qkv.shape[-1]
    d_wo = jnp.einsum("bqne,bqh->neh", heads_out, d_bf, preferred_element_type=F32)
    d_heads = jnp.einsum("bqh,neh->bqne", d_bf, w_o, preferred_element_type=F32).astype(BF16)
    d_v = jnp.einsum("bnqk,bqne->bkne", probs_bf, d_heads, preferred_element_type=F32)
    d_probs = jnp.einsum("bqne,bkne->bnqk", d_heads, qkv_all[2], preferred_element_type=F32)
    d_scores = attn_probs * (d_probs - jnp.sum(d_probs * attn_probs, axis=-1, keepdims=True)) * head_dim ** -0.5
    ds_bf = d_scores.astype(BF16)
    d_q = jnp.einsum("bnqk,bkne->bqne", ds_bf, qkv_all[1], preferred_element_type=F32)
    d_k = jnp.einsum("bnqk,bqne->bkne", ds_bf, qkv_all[0], preferred_element_type=F32)
    d_qkv = jnp.stack([d_q.astype(BF16), d_k.astype(BF16), d_v.astype(BF16)], axis=2)
    d_normed = jnp.einsum("bskne,hkne->bsh", d_qkv, w_qkv, preferred_element_type=F32)
    d_wqkv = jnp.einsum("bsh,bskne->hkne", normed, d_qkv, preferred_element_type=F32)
    return d_normed, d_wqkv, d_wo


def mlp_forward(normed, w_in):
    hidden = jnp.einsum("bsh,hf->bsf", normed, w_in, preferred_element_type=F32)
    gelu_out, gelu_pull = jax.vjp(gelu_tanh, hidden)
    return gelu_out.astype(BF16), gelu_pull


def mlp_backward(normed, w_in, w_out, act_bf, gelu_pull, d_bf):
    d_act = jnp.einsum("bsh,fh->bsf", d_bf, w_out, preferred_element_type=F32)
    d_hidden = gelu_pull(d_act)[0].astype(BF16)
    d_normed = jnp.einsum("bsf,hf->bsh", d_hidden, w_in, preferred_element_type=F32)
    d_wout = jnp.einsum("bsf,bsh->fh", act_bf, d_bf, preferred_element_type=F32)
    d_win = jnp.einsum("bsh,bsf->hf", normed, d_hidden, preferred_element_type=F32)
    return d_normed, d_win, d_wout


def scatter(part):
    return lax.psum_scatter(part, "tp", scatter_dimension=0, tiled=True)


def gather(shard):
    return lax.all_gather(shard, "tp", axis=0, tiled=True)


def solution(mesh):
    act_spec = P("dp", None, None)
    saved_spec = P(None, "dp", None, None)
    weight_specs = (P(None, None, None, "tp", None), P(None, "tp", None, None), P(None, None, "tp"), P(None, "tp", None))
    grad_specs = (P("dp", None, None, "tp", None), P("dp", "tp", None, None), P("dp", None, "tp"), P("dp", "tp", None))
    n_tp = mesh.shape["tp"]

    def per_device(y_one, y_two, dy_one, dy_two, saved_one, saved_two, w_qkv, w_o, w_in, w_out):
        n_layers = w_qkv.shape[0]
        n_pairs = saved_one.shape[0]
        rows = y_one.shape[0] // n_tp
        start = lax.axis_index("tp") * rows

        def own(state):
            return lax.dynamic_slice_in_dim(state, start, rows, 0)

        grads = [None] * n_layers

        top = n_layers - 1
        a_one = rms_bf(y_one)
        act, pull = mlp_forward(a_one, w_in[top])
        g_shard = scatter(jnp.einsum("bsf,fh->bsh", act, w_out[top], preferred_element_type=F32))
        d_two_bf = dy_two.astype(BF16)
        g_back, d_win, d_wout = mlp_backward(a_one, w_in[top], w_out[top], act, pull, d_two_bf)
        d_one = own(dy_one) + rms_pull(own(y_one), scatter(g_back.astype(BF16)).astype(F32))
        d_one_bf = gather(d_one.astype(BF16))
        x_two = own(y_two) - g_shard
        d_two = own(dy_two)
        f_in = gather(rms_bf(x_two))
        cache = attn_forward(f_in, w_qkv[top])
        f_back, d_wqkv, d_wo = attn_backward(f_in, w_qkv[top], w_o[top], cache, d_one_bf)
        d_two = d_two + rms_pull(x_two, scatter(f_back.astype(BF16)).astype(F32))
        grads[top] = (d_wqkv, d_wo, d_win, d_wout)

        for pair in reversed(range(n_pairs)):
            s_one, s_two = saved_one[pair], saved_two[pair]
            mid, low = 2 * pair + 1, 2 * pair
            a_one, a_two = rms_bf(s_one), rms_bf(s_two)
            d_two_bf = gather(d_two.astype(BF16))
            cache = attn_forward(a_two, w_qkv[mid])
            f_back, d_wqkv, d_wo = attn_backward(a_two, w_qkv[mid], w_o[mid], cache, d_one_bf)
            act, pull = mlp_forward(a_one, w_in[mid])
            g_back_mid, d_win, d_wout = mlp_backward(a_one, w_in[mid], w_out[mid], act, pull, d_two_bf)
            grads[mid] = (d_wqkv, d_wo, d_win, d_wout)
            d_two = d_two + rms_pull(own(s_two), scatter(f_back.astype(BF16)).astype(F32))
            d_two_bf = gather(d_two.astype(BF16))
            act, pull = mlp_forward(a_one, w_in[low])
            g_shard = scatter(jnp.einsum("bsf,fh->bsh", act, w_out[low], preferred_element_type=F32))
            x_two_shard = own(s_two) - g_shard
            x_two = gather(x_two_shard)
            f_in = rms_bf(x_two)
            cache = attn_forward(f_in, w_qkv[low])
            heads = cache[3]
            n_b, n_s, n_h, n_e = heads.shape
            heads_t = jnp.transpose(heads, (2, 3, 0, 1)).reshape(n_h * n_e, n_b * n_s)
            heads_all = gather(heads_t)
            wo_all = gather(w_o[low].reshape(n_h * n_e, -1))
            f_val = jnp.einsum("et,eh->th", heads_all, wo_all, preferred_element_type=F32)
            x_one = s_one - f_val.reshape(s_one.shape)
            g_back_low, d_win, d_wout = mlp_backward(a_one, w_in[low], w_out[low], act, pull, d_two_bf)
            g_back = scatter((g_back_mid + g_back_low).astype(BF16)).astype(F32)
            d_one = d_one + rms_pull(own(s_one), g_back)
            if pair == 0:
                d_one_full = gather(d_one)
                d_one_bf = d_one_full.astype(BF16)
            else:
                d_one_bf = gather(d_one.astype(BF16))
            f_back, d_wqkv, d_wo = attn_backward(f_in, w_qkv[low], w_o[low], cache, d_one_bf)
            d_two = d_two + rms_pull(x_two_shard, scatter(f_back.astype(BF16)).astype(F32))
            grads[low] = (d_wqkv, d_wo, d_win, d_wout)
        d_two_full = gather(d_two)
        stacked = tuple(jnp.stack([entry[slot] for entry in grads]) for slot in range(4))
        return (x_one, x_two, d_one_full, d_two_full) + stacked

    return jax.shard_map(
        per_device,
        mesh=mesh,
        in_specs=(act_spec,) * 4 + (saved_spec,) * 2 + weight_specs,
        out_specs=(act_spec,) * 4 + grad_specs,
        check_vma=False,
    )
```

time: 1450 us -> 876 us (0.60)
  waiting for transfers between devices: 873 us -> 361 us
  other arithmetic: 189 us -> 93.1 us
  local copies, waits for them, and re-layouts: 27.9 us -> 54.7 us
    psum x4 -> x0, waiting for transfers between devices: 873 us -> none  [the longest x1 305 us: reversible_block(): x_two = y_two - lax.psum(g_part, 'tp')]
    reduce_scatter x0 -> x7, waiting for transfers between devices: none -> 206 us  [scatter(): return lax.psum_scatter(part, 'tp', scatter_dimension=0, tiled=True)]
    all_gather x0 -> x9, waiting for transfers between devices: none -> 152 us  [gather(): return lax.all_gather(shard, 'tp', axis=0, tiled=True)]
    reduce_sum x9 -> x13, other arithmetic: 80 us -> 36 us  [the longest x8 27.3 us: rms_scale(): return lax.rsqrt(jnp.mean(state * state, axis=-1, keepdims=True) + EPS)]
    add x3 -> x2, other arithmetic: 47.8 us -> 6.75 us  [the longest x1 4.19 us: per_device(): d_one = d_one + rms_pull(own(s_one), g_back)]
    unnamed x188 -> x132, local copies, waits for them, and re-layouts: 27.9 us -> 52.6 us
  transfers between devices with their start and end apart: 4 -> 16, of which waited for: 4 -> 12; matrix products, arithmetic and copies ran while one was open for 11% -> 39% of each run, Pallas kernels for 0% -> 0%
where the time goes in v1:
time: 876 us; the launch traced here: 868 us
  waiting for transfers between devices  361 us (41%)
  matrix products  342 us (39%)
  other arithmetic  93.1 us (11%)
  local copies, waits for them, and re-layouts  54.7 us (6%)
  between operations  15.2 us (2%)
    reduce_scatter x7, waiting for transfers between devices, scatter(): return lax.psum_scatter(part, 'tp', scatter_dimension=0, tiled=True)  206 us
    all_gather x9, waiting for transfers between devices, gather(): return lax.all_gather(shard, 'tp', axis=0, tiled=True)  152 us
    unnamed x132, local copies, waits for them, and re-layouts  52.6 us
    dot_general x3, matrix products, mlp_backward(): d_act = jnp.einsum('bsh,fh->bsf', d_bf, w_out, preferred_element_type=F32)  36.8 us
    dot_general x3, matrix products, mlp_backward(): d_wout = jnp.einsum('bsf,bsh->fh', act_bf, d_bf, preferred_element_type=F32)  31 us
    reduce_sum x8, other arithmetic, rms_scale(): return lax.rsqrt(jnp.mean(state * state, axis=-1, keepdims=True) + EPS)  27.3 us
    dot_general x3, matrix products, mlp_backward(): jnp.einsum('bsf,hf->bsh', d_hidden, w_in, preferred_element_type=F32)  26.4 us
    dot_general x3, matrix products, mlp_forward(): hidden = jnp.einsum('bsh,hf->bsf', normed, w_in, preferred_element_type=F32)  26 us
  transfers between devices with their start and end apart: 16, of which 12 were waited for; matrix products, arithmetic and copies ran while one was open for 39% of the time, Pallas kernels for 0%

profile of v1, /device:TPU:113, one launch (start us, length us, event | category | flops | bytes accessed | tf_op | source)
XLA Modules:
  0.0 867.8 jit_solution(12585355150506730799)
XLA Ops:
  21.7 13.7 %fusion.23 = bf16[8,256,768]{2,1,0:T(8,128)(2,1)S(1)} fusion(f32[8,256,768]{2,1,0:T(8,128)S(1)} %fusion.126, f32[8,256,1408]{2,1,0:T(8,128)} %param.13, bf16[3,768,1408]{2,1,0:T(8,128)(2,1)} %param.19), kind=kOutput, calls=%fused_computation.47 | convolution fusion | flops 4463525888 | bytes 23134208 | tf_op jit(solution)/shard_map/bsh,fh->bsf/dot_general | solution.py:62
  46.3 10.7 %fusion.135 = f32[8,256,1408]{2,1,0:T(8,128)} fusion(bf16[3,768,1408]{2,1,0:T(8,128)(2,1)} %param.19, f32[8,256,768]{2,1,0:T(8,128)} %copy-done.36), kind=kOutput, calls=%fused_computation.143 | convolution fusion | flops 4443340800 | bytes 19988480 | tf_op jit(solution)/shard_map/bsf,fh->bsh/dot_general | solution.py:99
  58.7 25.6 %reduce-scatter.10.cloned.1.call-done = bf16[1,256,1408]{2,1,0:T(8,128)(2,1)} async-done(((bf16[8,256,1408]{2,1,0:T(8,128)(2,1)}), bf16[1,256,1408]{2,1,0:T(8,128)(2,1)}) %reduce-scatter.10.cloned.1.call-update) | async-done | bytes 720912 | tf_op jit(solution)/shard_map/reduce_scatter | solution.py:71
  90.1 61.1 %reduce-scatter.12.cloned.1.call-done = f32[1,256,1408]{2,1,0:T(8,128)} async-done(((f32[8,256,1408]{2,1,0:T(8,128)}), f32[1,256,1408]{2,1,0:T(8,128)}) %reduce-scatter.12.cloned.1.call-update) | async-done | bytes 1441808 | tf_op jit(solution)/shard_map/reduce_scatter | solution.py:71
  175.0 13.2 %all-gather.18.cloned.1.call-done = bf16[8,256,1408]{2,1,0:T(8,128)(2,1)} async-done(((bf16[1,256,1408]{2,1,0:T(8,128)(2,1)}), bf16[8,256,1408]{2,1,0:T(8,128)(2,1)}) %all-gather.18.cloned.1.call-update) | async-done | bytes 5767184 | tf_op jit(solution)/shard_map/all_gather | solution.py:75
  251.8 8.6 fusion.241
  266.2 8.6 bitcast_convert_fusion.2
  280.0 8.7 fusion.124
  291.4 9.7 %fusion.139 = f32[8,256,1408]{2,1,0:T(8,128)} fusion(bf16[3,768,1408]{2,1,0:T(8,128)(2,1)} %param.19, f32[8,256,768]{2,1,0:T(8,128)S(1)} %fusion.124), kind=kOutput, calls=%fused_computation.147 | convolution fusion | flops 4443340800 | bytes 19988480 | tf_op jit(solution)/shard_map/bsf,fh->bsh/dot_general | solution.py:125
  311.7 65.5 %reduce-scatter.8.cloned.1.call-done = f32[1,256,1408]{2,1,0:T(8,128)} async-done(((f32[8,256,1408]{2,1,0:T(8,128)}), f32[1,256,1408]{2,1,0:T(8,128)}) %reduce-scatter.8.cloned.1.call-update) | async-done | bytes 1441808 | tf_op jit(solution)/shard_map/reduce_scatter | solution.py:71
  383.2 10.5 %fusion.122 = f32[8,256,768]{2,1,0:T(8,128)} fusion(f32[1,8,256,1408]{3,2,1,0:T(8,128)} %param.14, f32[8,256]{1,0:T(8,128)S(1)} %add_rsqrt_fusion.3, bf16[3,1408,768]{2,1,0:T(8,128)(2,1)} %param.18), kind=kOutput, calls=%fused_computation.131 | convolution fusion | flops 4434952192 | bytes 19996672 | tf_op jit(solution)/shard_map/bsh,hf->bsf/dot_general | solution.py:56
  393.7 23.6 %all-gather.20.cloned.1.call-done = bf16[8,256,1408]{2,1,0:T(8,128)(2,1)} async-done(((bf16[1,256,1408]{2,1,0:T(8,128)(2,1)}), bf16[8,256,1408]{2,1,0:T(8,128)(2,1)}) %all-gather.20.cloned.1.call-update) | async-done | bytes 5767184 | tf_op jit(solution)/shard_map/all_gather | solution.py:75
  417.2 11.5 %fusion.30 = bf16[8,256,768]{2,1,0:T(8,128)(2,1)S(1)} fusion(f32[8,256,768]{2,1,0:T(8,128)} %fusion.122, bf16[8,256,1408]{2,1,0:T(8,128)(2,1)} %all-gather.20.cloned.1.call-done, bf16[3,768,1408]{2,1,0:T(8,128)(2,1)} %param.19), kind=kOutput, calls=%fused_computation.54 | convolution fusion | flops 4460642304 | bytes 17367040 | tf_op jit(solution)/shard_map/bsh,fh->bsf/dot_general | solution.py:62
  430.4 9.4 %fusion.129 = f32[8,256,1408]{2,1,0:T(8,128)} fusion(bf16[8,256,768]{2,1,0:T(8,128)(2,1)S(1)} %fusion.30, bf16[3,1408,768]{2,1,0:T(8,128)(2,1)} %param.18), kind=kOutput, calls=%fused_computation.137 | convolution fusion | flops 4429185024 | bytes 16842752 | tf_op jit(solution)/shard_map/bsf,hf->bsh/dot_general | solution.py:64
  439.8 14.0 %all-gather.22.cloned.1.call-done = bf16[8,256,1408]{2,1,0:T(8,128)(2,1)} async-done(((bf16[1,256,1408]{2,1,0:T(8,128)(2,1)}), bf16[8,256,1408]{2,1,0:T(8,128)(2,1)}) %all-gather.22.cloned.1.call-update) | async-done | bytes 5767184 | tf_op jit(solution)/shard_map/all_gather | solution.py:75
  453.8 11.6 %fusion.16 = bf16[8,256,768]{2,1,0:T(8,128)(2,1)S(1)} fusion(f32[8,256,768]{2,1,0:T(8,128)} %copy-done.38, bf16[8,256,1408]{2,1,0:T(8,128)(2,1)} %all-gather.22.cloned.1.call-done, bf16[3,768,1408]{2,1,0:T(8,128)(2,1)} %param.19), kind=kOutput, calls=%fused_computation.40 | convolution fusion | flops 4460642304 | bytes 17367040 | tf_op jit(solution)/shard_map/bsh,fh->bsf/dot_general | solution.py:62
  467.1 8.5 add_convert_fusion
  478.5 32.6 %reduce-scatter.18.cloned.1.call-done = bf16[1,256,1408]{2,1,0:T(8,128)(2,1)} async-done(((bf16[8,256,1408]{2,1,0:T(8,128)(2,1)}), bf16[1,256,1408]{2,1,0:T(8,128)(2,1)}) %reduce-scatter.18.cloned.1.call-update) | async-done | bytes 720912 | tf_op jit(solution)/shard_map/reduce_scatter | solution.py:71
  517.4 55.6 %all-gather.10.cloned.1.call-done = f32[8,256,1408]{2,1,0:T(8,128)} async-done(((f32[1,256,1408]{2,1,0:T(8,128)}), f32[8,256,1408]{2,1,0:T(8,128)}) %all-gather.10.cloned.1.call-update) | async-done | bytes 11534352 | tf_op jit(solution)/shard_map/all_gather | solution.py:75
  591.3 42.9 %all-gather.24.cloned.1.call-done = f32[8,256,1408]{2,1,0:T(8,128)} async-done(((f32[1,256,1408]{2,1,0:T(8,128)}), f32[8,256,1408]{2,1,0:T(8,128)}) %all-gather.24.cloned.1.call-update) | async-done | bytes 11534352 | tf_op jit(solution)/shard_map/all_gather | solution.py:75
  645.5 8.6 fusion.253
  678.5 12.2 %convolution_bitcast_fusion.3 = f32[1,1408,768]{2,1,0:T(8,128)} fusion(bf16[8,256,768]{2,1,0:T(8,128)(2,1)} %copy-done.41, f32[8,256,1408]{2,1,0:T(8,128)} %param.10, f32[8,256]{1,0:T(8,128)S(1)} %copy-done.29), kind=kOutput, calls=%fused_computation.101 | convolution fusion | flops 4434952192 | bytes 19013632 | tf_op jit(solution)/shard_map/bsh,bsf->hf/dot_general | solution.py:66
  690.7 16.0 %reduce-scatter.20.cloned.1.call-done = bf16[1,256,1408]{2,1,0:T(8,128)(2,1)} async-done(((bf16[8,256,1408]{2,1,0:T(8,128)(2,1)}), bf16[1,256,1408]{2,1,0:T(8,128)(2,1)}) %reduce-scatter.20.cloned.1.call-update) | async-done | bytes 720912 | tf_op jit(solution)/shard_map/reduce_scatter | solution.py:71
  710.7 12.2 %convolution_bitcast_fusion = f32[1,768,1408]{2,1,0:T(8,128)} fusion(f32[8,256,1408]{2,1,0:T(8,128)} %param.13, f32[8,256,768]{2,1,0:T(8,128)} %copy-done.36), kind=kOutput, calls=%fused_computation.98 | convolution fusion | flops 4446224384 | bytes 22151168 | tf_op jit(solution)/shard_map/bsf,bsh->fh/dot_general | solution.py:65
  728.5 9.9 %fusion.66 = f32[1,1408,3,2,88]{1,4,3,2,0:T(8,128)} fusion(f32[1,8,256,1408]{3,2,1,0:T(8,128)} %param.15, f32[8,256]{1,0:T(8,128)S(1)} %copy-done.31, bf16[8,256,1,2,88]{1,4,3,0,2:T(8,128)(2,1)S(1)} %copy-done.20, bf16[8,256,1,2,88]{1,4,3,0,2:T(8,128)(2,1)} %fusion.244, bf16[8,256,1,2,88]{1,4,3,0,2:T(8,128)(2,1)S(1)} %copy-done.46), kind=kOutput, calls=%fused_computation.110 | convolution fusion | flops 3057319936 | bytes 16678912 | tf_op jit(solution)/shard_map/bsh,bskne->hkne/dot_general | solution.py:51
  751.2 9.6 %convolution_bitcast_fusion.1 = f32[1,768,1408]{2,1,0:T(8,128)S(1)} fusion(bf16[8,256,1408]{2,1,0:T(8,128)(2,1)} %all-gather.20.cloned.1.call-done, f32[8,256,768]{2,1,0:T(8,128)} %fusion.122), kind=kOutput, calls=%fused_computation.99 | convolution fusion | flops 4443340800 | bytes 16384000 | tf_op jit(solution)/shard_map/bsf,bsh->fh/dot_general | solution.py:65
  760.8 9.2 %convolution_bitcast_fusion.2 = f32[1,768,1408]{2,1,0:T(8,128)S(1)} fusion(bf16[8,256,1408]{2,1,0:T(8,128)(2,1)} %all-gather.22.cloned.1.call-done, f32[8,256,768]{2,1,0:T(8,128)} %copy-done.38), kind=kOutput, calls=%fused_computation.100 | convolution fusion | flops 4443340800 | bytes 16384000 | tf_op jit(solution)/shard_map/bsf,bsh->fh/dot_general | solution.py:65
  792.3 13.8 %fusion.319 = f32[2048,1408]{1,0:T(8,128)S(1)} fusion(bf16[1408,2048]{1,0:T(8,128)(2,1)} %all-gather.12.cloned.1.call-done, bf16[1408,1408]{1,0:T(8,128)(2,1)} %all-gather.14.cloned.1.call-done), kind=kOutput, calls=%fused_computation.329 | convolution fusion | flops 8120172544 | bytes 21266432 | tf_op jit(solution)/shard_map/et,eh->th/dot_general | solution.py:135
  806.1 11.0 %bitcast_subtract_fusion = f32[8,256,1408]{2,1,0:T(8,128)} fusion(f32[8,256,1408]{2,1,0:T(8,128)S(1)} %bitcast.379, f32[1,8,256,1408]{3,2,1,0:T(8,128)} %param.14), kind=kLoop, calls=%fused_computation.16 | loop fusion | flops 2883584 | bytes 34603008 | tf_op jit(solution)/shard_map/sub | solution.py:136
  832.4 9.5 %copy.154 = f32[8,256,1408]{2,1,0:T(8,128)} copy(f32[8,256,1408]{2,1,0:T(8,128)} %all-gather.10.cloned.1.call-done) | data formatting | bytes 23068672
  842.0 9.5 %copy.155 = f32[8,256,1408]{2,1,0:T(8,128)} copy(f32[8,256,1408]{2,1,0:T(8,128)} %all-gather.24.cloned.1.call-done) | data formatting | bytes 23068672
  851.5 9.5 %copy.156 = f32[8,256,1408]{2,1,0:T(8,128)} copy(f32[8,256,1408]{2,1,0:T(8,128)} %all-gather.26.cloned.1.call-done) | data formatting | bytes 23068672
  (246 shorter events, 276.2 us)
Async XLA Ops:
  7.2 77.1 %reduce-scatter.10.cloned.1.call-start = ((), (), s32[]{:S(2)}) async-start(), calls=%async_computation.11 | async-start | bytes 6488064 | tf_op jit(solution)/shard_map/reduce_scatter | solution.py:71
  21.7 13.8 %copy-start.36 = (f32[8,256,768]{2,1,0:T(8,128)}, f32[8,256,768]{2,1,0:T(8,128)S(1)}, u32[]{:S(2)}) copy-start(f32[8,256,768]{2,1,0:T(8,128)S(1)} %fusion.126) | copy-start | bytes 18874372
  45.7 105.5 %reduce-scatter.12.cloned.1.call-start = ((), (), s32[]{:S(2)}) async-start(), calls=%async_computation.12 | async-start | bytes 12976128 | tf_op jit(solution)/shard_map/reduce_scatter | solution.py:71
  57.0 131.2 %all-gather.18.cloned.1.call-start = ((), (), s32[]{:S(2)}) async-start(), calls=%async_computation.14 | async-start | bytes 6488064 | tf_op jit(solution)/shard_map/all_gather | solution.py:75
  58.7 31.5 %copy-start.24 = (f32[256]{0:T(256)}, f32[256]{0:T(256)S(1)}, u32[]{:S(2)}) copy-start(f32[256]{0:T(256)S(1)} %add_rsqrt_fusion.8) | copy-start | bytes 3076
  90.1 141.0 %all-gather.16.cloned.1.call-start = ((), (), s32[]{:S(2)}) async-start(), calls=%async_computation.13 | async-start | bytes 6488064 | tf_op jit(solution)/shard_map/all_gather | solution.py:75
  154.9 147.9 %reduce-scatter.16.cloned.1.call-start = ((), (), s32[]{:S(2)}) async-start(), calls=%async_computation.17 | async-start | bytes 6488064 | tf_op jit(solution)/shard_map/reduce_scatter | solution.py:71
  175.0 39.6 %copy-start.4 = (bf16[8,2,256,256]{2,3,1,0:T(8,128)(2,1)}, bf16[8,2,256,256]{2,3,1,0:T(8,128)(2,1)S(1)}, u32[]{:S(2)}) copy-start(bf16[8,2,256,256]{2,3,1,0:T(8,128)(2,1)S(1)} %fusion.313) | copy-start | bytes 6291460
  225.9 84.3 %reduce-scatter.14.cloned.1.call-start = ((), (), s32[]{:S(2)}) async-start(), calls=%async_computation.15 | async-start | bytes 6488064 | tf_op jit(solution)/shard_map/reduce_scatter | solution.py:71
  274.8 102.3 %reduce-scatter.8.cloned.1.call-start = ((), (), s32[]{:S(2)}) async-start(), calls=%async_computation.7 | async-start | bytes 12976128 | tf_op jit(solution)/shard_map/reduce_scatter | solution.py:71
  280.0 103.2 %copy-start.32 = (f32[8,256]{1,0:T(8,128)}, f32[8,256]{1,0:T(8,128)S(1)}, u32[]{:S(2)}) copy-start(f32[8,256]{1,0:T(8,128)S(1)} %add_rsqrt_fusion.3) | copy-start | bytes 24580
  301.2 116.1 %all-gather.20.cloned.1.call-start = ((), (), s32[]{:S(2)}) async-start(), calls=%async_computation.16 | async-start | bytes 6488064 | tf_op jit(solution)/shard_map/all_gather | solution.py:75
  382.3 71.5 %all-gather.22.cloned.1.call-start = ((), (), s32[]{:S(2)}) async-start(), calls=%async_computation.18 | async-start | bytes 6488064 | tf_op jit(solution)/shard_map/all_gather | solution.py:75
  383.1 128.0 %reduce-scatter.18.cloned.1.call-start = ((), (), s32[]{:S(2)}) async-start(), calls=%async_computation.19 | async-start | bytes 6488064 | tf_op jit(solution)/shard_map/reduce_scatter | solution.py:71
  475.6 37.4 %copy-start.8 = (bf16[1,256,1408]{2,1,0:T(8,128)(2,1)S(1)}, bf16[1,256,1408]{2,1,0:T(8,128)(2,1)}, u32[]{:S(2)}) copy-start(bf16[1,256,1408]{2,1,0:T(8,128)(2,1)} %reduce-scatter.10.cloned.1.call-done) | copy-start | bytes 2162692
  475.6 37.4 %copy-start.25 = (f32[256]{0:T(256)S(1)}, f32[256]{0:T(256)}, u32[]{:S(2)}) copy-start(f32[256]{0:T(256)} %copy-done.24) | copy-start | bytes 3076
  475.6 37.4 %copy-start.27 = (f32[256]{0:T(256)S(1)}, f32[256]{0:T(256)}, u32[]{:S(2)}) copy-start(f32[256]{0:T(256)} %copy-done.26) | copy-start | bytes 3076
  475.7 97.3 %all-gather.10.cloned.1.call-start = ((), (), s32[]{:S(2)}) async-start(), calls=%async_computation.8 | async-start | bytes 12976128 | tf_op jit(solution)/shard_map/all_gather | solution.py:75
  476.5 157.7 %all-gather.24.cloned.1.call-start = ((), (), s32[]{:S(2)}) async-start(), calls=%async_computation.20 | async-start | bytes 12976128 | tf_op jit(solution)/shard_map/all_gather | solution.py:75
  517.3 189.3 %reduce-scatter.20.cloned.1.call-start = ((), (), s32[]{:S(2)}) async-start(), calls=%async_computation.21 | async-start | bytes 6488064 | tf_op jit(solution)/shard_map/reduce_scatter | solution.py:71
  645.5 17.0 %copy-start.44 = (bf16[8,256,1,2,88]{1,4,3,0,2:T(8,128)(2,1)}, bf16[8,256,1,2,88]{1,4,3,0,2:T(8,128)(2,1)S(1)}, u32[]{:S(2)}) copy-start(bf16[8,256,1,2,88]{1,4,3,0,2:T(8,128)(2,1)S(1)} %fusion.237) | copy-start | bytes 2162692
  671.0 121.3 %all-gather.14.cloned.1.call-start = ((), (), s32[]{:S(2)}) async-start(), calls=%async_computation.10 | async-start | bytes 4460544 | tf_op jit(solution)/shard_map/all_gather | solution.py:75
  673.0 119.3 %all-gather.12.cloned.1.call-start = ((), (), s32[]{:S(2)}) async-start(), calls=%async_computation.9 | async-start | bytes 6488064 | tf_op jit(solution)/shard_map/all_gather | solution.py:75
  678.4 28.2 %copy-start.2 = (f32[1,256,1408]{2,1,0:T(8,128)S(1)}, f32[1,256,1408]{2,1,0:T(8,128)}, u32[]{:S(2)}) copy-start(f32[1,256,1408]{2,1,0:T(8,128)} %get-tuple-element.16) | copy-start | bytes 4325380
  678.4 154.0 %all-gather.26.cloned.1.call-start = ((), (), s32[]{:S(2)}) async-start(), calls=%async_computation.22 | async-start | bytes 12976128 | tf_op jit(solution)/shard_map/all_gather | solution.py:75
  751.2 18.8 %slice-start.11 = ((s8[4325376]{0:T(1024)(128)(4,1)}), s8[4194304]{0:T(1024)(128)(4,1)S(1)}, s32[]{:S(2)}) async-start(s8[4325376]{0:T(1024)(128)(4,1)} %bitcast.383), calls=%async_computation.34 | async-start | bytes 8388608
  760.8 15.5 %slice-start.3 = ((s8[11534336]{0:T(1024)(128)(4,1)}), s8[4194304]{0:T(1024)(128)(4,1)S(1)}, s32[]{:S(2)}) async-start(s8[11534336]{0:T(1024)(128)(4,1)} %bitcast.375), calls=%async_computation.26 | async-start | bytes 8388608
  760.8 15.5 %slice-start.4 = ((s8[11534336]{0:T(1024)(128)(4,1)}), s8[4194304]{0:T(1024)(128)(4,1)S(1)}, s32[]{:S(2)}) async-start(s8[11534336]{0:T(1024)(128)(4,1)} %bitcast.375), calls=%async_computation.27 | async-start | bytes 8388608
  792.3 24.8 %slice-start = ((s8[11534336]{0:T(1024)(128)(4,1)}), s8[4194304]{0:T(1024)(128)(4,1)S(1)}, s32[]{:S(2)}) async-start(s8[11534336]{0:T(1024)(128)(4,1)} %bitcast.373), calls=%async_computation.23 | async-start | bytes 8388608
  792.3 24.8 %slice-start.1 = ((s8[11534336]{0:T(1024)(128)(4,1)}), s8[4194304]{0:T(1024)(128)(4,1)S(1)}, s32[]{:S(2)}) async-start(s8[11534336]{0:T(1024)(128)(4,1)} %bitcast.373), calls=%async_computation.24 | async-start | bytes 8388608
  806.1 14.2 %slice-start.6 = ((s8[11534336]{0:T(1024)(128)(4,1)}), s8[4194304]{0:T(1024)(128)(4,1)S(1)}, s32[]{:S(2)}) async-start(s8[11534336]{0:T(1024)(128)(4,1)} %bitcast.377), calls=%async_computation.29 | async-start | bytes 8388608
  806.1 14.2 %slice-start.7 = ((s8[11534336]{0:T(1024)(128)(4,1)}), s8[4194304]{0:T(1024)(128)(4,1)S(1)}, s32[]{:S(2)}) async-start(s8[11534336]{0:T(1024)(128)(4,1)} %bitcast.377), calls=%async_computation.30 | async-start | bytes 8388608
  (48 other events, 236.4 us)
Sparse Core Ops, SparseCore 0:
  45.8 38.4 reduce-scatter.9
  87.1 64.0 reduce-scatter.11
  153.4 34.7 all-gather.17
  190.2 34.3 all-gather.15
  227.3 35.2 reduce-scatter.15
  274.9 35.2 reduce-scatter.13
  313.1 64.0 reduce-scatter.7
  382.4 34.7 all-gather.19
  419.4 34.3 all-gather.21
  475.8 35.2 reduce-scatter.17
  512.7 60.2 all-gather.9
  575.0 59.1 all-gather.23
  671.1 35.4 reduce-scatter.19
  708.1 28.2 all-gather.13
  737.8 34.1 all-gather.11
  773.5 58.9 all-gather.25

commit v2 on v0

v2 whole, which is shorter than its diff:
```python
import functools

import jax
import jax.numpy as jnp
from jax import lax
from jax.experimental import pallas as pl
from jax.experimental.pallas import tpu as pltpu
from jax.sharding import PartitionSpec as P

EPS = 1e-6
F32, BF16 = jnp.float32, jnp.bfloat16
CORES = 2
VMEM = 60 * 1024 * 1024


def dot(lhs, rhs, lhs_dim, rhs_dim):
    return lax.dot_general(lhs, rhs, (((lhs_dim,), (rhs_dim,)), ((), ())), preferred_element_type=F32)


def later(value, *others):
    return lax.optimization_barrier((value,) + others)[0]


def rms_scale(state):
    return lax.rsqrt(jnp.mean(state * state, axis=-1, keepdims=True) + EPS)


def rms_bf(state):
    return (state * rms_scale(state)).astype(BF16)


def rms_pull(state, cot):
    scale = rms_scale(state)
    normed = state * scale
    return scale * (cot - normed * jnp.mean(normed * cot, axis=-1, keepdims=True))


class Plan:
    def __init__(self, core, n_seq):
        self.core = core
        self.n_seq = n_seq
        self.half = n_seq // CORES

    def after(self, *values):
        return Plan(later(self.core, *values), self.n_seq)

    def seq(self, g, core):
        far = g < self.half
        return CORES * lax.rem(g, self.half) + jnp.where(far, 1 - core[0], core[0])

    def whole(self, rows, cols):
        return pl.BlockSpec((1, rows, cols), lambda g, core: (self.seq(g, core), 0, 0))

    def step(self, rows, cols):
        return pl.BlockSpec((1, rows, cols), lambda g, core: (g, 0, 0))

    def far(self, rows, cols):
        return pl.BlockSpec((1, rows, cols), lambda g, core: (jnp.minimum(g, self.half - 1), 0, 0))

    def near(self, rows, cols):
        return pl.BlockSpec((1, rows, cols), lambda g, core: (jnp.maximum(g - self.half, 0), 0, 0))

    def pair(self, rows, cols):
        return [self.far(rows, cols), self.near(rows, cols)]

    def pair_shape(self, rows, cols, dtype):
        return [jax.ShapeDtypeStruct((self.half, rows, cols), dtype)] * CORES

    @staticmethod
    def layer(index, rows, cols):
        return pl.BlockSpec((1, rows, cols), lambda g, core: (index, 0, 0))

    def call(self, body, name, in_specs, out_specs, out_shape, args, flops, aliases=None):
        n_bytes = sum(x.size * x.dtype.itemsize for x in out_shape)
        return pl.pallas_call(
            body,
            name=name,
            grid_spec=pltpu.PrefetchScalarGridSpec(
                num_scalar_prefetch=1, grid=(self.n_seq,), in_specs=in_specs, out_specs=out_specs
            ),
            out_shape=out_shape,
            input_output_aliases=aliases or {},
            cost_estimate=pl.CostEstimate(flops=int(flops), bytes_accessed=int(n_bytes), transcendentals=0),
            compiler_params=pltpu.CompilerParams(dimension_semantics=("arbitrary",), vmem_limit_bytes=VMEM),
        )(self.core, *args)


def put_pair(half, far_ref, near_ref, value):
    g = pl.program_id(0)

    @pl.when(g < half)
    def _():
        far_ref[0] = value.astype(far_ref.dtype)

    @pl.when(g >= half)
    def _():
        near_ref[0] = value.astype(near_ref.dtype)


def get_pair(half, far_ref, near_ref):
    return jnp.where(pl.program_id(0) < half, far_ref[0], near_ref[0])


def gelu_parts(hidden):
    root = (2.0 / jnp.pi) ** 0.5
    square = hidden * hidden
    bent = jnp.tanh(root * (hidden + 0.044715 * (square * hidden)))
    cdf = 0.5 * (1.0 + bent)
    return hidden * cdf, bent, cdf, root, square


def mlp_forward(plan, state, w_in, w_out, layer):
    n_seq, rows, width = state.shape
    ff = w_in.shape[-1]

    def body(core, x_ref, win_ref, wout_ref, far_ref, near_ref):
        normed = rms_bf(x_ref[0])
        act = gelu_parts(dot(normed, win_ref[0], 1, 0))[0].astype(BF16)
        put_pair(plan.half, far_ref, near_ref, dot(act, wout_ref[0], 1, 0))

    return plan.call(
        body,
        "mlp_forward",
        [plan.whole(rows, width), plan.layer(layer, width, ff), plan.layer(layer, ff, width)],
        plan.pair(rows, width),
        plan.pair_shape(rows, width, F32),
        (state, w_in, w_out),
        4 * n_seq * rows * width * ff,
    )


def mlp_back(plan, state, d_out, w_in, w_out, layer, extra=None):
    n_seq, rows, width = state.shape
    ff = w_in.shape[-1]
    split_d = isinstance(d_out, (list, tuple))
    n_d, n_e = (CORES if split_d else 1), (CORES if extra is not None else 0)

    def body(core, x_ref, *refs):
        d_refs, e_refs, refs = refs[:n_d], refs[n_d : n_d + n_e], refs[n_d + n_e :]
        win_ref, wout_ref, dx_far, dx_near, a_ref, act_ref, dh_ref = refs
        normed = rms_bf(x_ref[0])
        d_bf = get_pair(plan.half, *d_refs) if split_d else d_refs[0][0].astype(BF16)
        hidden = dot(normed, win_ref[0], 1, 0)
        d_act = dot(d_bf, wout_ref[0], 1, 1)
        act, bent, cdf, root, square = gelu_parts(hidden)
        act = act.astype(BF16)
        slope = cdf + 0.5 * hidden * (1.0 - bent * bent) * (root * (1.0 + 3.0 * 0.044715 * square))
        d_hidden = (slope * d_act).astype(BF16)
        d_x = dot(d_hidden, win_ref[0], 1, 1)
        if n_e:
            d_x = d_x + get_pair(plan.half, *e_refs).astype(F32)
        put_pair(plan.half, dx_far, dx_near, d_x)
        a_ref[0] = normed
        act_ref[0] = act
        dh_ref[0] = d_hidden

    in_specs = [plan.whole(rows, width)]
    in_specs += plan.pair(rows, width) if split_d else [plan.whole(rows, width)]
    args = [state] + (list(d_out) if split_d else [d_out])
    if n_e:
        in_specs += plan.pair(rows, width)
        args += list(extra)
    in_specs += [plan.layer(layer, width, ff), plan.layer(layer, ff, width)]
    args += [w_in, w_out]
    out_specs = plan.pair(rows, width) + [plan.step(rows, width), plan.step(rows, ff), plan.step(rows, ff)]
    out_shape = plan.pair_shape(rows, width, BF16) + [
        jax.ShapeDtypeStruct((n_seq, rows, width), BF16),
        jax.ShapeDtypeStruct((n_seq, rows, ff), BF16),
        jax.ShapeDtypeStruct((n_seq, rows, ff), BF16),
    ]
    outs = plan.call(body, "mlp_back", in_specs, out_specs, out_shape, args, 6 * n_seq * rows * width * ff)
    return tuple(outs[:2]), tuple(outs[2:])


def mlp_grads(plan, parts, d_out, layer, n_layers, held):
    normed, act, d_hidden = parts
    n_seq, rows, width = normed.shape
    ff = act.shape[-1]
    split_d = isinstance(d_out, (list, tuple))
    n_d = CORES if split_d else 1
    n_held = 0 if held is None else 2

    def body(core, a_ref, act_ref, dh_ref, *refs):
        d_refs, (dwin_ref, dwout_ref) = refs[:n_d], refs[n_d + n_held :]
        d_bf = get_pair(plan.half, *d_refs) if split_d else d_refs[0][0].astype(BF16)
        d_win = dot(a_ref[0], dh_ref[0], 0, 0)
        d_wout = dot(act_ref[0], d_bf, 0, 0)

        @pl.when(pl.program_id(0) == 0)
        def _():
            dwin_ref[0] = d_win
            dwout_ref[0] = d_wout

        @pl.when(pl.program_id(0) > 0)
        def _():
            dwin_ref[0] += d_win
            dwout_ref[0] += d_wout

    in_specs = [plan.step(rows, width), plan.step(rows, ff), plan.step(rows, ff)]
    in_specs += plan.pair(rows, width) if split_d else [plan.whole(rows, width)]
    args = [normed, act, d_hidden] + (list(d_out) if split_d else [d_out])
    aliases = {}
    if n_held:
        aliases = {len(args) + 1 + i: i for i in range(n_held)}
        in_specs += [pl.BlockSpec(memory_space=pl.ANY)] * n_held
        args += list(held)
    return plan.call(
        body,
        "mlp_grads",
        in_specs,
        [plan.layer(layer, width, ff), plan.layer(layer, ff, width)],
        [jax.ShapeDtypeStruct((n_layers, width, ff), F32), jax.ShapeDtypeStruct((n_layers, ff, width), F32)],
        args,
        4 * n_seq * rows * width * ff,
        aliases,
    )


def softmax(scores):
    powers = jnp.exp(scores - jnp.max(scores, axis=-1, keepdims=True))
    return powers / jnp.sum(powers, axis=-1, keepdims=True)


def attn_forward(plan, state, w_t, layer, n_heads):
    rows, width = state[0].shape[-2:]
    n_seq, depth = plan.n_seq, w_t.shape[1]
    size = depth // 3 // n_heads

    def body(core, far_ref, near_ref, w_ref, out_ref, state_ref):
        x = get_pair(plan.half, far_ref, near_ref)
        state_ref[0] = x
        qkv = dot(w_ref[0], rms_bf(x), 1, 1)
        outs = []
        for head in range(n_heads):
            q, k, v = (qkv[(kind * n_heads + head) * size :][:size].astype(BF16) for kind in range(3))
            probs = softmax(dot(q, k, 0, 0) * size ** -0.5).astype(BF16)
            outs.append(dot(v, probs, 1, 1))
        out_ref[...] = jnp.concatenate(outs, axis=0).astype(BF16)

    return plan.call(
        body,
        "attn_forward",
        plan.pair(rows, width) + [plan.layer(layer, depth, width)],
        [pl.BlockSpec((depth // 3, rows), lambda g, core: (0, plan.seq(g, core))), plan.whole(rows, width)],
        [jax.ShapeDtypeStruct((depth // 3, n_seq * rows), BF16), jax.ShapeDtypeStruct((n_seq, rows, width), F32)],
        (*state, w_t),
        2 * n_seq * rows * width * depth,
    )


def attn_back(plan, state, d_out, w_t, w_o, layer, n_heads, n_layers, held, keep_d=False):
    split_x = isinstance(state, (list, tuple))
    split_d = isinstance(d_out, (list, tuple))
    rows, width = (state[0] if split_x else state).shape[-2:]
    n_seq, depth = plan.n_seq, w_t.shape[1]
    size = depth // 3 // n_heads
    n_x, n_d = (CORES if split_x else 1), (CORES if split_d else 1)
    n_held = 0 if held is None else 2

    def body(core, *refs):
        x_refs, d_refs, refs = refs[:n_x], refs[n_x : n_x + n_d], refs[n_x + n_d :]
        w_ref, wo_ref = refs[:2]
        dx_far, dx_near, dw_ref, dwo_ref = refs[2 + n_held :][:4]
        normed = get_pair(plan.half, *x_refs) if split_x else rms_bf(x_refs[0][0])
        d_all = get_pair(plan.half, *d_refs) if split_d else d_refs[0][0]
        d_bf = d_all.astype(BF16)
        if keep_d:
            refs[-1][0] = d_all
        qkv = dot(w_ref[0], normed, 1, 1)
        d_heads = dot(wo_ref[0], d_bf, 1, 1)
        outs, d_parts = [], [[], [], []]
        for head in range(n_heads):
            q, k, v = (qkv[(kind * n_heads + head) * size :][:size].astype(BF16) for kind in range(3))
            d_head = d_heads[head * size :][:size].astype(BF16)
            probs = softmax(dot(q, k, 0, 0) * size ** -0.5)
            probs_bf = probs.astype(BF16)
            outs.append(dot(v, probs_bf, 1, 1))
            d_probs = dot(d_head, v, 0, 0)
            d_scores = probs * (d_probs - jnp.sum(d_probs * probs, axis=-1, keepdims=True)) * size ** -0.5
            d_scores = d_scores.astype(BF16)
            d_parts[0].append(dot(k, d_scores, 1, 1))
            d_parts[1].append(dot(q, d_scores, 1, 0))
            d_parts[2].append(dot(d_head, probs_bf, 1, 0))
        d_qkv = jnp.concatenate(d_parts[0] + d_parts[1] + d_parts[2], axis=0).astype(BF16)
        put_pair(plan.half, dx_far, dx_near, dot(d_qkv, w_ref[0], 0, 0))
        d_w = dot(d_qkv, normed, 1, 0)
        d_wo = dot(jnp.concatenate(outs, axis=0).astype(BF16), d_bf, 1, 0)

        @pl.when(pl.program_id(0) == 0)
        def _():
            dw_ref[0] = d_w
            dwo_ref[0] = d_wo

        @pl.when(pl.program_id(0) > 0)
        def _():
            dw_ref[0] += d_w
            dwo_ref[0] += d_wo

    in_specs = plan.pair(rows, width) if split_x else [plan.whole(rows, width)]
    in_specs = in_specs + (plan.pair(rows, width) if split_d else [plan.whole(rows, width)])
    in_specs += [plan.layer(layer, depth, width), plan.layer(layer, depth // 3, width)]
    args = (list(state) if split_x else [state]) + (list(d_out) if split_d else [d_out]) + [w_t, w_o]
    aliases = {}
    if n_held:
        aliases = {len(args) + 1 + i: CORES + i for i in range(n_held)}
        in_specs += [pl.BlockSpec(memory_space=pl.ANY)] * n_held
        args += list(held)
    out_specs = plan.pair(rows, width) + [plan.layer(layer, depth, width), plan.layer(layer, depth // 3, width)]
    out_shape = plan.pair_shape(rows, width, BF16)
    out_shape += [jax.ShapeDtypeStruct((n_layers, depth, width), F32), jax.ShapeDtypeStruct((n_layers, depth // 3, width), F32)]
    if keep_d:
        out_specs.append(plan.whole(rows, width))
        out_shape.append(jax.ShapeDtypeStruct((n_seq, rows, width), F32))
    outs = plan.call(body, "attn_back", in_specs, out_specs, out_shape, args, 8 * n_seq * rows * width * depth, aliases)
    return tuple(outs[:2]), tuple(outs[2:4]), (outs[4] if keep_d else None)


def in_order(plan, pair):
    rows, width = pair[0].shape[-2:]

    def body(core, far_ref, near_ref, out_ref):
        out_ref[0] = get_pair(plan.half, far_ref, near_ref)

    shape = jax.ShapeDtypeStruct((plan.n_seq, rows, width), pair[0].dtype)
    specs = plan.pair(rows, width)
    return plan.call(body, "in_order", specs, [plan.whole(rows, width)], [shape], pair, plan.n_seq * rows * width)[0]


def project_out(plan, base, heads, w_o):
    n_seq, rows, width = base.shape
    depth = heads[0].shape[0]

    def body(core, x_ref, h0_ref, h1_ref, w0_ref, w1_ref, out_ref):
        total = dot(h0_ref[...], w0_ref[...], 0, 0) + dot(h1_ref[...], w1_ref[...], 0, 0)
        out_ref[0] = x_ref[0] - total

    head_spec = pl.BlockSpec((depth, rows), lambda g, core: (0, g))
    w_spec = pl.BlockSpec((depth, width), lambda g, core: (0, 0))
    return plan.call(
        body,
        "project_out",
        [plan.step(rows, width), head_spec, head_spec, w_spec, w_spec],
        [plan.step(rows, width)],
        [jax.ShapeDtypeStruct(base.shape, F32)],
        (base, *heads, *w_o),
        4 * n_seq * rows * width * depth,
    )[0]


def solution(mesh):
    act_spec = P("dp", None, None)
    saved_spec = P(None, "dp", None, None)
    weight_specs = (P(None, None, None, "tp", None), P(None, "tp", None, None), P(None, None, "tp"), P(None, "tp", None))
    grad_specs = (P("dp", None, None, "tp", None), P("dp", "tp", None, None), P("dp", None, "tp"), P("dp", "tp", None))
    n_tp = mesh.shape["tp"]
    alike = [list(range(core, n_tp, CORES)) for core in range(CORES)]
    partners = [(i, i + 1 - 2 * (i % CORES)) for i in range(n_tp)]

    def swap(value):
        return lax.ppermute(value, "tp", partners)

    def scatter(pair):
        far, near = pair
        both = near.astype(F32) + swap(far).astype(F32)
        return lax.psum_scatter(both.astype(far.dtype), "tp", scatter_dimension=0, axis_index_groups=alike, tiled=True)

    def gather(shard, *others):
        near = lax.all_gather(shard, "tp", axis=0, axis_index_groups=alike, tiled=True)
        near = later(near, *others)
        return swap(near), near

    def per_device(y_one, y_two, dy_one, dy_two, saved_one, saved_two, w_qkv, w_o, w_in, w_out):
        n_layers, width, _, n_heads, size = w_qkv.shape
        n_pairs = saved_one.shape[0]
        me = lax.axis_index("tp")
        core = lax.rem(me, CORES)
        plan = Plan(core.reshape(1).astype(jnp.int32), y_one.shape[0])
        w_t = jnp.transpose(w_qkv, (0, 2, 3, 4, 1)).reshape(n_layers, 3 * n_heads * size, width)
        w_o2 = w_o.reshape(n_layers, n_heads * size, width)

        def own(state):
            return lax.dynamic_slice_in_dim(state, me, 1, 0)

        wo_low = gather(w_o2[0])
        top = n_layers - 1
        dx_pair, parts = mlp_back(plan, y_one, dy_two, w_in, w_out, top)
        g_back = scatter(dx_pair)
        g_top = mlp_forward(plan.after(dx_pair[0], wo_low[1]), y_one, w_in, w_out, top)
        mlp_held = mlp_grads(plan.after(g_top[0]), parts, dy_two, top, n_layers, None)
        d_one = own(dy_one) + rms_pull(own(y_one), later(g_back, mlp_held[0]).astype(F32))
        g_sum, x_two_out = scatter(g_top), own(y_two)
        d_two, attn_held, last = own(dy_two), None, mlp_held[0]

        for layer_pair in reversed(range(n_pairs)):
            s_one, s_two = saved_one[layer_pair], saved_two[layer_pair]
            mid, low = 2 * layer_pair + 1, 2 * layer_pair
            g_part = mlp_forward(plan.after(last), s_one, w_in, w_out, low)
            d_one_bf = gather(d_one.astype(BF16), g_part[0])
            mid_back, attn_held, _ = attn_back(
                plan.after(g_part[0]), s_two, d_one_bf, w_t, w_o2, mid, n_heads, n_layers, attn_held
            )
            x_two_shard = x_two_out - later(g_sum, mid_back[0])
            f_in = gather(rms_bf(x_two_shard))
            g_sum, x_two_out = scatter(g_part), own(s_two)
            f_back, attn_held, _ = attn_back(
                plan.after(mid_back[0]), f_in, d_one_bf, w_t, w_o2, mid + 1, n_heads, n_layers, attn_held
            )
            d_two = d_two + rms_pull(x_two_shard, scatter(f_back).astype(F32))
            mid_d = gather(d_two.astype(BF16))
            d_two = d_two + rms_pull(own(s_two), scatter(mid_back).astype(F32))
            low_d = gather(d_two.astype(BF16))
            dx_pair, mid_parts = mlp_back(plan, s_one, mid_d, w_in, w_out, mid)
            x_two_shard = x_two_out - later(g_sum, dx_pair[0])
            dx_pair, low_parts = mlp_back(plan, s_one, low_d, w_in, w_out, low, dx_pair)
            heads, x_two = attn_forward(plan.after(dx_pair[0]), gather(x_two_shard), w_t, low, n_heads)
            d_one = d_one + rms_pull(own(s_one), scatter(dx_pair).astype(F32))
            if layer_pair:
                last = dx_pair[0]
                g_sum, x_two_out = jnp.zeros_like(x_two_shard), x_two_shard
                mlp_held = mlp_grads(plan, mid_parts, mid_d, mid, n_layers, mlp_held)
                mlp_held = mlp_grads(plan, low_parts, low_d, low, n_layers, mlp_held)
        f_back, attn_held, d_one_full = attn_back(
            plan.after(heads), x_two, gather(d_one), w_t, w_o2, 0, n_heads, n_layers, attn_held, True
        )
        heads_all = gather(heads)
        d_two = d_two + rms_pull(x_two_shard, scatter((f_back[0], later(f_back[1], heads_all[1]))).astype(F32))
        tail = plan.after(f_back[0])
        mlp_held = mlp_grads(tail, mid_parts, mid_d, 1, n_layers, mlp_held)
        mlp_held = mlp_grads(tail, low_parts, low_d, 0, n_layers, mlp_held)
        x_one = project_out(tail, s_one, heads_all, wo_low)
        d_two_full = in_order(plan, gather(d_two, x_one, mlp_held[0]))
        d_w = jnp.transpose(attn_held[0].reshape(n_layers, 3, n_heads, size, width), (0, 4, 1, 2, 3))
        d_wo = attn_held[1].reshape(n_layers, n_heads, size, width)
        return (x_one, x_two, d_one_full, d_two_full, d_w, d_wo) + tuple(mlp_held)

    return jax.shard_map(
        per_device,
        mesh=mesh,
        in_specs=(act_spec,) * 4 + (saved_spec,) * 2 + weight_specs,
        out_specs=(act_spec,) * 4 + grad_specs,
        check_vma=False,
    )
```

time: 1450 us -> 831 us (0.57)
  waiting for transfers between devices: 873 us -> 363 us
  Pallas kernels: 0 us -> 358 us
  matrix products: 340 us -> 0 us
  other arithmetic: 189 us -> 70.5 us
  local copies, waits for them, and re-layouts: 27.9 us -> 4.97 us
    psum x4 -> x0, waiting for transfers between devices: 873 us -> none  [the longest x1 305 us: reversible_block(): x_two = y_two - lax.psum(g_part, 'tp')]
    pallas_call x0 -> x14, Pallas kernels: none -> 358 us  [call(): pl.pallas_call(body, name=name, grid_spec=pltpu.PrefetchScalarGridSpec(nu...]
    dot_general x49 -> x0, matrix products: 340 us -> none  [the longest x3 37.3 us: mlp_backward(): jnp.einsum('bsh,fh->bsf', d_bf, w_out, preferred_element_type=jnp.float32)]
    all_gather x0 -> x9, waiting for transfers between devices: none -> 215 us  [gather(): lax.all_gather(shard, 'tp', axis=0, axis_index_groups=alike, tiled=True)]
    reduce_scatter x0 -> x7, waiting for transfers between devices: none -> 97.2 us  [scatter(): lax.psum_scatter(both.astype(far.dtype), 'tp', scatter_dimension=0, axis_...]
    reduce_sum x9 -> x10, other arithmetic: 80 us -> 18.4 us  [the longest x5 9.76 us: rms_scale(): return lax.rsqrt(jnp.mean(state * state, axis=-1, keepdims=True) + EPS)]
    ppermute x0 -> x16, waiting for transfers between devices: none -> 49.1 us  [swap(): return lax.ppermute(value, 'tp', partners)]
    add x3 -> x4, other arithmetic: 47.8 us -> 21.6 us  [the longest x2 14.9 us: scatter(): both = near.astype(F32) + swap(far).astype(F32)]
  transfers between devices with their start and end apart: 4 -> 32, of which waited for: 4 -> 19; matrix products, arithmetic and copies ran while one was open for 11% -> 7% of each run, Pallas kernels for 0% -> 39%
where the time goes in v2:
time: 831 us; the launch traced here: 823 us
  waiting for transfers between devices  363 us (44%)
  Pallas kernels  358 us (43%)
  other arithmetic  70.5 us (8%)
  between operations  14.6 us (2%)
  starting transfers between devices  12.5 us (2%)
    pallas_call x14, Pallas kernels, call(): pl.pallas_call(body, name=name, grid_spec=pltpu.PrefetchScalarGridSpec(nu...  358 us
    all_gather x9, waiting for transfers between devices, gather(): lax.all_gather(shard, 'tp', axis=0, axis_index_groups=alike, tiled=True)  215 us
    reduce_scatter x7, waiting for transfers between devices, scatter(): lax.psum_scatter(both.astype(far.dtype), 'tp', scatter_dimension=0, axis_...  97.2 us
    ppermute x16, waiting for transfers between devices, swap(): return lax.ppermute(value, 'tp', partners)  49.1 us
    convert_element_type x5, other arithmetic, scatter(): both.astype(far.dtype)  22.1 us
  transfers between devices with their start and end apart: 32, of which 19 were waited for; matrix products, arithmetic and copies ran while one was open for 7% of the time, Pallas kernels for 39%

profile of v2, /device:TPU:113, one launch (start us, length us, event | category | flops | bytes accessed | tf_op | source)
XLA Modules:
  0.0 822.9 jit_solution(10145019792297870769)
XLA Ops:
  7.3 24.1 %mlp_back.3 = (bf16[4,256,1408]{2,1,0:T(8,128)(2,1)}, bf16[4,256,1408]{2,1,0:T(8,128)(2,1)}, bf16[8,256,1408]{2,1,0:T(8,128)(2,1)}, bf16[8,256,768]{2,1,0:T(8,128)(2,1)}, bf16[8,256,768]{2,1,0:T(8,128)(2,1)}) custom-call(s32[1]{0:T(128)} %bitcast.core, f32[8,256,1408]{2,1,0:T(8,128)} %x_ref.3, f32[8,256,1408]{2,1,0:T(8,128)} %refs_0_.3, ...), custom_call_target="tpu_custom_call" | custom-call | flops 13287555072 | bytes 17825792 | tf_op jit(solution)/shard_map/mlp_back/pallas_call | solution.py:75
  42.7 19.0 %all-gather.10.cloned.1.call-done.w1_ref = bf16[704,1408]{1,0:T(8,128)(2,1)} async-done(((bf16[176,1408]{1,0:T(8,128)(2,1)}), bf16[704,1408]{1,0:T(8,128)(2,1)}) %all-gather.10.cloned.1.call-update) | async-done | bytes 1982480 | tf_op jit(solution)/shard_map/all_gather | solution.py:368
  61.7 20.2 %mlp_forward.2 = (f32[4,256,1408]{2,1,0:T(8,128)}, f32[4,256,1408]{2,1,0:T(8,128)}) custom-call(s32[1]{0:T(128)} %bitcast.core, f32[8,256,1408]{2,1,0:T(8,128)} %x_ref.3, bf16[3,1408,768]{2,1,0:T(8,128)(2,1)} %refs_4_.1, bf16[3,768,1408]{2,1,0:T(8,128)(2,1)} %refs_5_.1), custom_call_target="tpu_custom_call" | custom-call | flops 8858370048 | bytes 11534336 | tf_op jit(solution)/shard_map/mlp_forward/pallas_call | solution.py:75
  82.9 23.0 %mlp_grads.3 = (f32[3,1408,768]{2,1,0:T(8,128)}, f32[3,768,1408]{2,1,0:T(8,128)}) custom-call(s32[1]{0:T(128)} %bitcast.core, bf16[8,256,1408]{2,1,0:T(8,128)(2,1)} %get-tuple-element.67.a_ref, bf16[8,256,768]{2,1,0:T(8,128)(2,1)} %get-tuple-element.68.act_ref, bf16[8,256,768]{2,1,0:T(8,128)(2,1)} %get-tuple-element.69.dh_ref, f32[8,256,1408]{2,1,0:T(8,128)} %refs_0_.3), custom_call_target="tpu_custom_call" | custom-call | flops 8858370048 | bytes 25952256 | tf_op jit(solution)/shard_map/mlp_grads/pallas_call | solution.py:75
  111.2 7.4 add.101
  119.0 20.3 %mlp_forward.3 = (f32[4,256,1408]{2,1,0:T(8,128)}, f32[4,256,1408]{2,1,0:T(8,128)}) custom-call(s32[1]{0:T(128)} %bitcast.core, f32[8,256,1408]{2,1,0:T(8,128)} %bitcast.33, bf16[3,1408,768]{2,1,0:T(8,128)(2,1)} %refs_4_.1, bf16[3,768,1408]{2,1,0:T(8,128)(2,1)} %refs_5_.1), custom_call_target="tpu_custom_call" | custom-call | flops 8858370048 | bytes 11534336 | tf_op jit(solution)/shard_map/mlp_forward/pallas_call | solution.py:75
  150.8 42.6 %attn_back.3 = (bf16[4,256,1408]{2,1,0:T(8,128)(2,1)}, bf16[4,256,1408]{2,1,0:T(8,128)(2,1)}, f32[3,528,1408]{2,1,0:T(8,128)}, f32[3,176,1408]{2,1,0:T(8,128)}) custom-call(s32[1]{0:T(128)} %bitcast.core, f32[8,256,1408]{2,1,0:T(8,128)} %bitcast.41, bf16[4,256,1408]{2,1,0:T(8,128)(2,1)} %copy-done.3, ...), custom_call_target="tpu_custom_call" | custom-call | flops 12180258816 | bytes 17661952 | tf_op jit(solution)/shard_map/attn_back/pallas_call | solution.py:75
  193.4 8.6 %reduce-scatter.8.cloned.1.call-done = f32[1,256,1408]{2,1,0:T(8,128)} async-done(((f32[4,256,1408]{2,1,0:T(8,128)}), f32[1,256,1408]{2,1,0:T(8,128)}) %reduce-scatter.8.cloned.1.call-update) | async-done | bytes 1441808 | tf_op jit(solution)/shard_map/reduce_scatter | solution.py:365
  206.2 31.7 %all-gather.14.cloned.1.call-done.refs_1_ = bf16[4,256,1408]{2,1,0:T(8,128)(2,1)} async-done(((bf16[1,256,1408]{2,1,0:T(8,128)(2,1)}), bf16[4,256,1408]{2,1,0:T(8,128)(2,1)}) %all-gather.14.cloned.1.call-update) | async-done | bytes 2883600 | tf_op jit(solution)/shard_map/all_gather | solution.py:368
  243.9 41.5 %attn_back.4 = (bf16[4,256,1408]{2,1,0:T(8,128)(2,1)}, bf16[4,256,1408]{2,1,0:T(8,128)(2,1)}, f32[3,528,1408]{2,1,0:T(8,128)}, f32[3,176,1408]{2,1,0:T(8,128)}) custom-call(s32[1]{0:T(128)} %bitcast.core, bf16[4,256,1408]{2,1,0:T(8,128)(2,1)} %collective-permute-done.3.refs_0_, ...), custom_call_target="tpu_custom_call", output_to_operand_aliasing={{2}: (7, {}), {3}: (8, {})} | custom-call | flops 12180258816 | bytes 17661952 | tf_op jit(solution)/shard_map/attn_back/pallas_call | solution.py:75
  285.6 5.2 collective-permute-done.4
  298.7 27.9 %reduce-scatter.12.cloned.1.call-done = bf16[1,256,1408]{2,1,0:T(8,128)(2,1)} async-done(((bf16[4,256,1408]{2,1,0:T(8,128)(2,1)}), bf16[1,256,1408]{2,1,0:T(8,128)(2,1)}) %reduce-scatter.12.cloned.1.call-update) | async-done | bytes 720912 | tf_op jit(solution)/shard_map/reduce_scatter | solution.py:365
  333.3 8.9 %collective-permute-done.8 = f32[4,256,1408]{2,1,0:T(8,128)} collective-permute-done((f32[4,256,1408]{2,1,0:T(8,128)}, f32[4,256,1408]{2,1,0:T(8,128)}, u32[]{:S(2)}, u32[]{:S(2)}) %collective-permute-start.8) | collective-permute-done | bytes 5767200 | tf_op jit(solution)/shard_map/ppermute | solution.py:360
  342.2 7.4 add.111
  349.8 15.1 %all-gather.18.cloned.1.call-done.refs_1_ = bf16[4,256,1408]{2,1,0:T(8,128)(2,1)} async-done(((bf16[1,256,1408]{2,1,0:T(8,128)(2,1)}), bf16[4,256,1408]{2,1,0:T(8,128)(2,1)}) %all-gather.18.cloned.1.call-update) | async-done | bytes 2883600 | tf_op jit(solution)/shard_map/all_gather | solution.py:368
  365.8 34.4 %all-gather.16.cloned.1.call-done.refs_1_ = bf16[4,256,1408]{2,1,0:T(8,128)(2,1)} async-done(((bf16[1,256,1408]{2,1,0:T(8,128)(2,1)}), bf16[4,256,1408]{2,1,0:T(8,128)(2,1)}) %all-gather.16.cloned.1.call-update) | async-done | bytes 2883600 | tf_op jit(solution)/shard_map/all_gather | solution.py:368
  401.2 24.3 %mlp_back.4 = (bf16[4,256,1408]{2,1,0:T(8,128)(2,1)}, bf16[4,256,1408]{2,1,0:T(8,128)(2,1)}, bf16[8,256,1408]{2,1,0:T(8,128)(2,1)}, bf16[8,256,768]{2,1,0:T(8,128)(2,1)}, bf16[8,256,768]{2,1,0:T(8,128)(2,1)}) custom-call(s32[1]{0:T(128)} %bitcast.core, f32[8,256,1408]{2,1,0:T(8,128)} %bitcast.34, bf16[4,256,1408]{2,1,0:T(8,128)(2,1)} %collective-permute-done.7.refs_0_, ...), custom_call_target="tpu_custom_call" | custom-call | flops 13287555072 | bytes 17825792 | tf_op jit(solution)/shard_map/mlp_back/pallas_call | solution.py:75
  425.5 25.0 %mlp_back.5 = (bf16[4,256,1408]{2,1,0:T(8,128)(2,1)}, bf16[4,256,1408]{2,1,0:T(8,128)(2,1)}, bf16[8,256,1408]{2,1,0:T(8,128)(2,1)}, bf16[8,256,768]{2,1,0:T(8,128)(2,1)}, bf16[8,256,768]{2,1,0:T(8,128)(2,1)}) custom-call(s32[1]{0:T(128)} %bitcast.core, f32[8,256,1408]{2,1,0:T(8,128)} %bitcast.35, bf16[4,256,1408]{2,1,0:T(8,128)(2,1)} %collective-permute-done.6.refs_0_, ...), custom_call_target="tpu_custom_call" | custom-call | flops 13287555072 | bytes 17825792 | tf_op jit(solution)/shard_map/mlp_back/pallas_call | solution.py:75
  450.5 5.3 collective-permute-done.10
  464.8 28.7 %reduce-scatter.18.cloned.1.call-done = bf16[1,256,1408]{2,1,0:T(8,128)(2,1)} async-done(((bf16[4,256,1408]{2,1,0:T(8,128)(2,1)}), bf16[1,256,1408]{2,1,0:T(8,128)(2,1)}) %reduce-scatter.18.cloned.1.call-update) | async-done | bytes 720912 | tf_op jit(solution)/shard_map/reduce_scatter | solution.py:365
  499.8 52.1 %all-gather.20.cloned.1.call-done.near_ref = f32[4,256,1408]{2,1,0:T(8,128)} async-done(((f32[1,256,1408]{2,1,0:T(8,128)}), f32[4,256,1408]{2,1,0:T(8,128)}) %all-gather.20.cloned.1.call-update) | async-done | bytes 5767184 | tf_op jit(solution)/shard_map/all_gather | solution.py:368
  552.8 59.0 %all-gather.22.cloned.1.call-done.refs_2_ = f32[4,256,1408]{2,1,0:T(8,128)} async-done(((f32[1,256,1408]{2,1,0:T(8,128)}), f32[4,256,1408]{2,1,0:T(8,128)}) %all-gather.22.cloned.1.call-update) | async-done | bytes 5767184 | tf_op jit(solution)/shard_map/all_gather | solution.py:368
  612.7 17.7 %attn_forward.1 = (bf16[176,2048]{1,0:T(8,128)(2,1)}, f32[8,256,1408]{2,1,0:T(8,128)}) custom-call(s32[1]{0:T(128)} %bitcast.core, f32[4,256,1408]{2,1,0:T(8,128)} %collective-permute-done.9.far_ref, f32[4,256,1408]{2,1,0:T(8,128)} %all-gather.20.cloned.1.call-done.near_ref, bf16[3,528,1408]{2,1,0:T(8,128)(2,1)} %bitcast.39), custom_call_target="tpu_custom_call" | custom-call | flops 3045064704 | bytes 12255232 | tf_op jit(solution)/shard_map/attn_forward/pallas_call | solution.py:75
  630.8 43.9 %attn_back.5 = (bf16[4,256,1408]{2,1,0:T(8,128)(2,1)}, bf16[4,256,1408]{2,1,0:T(8,128)(2,1)}, f32[3,528,1408]{2,1,0:T(8,128)}, f32[3,176,1408]{2,1,0:T(8,128)}, f32[8,256,1408]{2,1,0:T(8,128)}) custom-call(s32[1]{0:T(128)} %bitcast.core, f32[8,256,1408]{2,1,0:T(8,128)} %get-tuple-element.55.refs_0_, ...), custom_call_target="tpu_custom_call", output_to_operand_aliasing={{2}: (6, {}), {3}: (7, {})} | custom-call | flops 12180258816 | bytes 29196288 | tf_op jit(solution)/shard_map/attn_back/pallas_call | solution.py:75
  674.8 5.2 collective-permute-done.14
  685.0 32.0 %reduce-scatter.20.cloned.1.call-done = bf16[1,256,1408]{2,1,0:T(8,128)(2,1)} async-done(((bf16[4,256,1408]{2,1,0:T(8,128)(2,1)}), bf16[1,256,1408]{2,1,0:T(8,128)(2,1)}) %reduce-scatter.20.cloned.1.call-update) | async-done | bytes 720912 | tf_op jit(solution)/shard_map/reduce_scatter | solution.py:365
  722.2 7.7 collective-permute-done.13.w0_ref
  731.4 17.8 %project_out.1 = f32[8,256,1408]{2,1,0:T(8,128)} custom-call(s32[1]{0:T(128)} %bitcast.core, f32[8,256,1408]{2,1,0:T(8,128)} %bitcast.36, bf16[704,2048]{1,0:T(8,128)(2,1)} %copy-done.2, bf16[704,2048]{1,0:T(8,128)(2,1)} %all-gather.24.cloned.1.call-done.h1_ref, bf16[704,1408]{1,0:T(8,128)(2,1)} %collective-permute-done.13.w0_ref, ...), custom_call_target="tpu_custom_call" | custom-call | flops 8120172544 | bytes 11534336 | tf_op jit(solution)/shard_map/project_out/pallas_call | solution.py:75
  749.2 23.0 %mlp_grads.4 = (f32[3,1408,768]{2,1,0:T(8,128)}, f32[3,768,1408]{2,1,0:T(8,128)}) custom-call(s32[1]{0:T(128)} %bitcast.core, bf16[8,256,1408]{2,1,0:T(8,128)(2,1)} %get-tuple-element.105.a_ref, bf16[8,256,768]{2,1,0:T(8,128)(2,1)} %get-tuple-element.106.act_ref, ...), custom_call_target="tpu_custom_call", output_to_operand_aliasing={{0}: (6, {}), {1}: (7, {})} | custom-call | flops 8858370048 | bytes 25952256 | tf_op jit(solution)/shard_map/mlp_grads/pallas_call | solution.py:75
  772.1 23.0 %mlp_grads.5 = (f32[3,1408,768]{2,1,0:T(8,128)}, f32[3,768,1408]{2,1,0:T(8,128)}) custom-call(s32[1]{0:T(128)} %bitcast.core, bf16[8,256,1408]{2,1,0:T(8,128)(2,1)} %get-tuple-element.102.a_ref, bf16[8,256,768]{2,1,0:T(8,128)(2,1)} %get-tuple-element.103.act_ref, ...), custom_call_target="tpu_custom_call", output_to_operand_aliasing={{0}: (6, {}), {1}: (7, {})} | custom-call | flops 8858370048 | bytes 25952256 | tf_op jit(solution)/shard_map/mlp_grads/pallas_call | solution.py:75
  795.4 9.0 %collective-permute-done.15.far_ref = f32[4,256,1408]{2,1,0:T(8,128)} collective-permute-done((f32[4,256,1408]{2,1,0:T(8,128)}, f32[4,256,1408]{2,1,0:T(8,128)}, u32[]{:S(2)}, u32[]{:S(2)}) %collective-permute-start.15) | collective-permute-done | bytes 5767200 | tf_op jit(solution)/shard_map/ppermute | solution.py:360
  804.4 11.4 %in_order.1 = f32[8,256,1408]{2,1,0:T(8,128)} custom-call(s32[1]{0:T(128)} %bitcast.core, f32[4,256,1408]{2,1,0:T(8,128)} %collective-permute-done.15.far_ref, f32[4,256,1408]{2,1,0:T(8,128)} %all-gather.26.cloned.1.call-done.near_ref), custom_call_target="tpu_custom_call" | custom-call | flops 2883584 | bytes 11534336 | tf_op jit(solution)/shard_map/in_order/pallas_call | solution.py:75
  (103 shorter events, 86.0 us)
Async XLA Ops:
  7.2 54.6 %all-gather.10.cloned.1.call-start = ((), (), s32[]{:S(2)}) async-start(), calls=%async_computation.7 | async-start | bytes 2478080 | tf_op jit(solution)/shard_map/all_gather | solution.py:368
  31.3 5.6 collective-permute-start.1
  34.0 71.9 %reduce-scatter.10.cloned.1.call-start = ((), (), s32[]{:S(2)}) async-start(), calls=%async_computation.9 | async-start | bytes 3604480 | tf_op jit(solution)/shard_map/reduce_scatter | solution.py:365
  41.1 102.3 %all-gather.12.cloned.1.call-start = ((), (), s32[]{:S(2)}) async-start(), calls=%async_computation.10 | async-start | bytes 3604480 | tf_op jit(solution)/shard_map/all_gather | solution.py:368
  82.0 29.2 %collective-permute-start = (f32[4,256,1408]{2,1,0:T(8,128)}, f32[4,256,1408]{2,1,0:T(8,128)}, u32[]{:S(2)}, u32[]{:S(2)}) collective-permute-start(f32[4,256,1408]{2,1,0:T(8,128)} %get-tuple-element.65), channel_id=1, source_target_pairs={{0,1},{1,0},{2,3},{3,2},{4,5},{5,4},{6,7},{7,6},{8,9},{9,8},{10,11... | collective-permute-start | bytes 17301512 | tf_op jit(solution)/shard_map/ppermute | solution.py:360
  111.1 90.9 %reduce-scatter.8.cloned.1.call-start = ((), (), s32[]{:S(2)}) async-start(), calls=%async_computation.8 | async-start | bytes 7208960 | tf_op jit(solution)/shard_map/reduce_scatter | solution.py:365
  118.7 119.2 %all-gather.14.cloned.1.call-start = ((), (), s32[]{:S(2)}) async-start(), calls=%async_computation.11 | async-start | bytes 3604480 | tf_op jit(solution)/shard_map/all_gather | solution.py:368
  143.4 5.8 collective-permute-start.2
  205.1 91.6 %reduce-scatter.14.cloned.1.call-start = ((), (), s32[]{:S(2)}) async-start(), calls=%async_computation.13 | async-start | bytes 3604480 | tf_op jit(solution)/shard_map/reduce_scatter | solution.py:365
  205.2 33.6 %collective-permute-start.5 = (bf16[4,256,1408]{2,1,0:T(8,128)(2,1)}, bf16[4,256,1408]{2,1,0:T(8,128)(2,1)}, u32[]{:S(2)}, u32[]{:S(2)}) collective-permute-start(bf16[4,256,1408]{2,1,0:T(8,128)(2,1)} %get-tuple-element.77), channel_id=1, source_target_pairs={{0,1},{1,0},{2,3},{3,2},{4,5},{5,4},{6,7},{7,6},{8,9},{9,8},{10,11... | collective-permute-start | bytes 8650760 | tf_op jit(solution)/shard_map/ppermute | solution.py:360
  237.9 6.0 collective-permute-start.3
  243.8 82.8 %reduce-scatter.12.cloned.1.call-start = ((), (), s32[]{:S(2)}) async-start(), calls=%async_computation.12 | async-start | bytes 3604480 | tf_op jit(solution)/shard_map/reduce_scatter | solution.py:365
  285.4 5.4 collective-permute-start.4
  294.9 70.0 %all-gather.18.cloned.1.call-start = ((), (), s32[]{:S(2)}) async-start(), calls=%async_computation.15 | async-start | bytes 3604480 | tf_op jit(solution)/shard_map/all_gather | solution.py:368
  332.2 68.1 %all-gather.16.cloned.1.call-start = ((), (), s32[]{:S(2)}) async-start(), calls=%async_computation.14 | async-start | bytes 3604480 | tf_op jit(solution)/shard_map/all_gather | solution.py:368
  332.2 10.0 %collective-permute-start.8 = (f32[4,256,1408]{2,1,0:T(8,128)}, f32[4,256,1408]{2,1,0:T(8,128)}, u32[]{:S(2)}, u32[]{:S(2)}) collective-permute-start(f32[4,256,1408]{2,1,0:T(8,128)} %get-tuple-element.72), channel_id=1, source_target_pairs={{0,1},{1,0},{2,3},{3,2},{4,5},{5,4},{6,7},{7,6},{8,9},{9,8},{10,11... | collective-permute-start | bytes 17301512 | tf_op jit(solution)/shard_map/ppermute | solution.py:360
  333.3 126.8 %reduce-scatter.16.cloned.1.call-start = ((), (), s32[]{:S(2)}) async-start(), calls=%async_computation.16 | async-start | bytes 7208960 | tf_op jit(solution)/shard_map/reduce_scatter | solution.py:365
  349.7 143.8 %reduce-scatter.18.cloned.1.call-start = ((), (), s32[]{:S(2)}) async-start(), calls=%async_computation.18 | async-start | bytes 3604480 | tf_op jit(solution)/shard_map/reduce_scatter | solution.py:365
  364.9 36.3 %collective-permute-start.7 = (bf16[4,256,1408]{2,1,0:T(8,128)(2,1)}, bf16[4,256,1408]{2,1,0:T(8,128)(2,1)}, u32[]{:S(2)}, u32[]{:S(2)}) collective-permute-start(bf16[4,256,1408]{2,1,0:T(8,128)(2,1)} %all-gather.18.cloned.1.call-done.refs_1_), channel_id=1, source_target_pairs={{0,1},{1,0},{2,3},{3,2},{4,5},{5,4},{6,7},{7,6},{8,9},{9,8},{10,11... | collective-permute-start | bytes 8650760 | tf_op jit(solution)/shard_map/ppermute | solution.py:360
  400.2 25.2 %collective-permute-start.6 = (bf16[4,256,1408]{2,1,0:T(8,128)(2,1)}, bf16[4,256,1408]{2,1,0:T(8,128)(2,1)}, u32[]{:S(2)}, u32[]{:S(2)}) collective-permute-start(bf16[4,256,1408]{2,1,0:T(8,128)(2,1)} %all-gather.16.cloned.1.call-done.refs_1_), channel_id=1, source_target_pairs={{0,1},{1,0},{2,3},{3,2},{4,5},{5,4},{6,7},{7,6},{8,9},{9,8},{10,11... | collective-permute-start | bytes 8650760 | tf_op jit(solution)/shard_map/ppermute | solution.py:360
  450.5 5.3 collective-permute-start.10
  459.9 91.9 %all-gather.20.cloned.1.call-start = ((), (), s32[]{:S(2)}) async-start(), calls=%async_computation.17 | async-start | bytes 7208960 | tf_op jit(solution)/shard_map/all_gather | solution.py:368
  463.1 148.7 %all-gather.22.cloned.1.call-start = ((), (), s32[]{:S(2)}) async-start(), calls=%async_computation.19 | async-start | bytes 7208960 | tf_op jit(solution)/shard_map/all_gather | solution.py:368
  499.7 175.0 %all-gather.24.cloned.1.call-start = ((), (), s32[]{:S(2)}) async-start(), calls=%async_computation.20 | async-start | bytes 3604480 | tf_op jit(solution)/shard_map/all_gather | solution.py:368
  551.9 60.9 %collective-permute-start.9 = (f32[4,256,1408]{2,1,0:T(8,128)}, f32[4,256,1408]{2,1,0:T(8,128)}, u32[]{:S(2)}, u32[]{:S(2)}) collective-permute-start(f32[4,256,1408]{2,1,0:T(8,128)} %all-gather.20.cloned.1.call-done.near_ref), channel_id=1, source_target_pairs={{0,1},{1,0},{2,3},{3,2},{4,5},{5,4},{6,7},{7,6},{8,9},{9,8},{10,11... | collective-permute-start | bytes 17301512 | tf_op jit(solution)/shard_map/ppermute | solution.py:360
  611.8 19.0 %collective-permute-start.11 = (f32[4,256,1408]{2,1,0:T(8,128)}, f32[4,256,1408]{2,1,0:T(8,128)}, u32[]{:S(2)}, u32[]{:S(2)}) collective-permute-start(f32[4,256,1408]{2,1,0:T(8,128)} %all-gather.22.cloned.1.call-done.refs_2_), channel_id=1, source_target_pairs={{0,1},{1,0},{2,3},{3,2},{4,5},{5,4},{6,7},{7,6},{8,9},{9,8},{10,11... | collective-permute-start | bytes 17301512 | tf_op jit(solution)/shard_map/ppermute | solution.py:360
  630.5 86.5 %reduce-scatter.20.cloned.1.call-start = ((), (), s32[]{:S(2)}) async-start(), calls=%async_computation.21 | async-start | bytes 3604480 | tf_op jit(solution)/shard_map/reduce_scatter | solution.py:365
  674.7 5.2 collective-permute-start.14
  685.0 110.1 %all-gather.26.cloned.1.call-start = ((), (), s32[]{:S(2)}) async-start(), calls=%async_computation.22 | async-start | bytes 7208960 | tf_op jit(solution)/shard_map/all_gather | solution.py:368
  721.1 8.7 %collective-permute-start.12 = (bf16[704,2048]{1,0:T(8,128)(2,1)}, bf16[704,2048]{1,0:T(8,128)(2,1)S(1)}, u32[]{:S(2)}, u32[]{:S(2)}) collective-permute-start(bf16[704,2048]{1,0:T(8,128)(2,1)} %all-gather.24.cloned.1.call-done.h1_ref), channel_id=1, source_target_pairs={{0,1},{1,0},{2,3},{3,2},{4,5},{5,4},{6,7},{7,6},{8,9},{9,8},{10,11... | collective-permute-start | bytes 8650760 | tf_op jit(solution)/shard_map/ppermute | solution.py:360
  722.1 7.7 collective-permute-start.13
  795.1 9.4 %collective-permute-start.15 = (f32[4,256,1408]{2,1,0:T(8,128)}, f32[4,256,1408]{2,1,0:T(8,128)}, u32[]{:S(2)}, u32[]{:S(2)}) collective-permute-start(f32[4,256,1408]{2,1,0:T(8,128)} %all-gather.26.cloned.1.call-done.near_ref), channel_id=1, source_target_pairs={{0,1},{1,0},{2,3},{3,2},{4,5},{5,4},{6,7},{7,6},{8,9},{9,8},{10,11... | collective-permute-start | bytes 17301512 | tf_op jit(solution)/shard_map/ppermute | solution.py:360
  (4 other events, 67.7 us)
Sparse Core Ops, SparseCore 0:
  34.1 27.6 all-gather.9
  64.6 32.0 reduce-scatter.9
  111.3 32.1 all-gather.11
  146.1 55.8 reduce-scatter.7
  205.2 32.6 all-gather.13
  244.0 31.5 reduce-scatter.13
  295.0 31.5 reduce-scatter.11
  332.3 32.5 all-gather.17
  367.0 33.1 all-gather.15
  403.0 55.8 reduce-scatter.15
  461.7 31.7 reduce-scatter.17
  495.0 56.8 all-gather.19
  554.0 57.7 all-gather.21
  630.6 32.7 all-gather.23
  685.1 31.8 reduce-scatter.19
  721.3 56.8 all-gather.25

commit v3 on v0

v3 whole, which is shorter than its diff:
```python
import functools

import jax
import jax.numpy as jnp
from jax import lax
from jax.experimental import pallas as pl
from jax.experimental.pallas import tpu as pltpu
from jax.sharding import PartitionSpec as P

EPS = 1e-6
F32, BF16 = jnp.float32, jnp.bfloat16
STEP = 2
VMEM = 60 * 1024 * 1024


def dot(lhs, rhs, lhs_dim, rhs_dim):
    return lax.dot_general(lhs, rhs, (((lhs_dim,), (rhs_dim,)), ((), ())), preferred_element_type=F32)


def later(value, *others):
    return lax.optimization_barrier((value,) + others)[0]


def rms_scale(state):
    return lax.rsqrt(jnp.mean(state * state, axis=-1, keepdims=True) + EPS)


def rms_bf(state):
    return (state * rms_scale(state)).astype(BF16)


def rms_pull(state, cot):
    scale = rms_scale(state)
    normed = state * scale
    return scale * (cot - normed * jnp.mean(normed * cot, axis=-1, keepdims=True))


class Plan:
    def __init__(self, gate, n_seq):
        self.gate = gate
        self.n_seq = n_seq

    def after(self, *values):
        return Plan(later(self.gate, *values), self.n_seq)

    @staticmethod
    def seqs(array, slot=None):
        rows, cols = array.shape[-2:]
        if array.ndim == 4:
            return pl.BlockSpec((STEP, None, rows, cols), lambda g, gate: (g, slot, 0, 0))
        return pl.BlockSpec((STEP, rows, cols), lambda g, gate: (g, 0, 0))

    @staticmethod
    def layer(index, rows, cols):
        return pl.BlockSpec((None, rows, cols), lambda g, gate: (index, 0, 0))

    def call(self, body, name, in_specs, out_specs, out_shape, args, flops, aliases=None):
        n_bytes = sum(x.size * x.dtype.itemsize for x in out_shape)
        return pl.pallas_call(
            body,
            name=name,
            grid_spec=pltpu.PrefetchScalarGridSpec(
                num_scalar_prefetch=1, grid=(self.n_seq // STEP,), in_specs=in_specs, out_specs=out_specs
            ),
            out_shape=out_shape,
            input_output_aliases=aliases or {},
            cost_estimate=pl.CostEstimate(flops=int(flops), bytes_accessed=int(n_bytes), transcendentals=0),
            compiler_params=pltpu.CompilerParams(dimension_semantics=("arbitrary",), vmem_limit_bytes=VMEM),
        )(self.gate, *args)


def flat(ref):
    return ref[...].reshape(-1, ref.shape[-1])


def put(ref, value):
    ref[...] = value.astype(ref.dtype).reshape(ref.shape)


def accumulate(pairs):
    @pl.when(pl.program_id(0) == 0)
    def _():
        for ref, value in pairs:
            ref[...] = value

    @pl.when(pl.program_id(0) > 0)
    def _():
        for ref, value in pairs:
            ref[...] += value


def gelu_parts(hidden):
    root = (2.0 / jnp.pi) ** 0.5
    square = hidden * hidden
    bent = jnp.tanh(root * (hidden + 0.044715 * (square * hidden)))
    cdf = 0.5 * (1.0 + bent)
    return hidden * cdf, bent, cdf, root, square


def mlp_forward(plan, state, w_in, w_out, layer):
    n_seq, rows, width = state.shape
    ff = w_in.shape[-1]

    def body(gate, x_ref, win_ref, wout_ref, out_ref):
        act = gelu_parts(dot(rms_bf(flat(x_ref)), win_ref[...], 1, 0))[0].astype(BF16)
        put(out_ref, dot(act, wout_ref[...], 1, 0))

    return plan.call(
        body,
        "mlp_forward",
        [plan.seqs(state), plan.layer(layer, width, ff), plan.layer(layer, ff, width)],
        [plan.seqs(state)],
        [jax.ShapeDtypeStruct(state.shape, F32)],
        (state, w_in, w_out),
        4 * n_seq * rows * width * ff,
    )[0]


def mlp_back(plan, state, d_out, slot, w_in, w_out, layer, extra=None):
    n_seq, rows, width = state.shape
    ff = w_in.shape[-1]
    n_e = 0 if extra is None else 1

    def body(gate, x_ref, d_ref, win_ref, wout_ref, *refs):
        dx_ref, a_ref, act_ref, dh_ref = refs[n_e:]
        normed = rms_bf(flat(x_ref))
        hidden = dot(normed, win_ref[...], 1, 0)
        d_act = dot(flat(d_ref).astype(BF16), wout_ref[...], 1, 1)
        act, bent, cdf, root, square = gelu_parts(hidden)
        slope = cdf + 0.5 * hidden * (1.0 - bent * bent) * (root * (1.0 + 3.0 * 0.044715 * square))
        d_hidden = (slope * d_act).astype(BF16)
        d_x = dot(d_hidden, win_ref[...], 1, 1)
        if n_e:
            d_x = d_x + flat(refs[0]).astype(F32)
        put(dx_ref, d_x)
        put(a_ref, normed)
        put(act_ref, act)
        put(dh_ref, d_hidden)

    in_specs = [plan.seqs(state), plan.seqs(d_out, slot), plan.layer(layer, width, ff), plan.layer(layer, ff, width)]
    args = [state, d_out, w_in, w_out]
    if n_e:
        in_specs.append(plan.seqs(extra))
        args.append(extra)
    wide = jax.ShapeDtypeStruct((n_seq, rows, width), BF16)
    narrow = jax.ShapeDtypeStruct((n_seq, rows, ff), BF16)
    out_shape = [wide, wide, narrow, narrow]
    outs = plan.call(
        body, "mlp_back", in_specs, [plan.seqs(x) for x in out_shape], out_shape, args, 6 * n_seq * rows * width * ff
    )
    return outs[0], tuple(outs[1:])


def mlp_grads(plan, parts, d_out, slot, layer, n_layers, held):
    normed, act, d_hidden = parts
    n_seq, rows, width = normed.shape
    ff = act.shape[-1]
    n_held = 0 if held is None else 2

    def body(gate, a_ref, act_ref, dh_ref, d_ref, *refs):
        dwin_ref, dwout_ref = refs[n_held:]
        d_win = dot(flat(a_ref), flat(dh_ref), 0, 0)
        d_wout = dot(flat(act_ref), flat(d_ref).astype(BF16), 0, 0)
        accumulate([(dwin_ref, d_win), (dwout_ref, d_wout)])

    in_specs = [plan.seqs(normed), plan.seqs(act), plan.seqs(d_hidden), plan.seqs(d_out, slot)]
    args = [normed, act, d_hidden, d_out]
    aliases = {}
    if n_held:
        aliases = {len(args) + 1 + i: i for i in range(n_held)}
        in_specs += [pl.BlockSpec(memory_space=pl.ANY)] * n_held
        args += list(held)
    return plan.call(
        body,
        "mlp_grads",
        in_specs,
        [plan.layer(layer, width, ff), plan.layer(layer, ff, width)],
        [jax.ShapeDtypeStruct((n_layers, width, ff), F32), jax.ShapeDtypeStruct((n_layers, ff, width), F32)],
        args,
        4 * n_seq * rows * width * ff,
        aliases,
    )


def softmax(scores):
    powers = jnp.exp(scores - jnp.max(scores, axis=-1, keepdims=True))
    return powers / jnp.sum(powers, axis=-1, keepdims=True)


def cut(value, row, size, col, rows):
    return value[row * size :][:size][:, col * rows :][:, :rows].astype(BF16)


def attn_forward(plan, state, w_t, layer, n_heads):
    n_seq, rows, width = state.shape
    depth = w_t.shape[1]
    size = depth // 3 // n_heads

    def body(gate, x_ref, w_ref, out_ref, state_ref):
        state_ref[...] = x_ref[...]
        qkv = dot(w_ref[...], rms_bf(flat(x_ref)), 1, 1)
        cols = []
        for col in range(STEP):
            outs = []
            for head in range(n_heads):
                q, k, v = (cut(qkv, kind * n_heads + head, size, col, rows) for kind in range(3))
                probs = softmax(dot(q, k, 0, 0) * size ** -0.5).astype(BF16)
                outs.append(dot(v, probs, 1, 1))
            cols.append(jnp.concatenate(outs, axis=0))
        out_ref[...] = jnp.concatenate(cols, axis=1).astype(BF16)

    return plan.call(
        body,
        "attn_forward",
        [plan.seqs(state), plan.layer(layer, depth, width)],
        [pl.BlockSpec((depth // 3, STEP * rows), lambda g, gate: (0, g)), plan.seqs(state)],
        [jax.ShapeDtypeStruct((depth // 3, n_seq * rows), BF16), jax.ShapeDtypeStruct(state.shape, F32)],
        (state, w_t),
        2 * n_seq * rows * width * depth,
    )


def attn_back(plan, state, d_out, w_t, w_o, layer, n_heads, n_layers, held, keep_d=False):
    n_seq, rows, width = state.shape
    depth = w_t.shape[1]
    size = depth // 3 // n_heads
    n_held = 0 if held is None else 2

    def body(gate, x_ref, d_ref, w_ref, wo_ref, *refs):
        dx_ref, dw_ref, dwo_ref = refs[n_held:][:3]
        normed = flat(x_ref) if x_ref.dtype == BF16 else rms_bf(flat(x_ref))
        d_bf = flat(d_ref).astype(BF16)
        if keep_d:
            refs[-1][...] = d_ref[...]
        qkv = dot(w_ref[...], normed, 1, 1)
        d_heads = dot(wo_ref[...], d_bf, 1, 1)
        out_cols, d_cols = [], []
        for col in range(STEP):
            outs, d_parts = [], [[], [], []]
            for head in range(n_heads):
                q, k, v = (cut(qkv, kind * n_heads + head, size, col, rows) for kind in range(3))
                d_head = cut(d_heads, head, size, col, rows)
                probs = softmax(dot(q, k, 0, 0) * size ** -0.5)
                probs_bf = probs.astype(BF16)
                outs.append(dot(v, probs_bf, 1, 1))
                d_probs = dot(d_head, v, 0, 0)
                d_scores = probs * (d_probs - jnp.sum(d_probs * probs, axis=-1, keepdims=True)) * size ** -0.5
                d_scores = d_scores.astype(BF16)
                d_parts[0].append(dot(k, d_scores, 1, 1))
                d_parts[1].append(dot(q, d_scores, 1, 0))
                d_parts[2].append(dot(d_head, probs_bf, 1, 0))
            out_cols.append(jnp.concatenate(outs, axis=0))
            d_cols.append(jnp.concatenate(d_parts[0] + d_parts[1] + d_parts[2], axis=0))
        d_qkv = jnp.concatenate(d_cols, axis=1).astype(BF16)
        put(dx_ref, dot(d_qkv, w_ref[...], 0, 0))
        heads = jnp.concatenate(out_cols, axis=1).astype(BF16)
        accumulate([(dw_ref, dot(d_qkv, normed, 1, 0)), (dwo_ref, dot(heads, d_bf, 1, 0))])

    in_specs = [plan.seqs(state), plan.seqs(d_out), plan.layer(layer, depth, width), plan.layer(layer, depth // 3, width)]
    args = [state, d_out, w_t, w_o]
    aliases = {}
    if n_held:
        aliases = {len(args) + 1 + i: 1 + i for i in range(n_held)}
        in_specs += [pl.BlockSpec(memory_space=pl.ANY)] * n_held
        args += list(held)
    out_specs = [plan.seqs(state), plan.layer(layer, depth, width), plan.layer(layer, depth // 3, width)]
    out_shape = [
        jax.ShapeDtypeStruct(state.shape, BF16),
        jax.ShapeDtypeStruct((n_layers, depth, width), F32),
        jax.ShapeDtypeStruct((n_layers, depth // 3, width), F32),
    ]
    if keep_d:
        out_specs.append(plan.seqs(d_out))
        out_shape.append(jax.ShapeDtypeStruct(d_out.shape, d_out.dtype))
    outs = plan.call(body, "attn_back", in_specs, out_specs, out_shape, args, 8 * n_seq * rows * width * depth, aliases)
    return outs[0], tuple(outs[1:3]), (outs[3] if keep_d else None)


def project_out(plan, base, heads, w_o):
    n_seq, rows, width = base.shape
    depth = heads.shape[0]

    def body(gate, x_ref, h_ref, w_ref, out_ref):
        put(out_ref, flat(x_ref) - dot(h_ref[...], w_ref[...], 0, 0))

    return plan.call(
        body,
        "project_out",
        [
            plan.seqs(base),
            pl.BlockSpec((depth, STEP * rows), lambda g, gate: (0, g)),
            pl.BlockSpec((depth, width), lambda g, gate: (0, 0)),
        ],
        [plan.seqs(base)],
        [jax.ShapeDtypeStruct(base.shape, F32)],
        (base, heads, w_o),
        2 * n_seq * rows * width * depth,
    )[0]


def solution(mesh):
    act_spec = P("dp", None, None)
    saved_spec = P(None, "dp", None, None)
    weight_specs = (P(None, None, None, "tp", None), P(None, "tp", None, None), P(None, None, "tp"), P(None, "tp", None))
    grad_specs = (P("dp", None, None, "tp", None), P("dp", "tp", None, None), P("dp", None, "tp"), P("dp", "tp", None))

    def scatter(part):
        return lax.psum_scatter(part, "tp", scatter_dimension=0, tiled=True)

    def gather(shard, *others):
        return later(lax.all_gather(shard, "tp", axis=0, tiled=True), *others)

    def per_device(y_one, y_two, dy_one, dy_two, saved_one, saved_two, w_qkv, w_o, w_in, w_out):
        n_layers, width, _, n_heads, size = w_qkv.shape
        n_pairs = saved_one.shape[0]
        me = lax.axis_index("tp")
        plan = Plan(me.reshape(1).astype(jnp.int32), y_one.shape[0])
        w_t = jnp.transpose(w_qkv, (0, 2, 3, 4, 1)).reshape(n_layers, 3 * n_heads * size, width)
        w_o2 = w_o.reshape(n_layers, n_heads * size, width)

        def own(state):
            return lax.dynamic_slice_in_dim(state, me, 1, 0)

        top = n_layers - 1
        dx, parts = mlp_back(plan, y_one, dy_two, None, w_in, w_out, top)
        g_back = scatter(dx)
        g_part = mlp_forward(plan.after(dx), y_one, w_in, w_out, top)
        d_one = own(dy_one) + rms_pull(own(y_one), later(g_back, g_part).astype(F32))
        d_shard = d_one.astype(BF16)
        mlp_held = mlp_grads(plan.after(d_shard), parts, dy_two, None, top, n_layers, None)
        g_sum, x_two_out = scatter(later(g_part, d_shard)), own(y_two)
        d_two, attn_held, last = own(dy_two), None, mlp_held[0]

        for layer_pair in reversed(range(n_pairs)):
            s_one, s_two = saved_one[layer_pair], saved_two[layer_pair]
            mid, low = 2 * layer_pair + 1, 2 * layer_pair
            g_part = mlp_forward(plan.after(last), s_one, w_in, w_out, low)
            d_one_bf = gather(d_shard, g_part)
            mid_back, attn_held, _ = attn_back(plan, s_two, d_one_bf, w_t, w_o2, mid, n_heads, n_layers, attn_held)
            x_two_shard = x_two_out - later(g_sum, mid_back)
            f_shard = rms_bf(x_two_shard)
            f_in = gather(f_shard)
            mid_sum = scatter(later(mid_back, f_shard))
            f_back, attn_held, _ = attn_back(plan, f_in, d_one_bf, w_t, w_o2, mid + 1, n_heads, n_layers, attn_held)
            g_sum, x_two_out = scatter(later(g_part, f_shard)), own(s_two)
            mid_two = d_two + rms_pull(x_two_shard, scatter(f_back).astype(F32))
            d_two = mid_two + rms_pull(own(s_two), later(mid_sum, f_back).astype(F32))
            both_d = gather(jnp.stack([mid_two.astype(BF16), d_two.astype(BF16)], axis=1))
            dx, mid_parts = mlp_back(plan, s_one, both_d, 0, w_in, w_out, mid)
            dx, low_parts = mlp_back(plan, s_one, both_d, 1, w_in, w_out, low, dx)
            x_two_shard = x_two_out - later(g_sum, dx)
            d_one = d_one + rms_pull(own(s_one), scatter(dx).astype(F32))
            heads, x_two = attn_forward(plan, gather(x_two_shard, d_one), w_t, low, n_heads)
            if layer_pair:
                d_shard, last = d_one.astype(BF16), dx
                g_sum, x_two_out = jnp.zeros_like(x_two_shard), x_two_shard
                mlp_held = mlp_grads(plan, mid_parts, both_d, 0, mid, n_layers, mlp_held)
                mlp_held = mlp_grads(plan, low_parts, both_d, 1, low, n_layers, mlp_held)
        f_back, attn_held, d_one_full = attn_back(
            plan.after(heads), x_two, gather(d_one), w_t, w_o2, 0, n_heads, n_layers, attn_held, True
        )
        heads_all, wo_all = gather(heads, f_back), gather(w_o2[0], f_back)
        d_two = d_two + rms_pull(x_two_shard, scatter(later(f_back, heads_all, wo_all)).astype(F32))
        tail = plan.after(f_back)
        mlp_held = mlp_grads(tail, mid_parts, both_d, 0, 1, n_layers, mlp_held)
        mlp_held = mlp_grads(tail, low_parts, both_d, 1, 0, n_layers, mlp_held)
        x_one = project_out(tail, s_one, heads_all, wo_all)
        d_two_full = gather(d_two, x_one, mlp_held[0])
        d_w = jnp.transpose(attn_held[0].reshape(n_layers, 3, n_heads, size, width), (0, 4, 1, 2, 3))
        d_wo = attn_held[1].reshape(n_layers, n_heads, size, width)
        return (x_one, x_two, d_one_full, d_two_full, d_w, d_wo) + tuple(mlp_held)

    return jax.shard_map(
        per_device,
        mesh=mesh,
        in_specs=(act_spec,) * 4 + (saved_spec,) * 2 + weight_specs,
        out_specs=(act_spec,) * 4 + grad_specs,
        check_vma=False,
    )
```

time: 1450 us -> 773 us (0.53)
  waiting for transfers between devices: 873 us -> 419 us
  matrix products: 340 us -> 0 us
  Pallas kernels: 0 us -> 287 us
  other arithmetic: 189 us -> 33.1 us
  local copies, waits for them, and re-layouts: 27.9 us -> 11.4 us
    psum x4 -> x0, waiting for transfers between devices: 873 us -> none  [the longest x1 305 us: reversible_block(): x_two = y_two - lax.psum(g_part, 'tp')]
    dot_general x49 -> x0, matrix products: 340 us -> none  [the longest x3 37.3 us: mlp_backward(): jnp.einsum('bsh,fh->bsf', d_bf, w_out, preferred_element_type=jnp.float32)]
    pallas_call x0 -> x13, Pallas kernels: none -> 287 us  [call(): pl.pallas_call(body, name=name, grid_spec=pltpu.PrefetchScalarGridSpec(nu...]
    all_gather x0 -> x8, waiting for transfers between devices: none -> 229 us  [gather(): return later(lax.all_gather(shard, 'tp', axis=0, tiled=True), *others)]
    reduce_scatter x0 -> x7, waiting for transfers between devices: none -> 187 us  [scatter(): return lax.psum_scatter(part, 'tp', scatter_dimension=0, tiled=True)]
    reduce_sum x9 -> x10, other arithmetic: 80 us -> 18.6 us  [the longest x5 9.73 us: rms_scale(): return lax.rsqrt(jnp.mean(state * state, axis=-1, keepdims=True) + EPS)]
    add x3 -> x2, other arithmetic: 47.8 us -> 5.47 us  [the longest x1 3.99 us: per_device(): d_one = d_one + rms_pull(own(s_one), scatter(dx).astype(F32))]
    sub x4 -> x0, other arithmetic: 22.9 us -> none  [the longest x1 12.9 us: reversible_block(): x_one = y_one - lax.psum(f_part, 'tp')]
  transfers between devices with their start and end apart: 4 -> 15, of which waited for: 4 -> 13; matrix products, arithmetic and copies ran while one was open for 11% -> 2% of each run, Pallas kernels for 0% -> 35%
where the time goes in v3:
time: 773 us; the launch traced here: 767 us
  waiting for transfers between devices  419 us (54%)
  Pallas kernels  287 us (37%)
  other arithmetic  33.1 us (4%)
  between operations  14.6 us (2%)
  local copies, waits for them, and re-layouts  11.4 us (1%)
    pallas_call x13, Pallas kernels, call(): pl.pallas_call(body, name=name, grid_spec=pltpu.PrefetchScalarGridSpec(nu...  287 us
    all_gather x8, waiting for transfers between devices, gather(): return later(lax.all_gather(shard, 'tp', axis=0, tiled=True), *others)  229 us
    reduce_scatter x7, waiting for transfers between devices, scatter(): return lax.psum_scatter(part, 'tp', scatter_dimension=0, tiled=True)  187 us
  transfers between devices with their start and end apart: 15, of which 13 were waited for; matrix products, arithmetic and copies ran while one was open for 2% of the time, Pallas kernels for 35%

profile of v3, /device:TPU:113, one launch (start us, length us, event | category | flops | bytes accessed | tf_op | source)
XLA Modules:
  0.0 766.5 jit_solution(1902305196792787018)
XLA Ops:
  7.3 21.2 %mlp_back.3 = (bf16[8,256,1408]{2,1,0:T(8,128)(2,1)}, bf16[8,256,1408]{2,1,0:T(8,128)(2,1)}, bf16[8,256,768]{2,1,0:T(8,128)(2,1)}, bf16[8,256,768]{2,1,0:T(8,128)(2,1)}) custom-call(s32[1]{0:T(128)} %bitcast.gate, f32[8,256,1408]{2,1,0:T(8,128)} %x_ref.3, f32[8,256,1408]{2,1,0:T(8,128)} %d_ref.3, bf16[3,1408,768]{2,1,0:T(8,128)(2,1)} %win_ref.9, ...), custom_call_target="tpu_custom_call" | custom-call | flops 13287555072 | bytes 17825792 | tf_op jit(solution)/shard_map/mlp_back/pallas_call | solution.py:59
  30.1 18.2 %mlp_forward.2 = f32[8,256,1408]{2,1,0:T(8,128)} custom-call(s32[1]{0:T(128)} %bitcast.gate, f32[8,256,1408]{2,1,0:T(8,128)} %x_ref.3, bf16[3,1408,768]{2,1,0:T(8,128)(2,1)} %win_ref.9, bf16[3,768,1408]{2,1,0:T(8,128)(2,1)} %wout_ref.9), custom_call_target="tpu_custom_call" | custom-call | flops 8858370048 | bytes 11534336 | tf_op jit(solution)/shard_map/mlp_forward/pallas_call | solution.py:59
  48.4 18.7 %reduce-scatter.8.cloned.1.call-done = bf16[1,256,1408]{2,1,0:T(8,128)(2,1)} async-done(((bf16[8,256,1408]{2,1,0:T(8,128)(2,1)}), bf16[1,256,1408]{2,1,0:T(8,128)(2,1)}) %reduce-scatter.8.cloned.1.call-update) | async-done | bytes 720912 | tf_op jit(solution)/shard_map/reduce_scatter | solution.py:308
  69.1 3.0 fusion.17
  73.5 19.6 %mlp_grads.3 = (f32[3,1408,768]{2,1,0:T(8,128)}, f32[3,768,1408]{2,1,0:T(8,128)}) custom-call(s32[1]{0:T(128)} %bitcast.gate, bf16[8,256,1408]{2,1,0:T(8,128)(2,1)} %get-tuple-element.60.a_ref, bf16[8,256,768]{2,1,0:T(8,128)(2,1)} %get-tuple-element.61.act_ref, bf16[8,256,768]{2,1,0:T(8,128)(2,1)} %get-tuple-element.62.dh_ref, f32[8,256,1408]{2,1,0:T(8,128)} %d_ref.3), custom_call_target="tpu_custom_call" | custom-call | flops 8858370048 | bytes 25952256 | tf_op jit(solution)/shard_map/mlp_grads/pallas_call | solution.py:59
  93.2 18.2 %mlp_forward.3 = f32[8,256,1408]{2,1,0:T(8,128)} custom-call(s32[1]{0:T(128)} %bitcast.gate, f32[8,256,1408]{2,1,0:T(8,128)} %bitcast.37, bf16[3,1408,768]{2,1,0:T(8,128)(2,1)} %win_ref.9, bf16[3,768,1408]{2,1,0:T(8,128)(2,1)} %wout_ref.9), custom_call_target="tpu_custom_call" | custom-call | flops 8858370048 | bytes 11534336 | tf_op jit(solution)/shard_map/mlp_forward/pallas_call | solution.py:59
  111.4 31.8 %attn_back.3 = (bf16[8,256,1408]{2,1,0:T(8,128)(2,1)}, f32[3,528,1408]{2,1,0:T(8,128)}, f32[3,176,1408]{2,1,0:T(8,128)}) custom-call(s32[1]{0:T(128)} %bitcast.gate, f32[8,256,1408]{2,1,0:T(8,128)} %bitcast.45, bf16[8,256,1408]{2,1,0:T(8,128)(2,1)} %all-gather.9.cloned.1.call-done.d_ref, bf16[3,528,1408]{2,1,0:T(8,128)(2,1)} %bitcast.41, ...), custom_call_target="tpu_custom_call" | custom-call | flops 12180258816 | bytes 17661952 | tf_op jit(solution)/shard_map/attn_back/pallas_call | solution.py:59
  143.2 30.5 %reduce-scatter.10.cloned.1.call-done = f32[1,256,1408]{2,1,0:T(8,128)} async-done(((f32[8,256,1408]{2,1,0:T(8,128)}), f32[1,256,1408]{2,1,0:T(8,128)}) %reduce-scatter.10.cloned.1.call-update) | async-done | bytes 1441808 | tf_op jit(solution)/shard_map/reduce_scatter | solution.py:308
  173.7 2.0 multiply_reduce_fusion.1
  177.6 34.2 %all-gather.11.cloned.1.call-done.x_ref = bf16[8,256,1408]{2,1,0:T(8,128)(2,1)} async-done(((bf16[1,256,1408]{2,1,0:T(8,128)(2,1)}), bf16[8,256,1408]{2,1,0:T(8,128)(2,1)}) %all-gather.11.cloned.1.call-update) | async-done | bytes 5767184 | tf_op jit(solution)/shard_map/all_gather | solution.py:311
  211.8 30.8 %attn_back.4 = (bf16[8,256,1408]{2,1,0:T(8,128)(2,1)}, f32[3,528,1408]{2,1,0:T(8,128)}, f32[3,176,1408]{2,1,0:T(8,128)}) custom-call(s32[1]{0:T(128)} %bitcast.gate, bf16[8,256,1408]{2,1,0:T(8,128)(2,1)} %all-gather.11.cloned.1.call-done.x_ref, ...), custom_call_target="tpu_custom_call", output_to_operand_aliasing={{1}: (5, {}), {2}: (6, {})} | custom-call | flops 12180258816 | bytes 17661952 | tf_op jit(solution)/shard_map/attn_back/pallas_call | solution.py:59
  244.3 5.5 reduce-scatter.16.cloned.1.call-done
  251.7 37.4 %reduce-scatter.14.cloned.1.call-done = bf16[1,256,1408]{2,1,0:T(8,128)(2,1)} async-done(((bf16[8,256,1408]{2,1,0:T(8,128)(2,1)}), bf16[1,256,1408]{2,1,0:T(8,128)(2,1)}) %reduce-scatter.14.cloned.1.call-update) | async-done | bytes 720912 | tf_op jit(solution)/shard_map/reduce_scatter | solution.py:308
  290.7 3.6 convert_bitcast_fusion
  296.5 59.5 %all-gather.13.cloned.1.call-done.d_ref = bf16[8,2,256,1408]{3,2,1,0:T(8,128)(2,1)} async-done(((bf16[1,2,256,1408]{3,2,1,0:T(8,128)(2,1)}), bf16[8,2,256,1408]{3,2,1,0:T(8,128)(2,1)}) %all-gather.13.cloned.1.call-update) | async-done | bytes 11534352 | tf_op jit(solution)/shard_map/all_gather | solution.py:311
  356.0 20.9 %mlp_back.4 = (bf16[8,256,1408]{2,1,0:T(8,128)(2,1)}, bf16[8,256,1408]{2,1,0:T(8,128)(2,1)}, bf16[8,256,768]{2,1,0:T(8,128)(2,1)}, bf16[8,256,768]{2,1,0:T(8,128)(2,1)}) custom-call(s32[1]{0:T(128)} %bitcast.gate, f32[8,256,1408]{2,1,0:T(8,128)} %bitcast.38, bf16[8,2,256,1408]{3,2,1,0:T(8,128)(2,1)} %all-gather.13.cloned.1.call-done.d_ref, ...), custom_call_target="tpu_custom_call" | custom-call | flops 13287555072 | bytes 17825792 | tf_op jit(solution)/shard_map/mlp_back/pallas_call | solution.py:59
  377.0 21.2 %mlp_back.5 = (bf16[8,256,1408]{2,1,0:T(8,128)(2,1)}, bf16[8,256,1408]{2,1,0:T(8,128)(2,1)}, bf16[8,256,768]{2,1,0:T(8,128)(2,1)}, bf16[8,256,768]{2,1,0:T(8,128)(2,1)}) custom-call(s32[1]{0:T(128)} %bitcast.gate, f32[8,256,1408]{2,1,0:T(8,128)} %bitcast.39, bf16[8,2,256,1408]{3,2,1,0:T(8,128)(2,1)} %all-gather.13.cloned.1.call-done.d_ref, ...), custom_call_target="tpu_custom_call" | custom-call | flops 13287555072 | bytes 17825792 | tf_op jit(solution)/shard_map/mlp_back/pallas_call | solution.py:59
  398.3 23.5 %reduce-scatter.12.cloned.1.call-done = f32[1,256,1408]{2,1,0:T(8,128)} async-done(((f32[8,256,1408]{2,1,0:T(8,128)}), f32[1,256,1408]{2,1,0:T(8,128)}) %reduce-scatter.12.cloned.1.call-update) | async-done | bytes 1441808 | tf_op jit(solution)/shard_map/reduce_scatter | solution.py:308
  421.8 3.1 multiply_reduce_fusion
  426.6 33.8 %reduce-scatter.18.cloned.1.call-done = bf16[1,256,1408]{2,1,0:T(8,128)(2,1)} async-done(((bf16[8,256,1408]{2,1,0:T(8,128)(2,1)}), bf16[1,256,1408]{2,1,0:T(8,128)(2,1)}) %reduce-scatter.18.cloned.1.call-update) | async-done | bytes 720912 | tf_op jit(solution)/shard_map/reduce_scatter | solution.py:308
  462.4 4.0 fusion.11
  468.5 53.6 %all-gather.15.cloned.1.call-done.x_ref = f32[8,256,1408]{2,1,0:T(8,128)} async-done(((f32[1,256,1408]{2,1,0:T(8,128)}), f32[8,256,1408]{2,1,0:T(8,128)}) %all-gather.15.cloned.1.call-update) | async-done | bytes 11534352 | tf_op jit(solution)/shard_map/all_gather | solution.py:311
  522.1 15.6 %attn_forward.1 = (bf16[176,2048]{1,0:T(8,128)(2,1)}, f32[8,256,1408]{2,1,0:T(8,128)}) custom-call(s32[1]{0:T(128)} %bitcast.gate, f32[8,256,1408]{2,1,0:T(8,128)} %all-gather.15.cloned.1.call-done.x_ref, bf16[3,528,1408]{2,1,0:T(8,128)(2,1)} %bitcast.43), custom_call_target="tpu_custom_call" | custom-call | flops 3045064704 | bytes 12255232 | tf_op jit(solution)/shard_map/attn_forward/pallas_call | solution.py:59
  537.8 45.6 %all-gather.17.cloned.1.call-done.d_ref = f32[8,256,1408]{2,1,0:T(8,128)} async-done(((f32[1,256,1408]{2,1,0:T(8,128)}), f32[8,256,1408]{2,1,0:T(8,128)}) %all-gather.17.cloned.1.call-update) | async-done | bytes 11534352 | tf_op jit(solution)/shard_map/all_gather | solution.py:311
  583.4 33.2 %attn_back.5 = (bf16[8,256,1408]{2,1,0:T(8,128)(2,1)}, f32[3,528,1408]{2,1,0:T(8,128)}, f32[3,176,1408]{2,1,0:T(8,128)}, f32[8,256,1408]{2,1,0:T(8,128)}) custom-call(s32[1]{0:T(128)} %bitcast.gate, f32[8,256,1408]{2,1,0:T(8,128)} %get-tuple-element.120.x_ref, ...), custom_call_target="tpu_custom_call", output_to_operand_aliasing={{1}: (5, {}), {2}: (6, {})} | custom-call | flops 12180258816 | bytes 29196288 | tf_op jit(solution)/shard_map/attn_back/pallas_call | solution.py:59
  616.7 31.7 %all-gather.19.cloned.1.call-done.h_ref = bf16[1408,2048]{1,0:T(8,128)(2,1)} async-done(((bf16[176,2048]{1,0:T(8,128)(2,1)}), bf16[1408,2048]{1,0:T(8,128)(2,1)}) %all-gather.19.cloned.1.call-update) | async-done | bytes 5767184 | tf_op jit(solution)/shard_map/all_gather | solution.py:311
  648.6 37.8 %reduce-scatter.20.cloned.1.call-done = bf16[1,256,1408]{2,1,0:T(8,128)(2,1)} async-done(((bf16[8,256,1408]{2,1,0:T(8,128)(2,1)}), bf16[1,256,1408]{2,1,0:T(8,128)(2,1)}) %reduce-scatter.20.cloned.1.call-update) | async-done | bytes 720912 | tf_op jit(solution)/shard_map/reduce_scatter | solution.py:308
  689.5 17.4 %project_out.1 = f32[8,256,1408]{2,1,0:T(8,128)} custom-call(s32[1]{0:T(128)} %bitcast.gate, f32[8,256,1408]{2,1,0:T(8,128)} %bitcast.40, bf16[1408,2048]{1,0:T(8,128)(2,1)} %all-gather.19.cloned.1.call-done.h_ref, bf16[1408,1408]{1,0:T(8,128)(2,1)} %all-gather.21.cloned.1.call-done.w_ref), custom_call_target="tpu_custom_call" | custom-call | flops 8120172544 | bytes 11534336 | tf_op jit(solution)/shard_map/project_out/pallas_call | solution.py:59
  706.9 19.1 %mlp_grads.4 = (f32[3,1408,768]{2,1,0:T(8,128)}, f32[3,768,1408]{2,1,0:T(8,128)}) custom-call(s32[1]{0:T(128)} %bitcast.gate, bf16[8,256,1408]{2,1,0:T(8,128)(2,1)} %get-tuple-element.93.a_ref, bf16[8,256,768]{2,1,0:T(8,128)(2,1)} %get-tuple-element.94.act_ref, ...), custom_call_target="tpu_custom_call", output_to_operand_aliasing={{0}: (5, {}), {1}: (6, {})} | custom-call | flops 8858370048 | bytes 25952256 | tf_op jit(solution)/shard_map/mlp_grads/pallas_call | solution.py:59
  726.1 19.2 %mlp_grads.5 = (f32[3,1408,768]{2,1,0:T(8,128)}, f32[3,768,1408]{2,1,0:T(8,128)}) custom-call(s32[1]{0:T(128)} %bitcast.gate, bf16[8,256,1408]{2,1,0:T(8,128)(2,1)} %get-tuple-element.90.a_ref, bf16[8,256,768]{2,1,0:T(8,128)(2,1)} %get-tuple-element.91.act_ref, ...), custom_call_target="tpu_custom_call", output_to_operand_aliasing={{0}: (5, {}), {1}: (6, {})} | custom-call | flops 8858370048 | bytes 25952256 | tf_op jit(solution)/shard_map/mlp_grads/pallas_call | solution.py:59
  745.2 4.7 all-gather.23.cloned.1.call-done
  749.9 9.5 %copy.35 = f32[8,256,1408]{2,1,0:T(8,128)} copy(f32[8,256,1408]{2,1,0:T(8,128)} %all-gather.23.cloned.1.call-done) | data formatting | bytes 23068672
  (68 shorter events, 23.3 us)
Async XLA Ops:
  7.2 59.9 %reduce-scatter.8.cloned.1.call-start = ((), (), s32[]{:S(2)}) async-start(), calls=%async_computation.7 | async-start | bytes 6488064 | tf_op jit(solution)/shard_map/reduce_scatter | solution.py:308
  28.5 82.9 %all-gather.9.cloned.1.call-start = ((), (), s32[]{:S(2)}) async-start(), calls=%async_computation.9 | async-start | bytes 6488064 | tf_op jit(solution)/shard_map/all_gather | solution.py:311
  67.1 2.0 copy-start.1
  72.2 101.5 %reduce-scatter.10.cloned.1.call-start = ((), (), s32[]{:S(2)}) async-start(), calls=%async_computation.8 | async-start | bytes 12976128 | tf_op jit(solution)/shard_map/reduce_scatter | solution.py:308
  73.0 138.8 %all-gather.11.cloned.1.call-start = ((), (), s32[]{:S(2)}) async-start(), calls=%async_computation.11 | async-start | bytes 6488064 | tf_op jit(solution)/shard_map/all_gather | solution.py:311
  176.8 72.9 %reduce-scatter.16.cloned.1.call-start = ((), (), s32[]{:S(2)}) async-start(), calls=%async_computation.13 | async-start | bytes 6488064 | tf_op jit(solution)/shard_map/reduce_scatter | solution.py:308
  177.5 111.6 %reduce-scatter.14.cloned.1.call-start = ((), (), s32[]{:S(2)}) async-start(), calls=%async_computation.12 | async-start | bytes 6488064 | tf_op jit(solution)/shard_map/reduce_scatter | solution.py:308
  242.7 113.4 %all-gather.13.cloned.1.call-start = ((), (), s32[]{:S(2)}) async-start(), calls=%async_computation.14 | async-start | bytes 12976128 | tf_op jit(solution)/shard_map/all_gather | solution.py:311
  251.7 39.0 %copy-start.6 = (bf16[1,256,1408]{2,1,0:T(8,128)(2,1)S(1)}, bf16[1,256,1408]{2,1,0:T(8,128)(2,1)}, u32[]{:S(2)}) copy-start(bf16[1,256,1408]{2,1,0:T(8,128)(2,1)} %reduce-scatter.16.cloned.1.call-done) | copy-start | bytes 2162692
  289.1 1.5 copy-start.5
  295.6 126.2 %reduce-scatter.12.cloned.1.call-start = ((), (), s32[]{:S(2)}) async-start(), calls=%async_computation.10 | async-start | bytes 12976128 | tf_op jit(solution)/shard_map/reduce_scatter | solution.py:308
  296.4 163.9 %reduce-scatter.18.cloned.1.call-start = ((), (), s32[]{:S(2)}) async-start(), calls=%async_computation.16 | async-start | bytes 6488064 | tf_op jit(solution)/shard_map/reduce_scatter | solution.py:308
  398.2 123.9 %all-gather.15.cloned.1.call-start = ((), (), s32[]{:S(2)}) async-start(), calls=%async_computation.15 | async-start | bytes 12976128 | tf_op jit(solution)/shard_map/all_gather | solution.py:311
  425.0 158.5 %all-gather.17.cloned.1.call-start = ((), (), s32[]{:S(2)}) async-start(), calls=%async_computation.17 | async-start | bytes 12976128 | tf_op jit(solution)/shard_map/all_gather | solution.py:311
  460.4 2.0 copy-start.4
  466.4 150.3 %all-gather.21.cloned.1.call-start = ((), (), s32[]{:S(2)}) async-start(), calls=%async_computation.19 | async-start | bytes 4460544 | tf_op jit(solution)/shard_map/all_gather | solution.py:311
  468.4 180.0 %all-gather.19.cloned.1.call-start = ((), (), s32[]{:S(2)}) async-start(), calls=%async_computation.18 | async-start | bytes 6488064 | tf_op jit(solution)/shard_map/all_gather | solution.py:311
  537.7 148.7 %reduce-scatter.20.cloned.1.call-start = ((), (), s32[]{:S(2)}) async-start(), calls=%async_computation.20 | async-start | bytes 6488064 | tf_op jit(solution)/shard_map/reduce_scatter | solution.py:308
  616.7 69.7 %copy-start = (f32[1,256,1408]{2,1,0:T(8,128)S(1)}, f32[1,256,1408]{2,1,0:T(8,128)}, u32[]{:S(2)}) copy-start(f32[1,256,1408]{2,1,0:T(8,128)} %get-tuple-element.105) | copy-start | bytes 4325380
  648.5 39.5 %copy-start.2 = (f32[1,256,1408]{2,1,0:T(8,128)S(1)}, f32[1,256,1408]{2,1,0:T(8,128)}, u32[]{:S(2)}) copy-start(f32[1,256,1408]{2,1,0:T(8,128)} %get-tuple-element.107) | copy-start | bytes 4325380
  648.5 101.4 %all-gather.23.cloned.1.call-start = ((), (), s32[]{:S(2)}) async-start(), calls=%async_computation.21 | async-start | bytes 12976128 | tf_op jit(solution)/shard_map/all_gather | solution.py:311
  686.4 1.5 copy-start.3
Sparse Core Ops, SparseCore 0:
  28.6 38.4 reduce-scatter.7
  72.3 35.7 all-gather.8
  111.0 62.6 reduce-scatter.9
  177.0 34.7 all-gather.10
  214.5 35.2 reduce-scatter.15
  252.5 36.5 reduce-scatter.13
  295.7 60.2 all-gather.12
  358.9 62.8 reduce-scatter.11
  424.7 35.6 reduce-scatter.17
  461.8 60.2 all-gather.14
  524.3 59.1 all-gather.16
  584.9 27.1 all-gather.20
  614.2 34.1 all-gather.18
  651.1 35.2 reduce-scatter.19
  689.6 60.2 all-gather.22

commit v4 on v3

--- a/solution.py
+++ b/solution.py
@@ -1,5 +1,3 @@
-import functools
-
 import jax
 import jax.numpy as jnp
 from jax import lax
@@ -7,8 +5,10 @@
 from jax.experimental.pallas import tpu as pltpu
 from jax.sharding import PartitionSpec as P
 
+
 EPS = 1e-6
 F32, BF16 = jnp.float32, jnp.bfloat16
+CORES = 2
 STEP = 2
 VMEM = 60 * 1024 * 1024
 
@@ -54,11 +54,10 @@
     def layer(index, rows, cols):
         return pl.BlockSpec((None, rows, cols), lambda g, gate: (index, 0, 0))
 
-    def call(self, body, name, in_specs, out_specs, out_shape, args, flops, aliases=None):
+    def call(self, body, in_specs, out_specs, out_shape, args, flops, aliases=None):
         n_bytes = sum(x.size * x.dtype.itemsize for x in out_shape)
         return pl.pallas_call(
             body,
-            name=name,
             grid_spec=pltpu.PrefetchScalarGridSpec(
                 num_scalar_prefetch=1, grid=(self.n_seq // STEP,), in_specs=in_specs, out_specs=out_specs
             ),
@@ -107,7 +106,6 @@
 
     return plan.call(
         body,
-        "mlp_forward",
         [plan.seqs(state), plan.layer(layer, width, ff), plan.layer(layer, ff, width)],
         [plan.seqs(state)],
         [jax.ShapeDtypeStruct(state.shape, F32)],
@@ -145,9 +143,7 @@
     wide = jax.ShapeDtypeStruct((n_seq, rows, width), BF16)
     narrow = jax.ShapeDtypeStruct((n_seq, rows, ff), BF16)
     out_shape = [wide, wide, narrow, narrow]
-    outs = plan.call(
-        body, "mlp_back", in_specs, [plan.seqs(x) for x in out_shape], out_shape, args, 6 * n_seq * rows * width * ff
-    )
+    outs = plan.call(body, in_specs, [plan.seqs(x) for x in out_shape], out_shape, args, 6 * n_seq * rows * width * ff)
     return outs[0], tuple(outs[1:])
 
 
@@ -172,7 +168,6 @@
         args += list(held)
     return plan.call(
         body,
-        "mlp_grads",
         in_specs,
         [plan.layer(layer, width, ff), plan.layer(layer, ff, width)],
         [jax.ShapeDtypeStruct((n_layers, width, ff), F32), jax.ShapeDtypeStruct((n_layers, ff, width), F32)],
@@ -211,7 +206,6 @@
 
     return plan.call(
         body,
-        "attn_forward",
         [plan.seqs(state), plan.layer(layer, depth, width)],
         [pl.BlockSpec((depth // 3, STEP * rows), lambda g, gate: (0, g)), plan.seqs(state)],
         [jax.ShapeDtypeStruct((depth // 3, n_seq * rows), BF16), jax.ShapeDtypeStruct(state.shape, F32)],
@@ -272,7 +266,7 @@
     if keep_d:
         out_specs.append(plan.seqs(d_out))
         out_shape.append(jax.ShapeDtypeStruct(d_out.shape, d_out.dtype))
-    outs = plan.call(body, "attn_back", in_specs, out_specs, out_shape, args, 8 * n_seq * rows * width * depth, aliases)
+    outs = plan.call(body, in_specs, out_specs, out_shape, args, 8 * n_seq * rows * width * depth, aliases)
     return outs[0], tuple(outs[1:3]), (outs[3] if keep_d else None)
 
 
@@ -285,7 +279,6 @@
 
     return plan.call(
         body,
-        "project_out",
         [
             plan.seqs(base),
             pl.BlockSpec((depth, STEP * rows), lambda g, gate: (0, g)),
@@ -310,6 +303,53 @@
     def gather(shard, *others):
         return later(lax.all_gather(shard, "tp", axis=0, tiled=True), *others)
 
+    n_tp = mesh.shape["tp"]
+    chips = n_tp // CORES
+
+    def shift(value, hops):
+        pairs = [(i, (i // CORES + hops) % chips * CORES + i % CORES) for i in range(n_tp)]
+        return lax.ppermute(value, "tp", pairs)
+
+    def swap(value):
+        return lax.ppermute(value, "tp", [(i, i + 1 - 2 * (i % CORES)) for i in range(n_tp)])
+
+    def ring_scatter(part):
+        chip, core = lax.div(lax.axis_index("tp"), CORES), lax.rem(lax.axis_index("tp"), CORES)
+        split = part.reshape((chips, CORES) + part.shape[1:])
+        half = part.shape[1] // 2
+        far = swap(lax.dynamic_index_in_dim(split, 1 - core, 1, False))
+        mine = lax.dynamic_index_in_dim(split, core, 1, False) + far
+        ahead, across, behind, here = (
+            lax.dynamic_index_in_dim(mine, lax.rem(chip + hops, chips), 0, False) for hops in (1, 2, 3, 0)
+        )
+        from_back, from_front = shift(across[:half], 1), shift(across[half:], -1)
+        back_low, front_high = shift(ahead[half:], 1), shift(behind[:half], -1)
+
+        def finish(second, third):
+            back_high = shift(ahead[:half] + later(from_back, *second), 1)
+            front_low = shift(behind[half:] + later(from_front, *second), -1)
+            high = later(back_high, *third) + front_high
+            low = later(front_low, *third) + back_low
+            return (here + jnp.concatenate([high, low], axis=0))[None]
+
+        return finish, mine
+
+    def ring_gather(shard, second, third):
+        chip, core = lax.div(lax.axis_index("tp"), CORES), lax.rem(lax.axis_index("tp"), CORES)
+        rows = shard.shape[0]
+        half = rows // 2
+        back, front = shift(shard, 1), shift(shard, -1)
+        back, front = later(back, *second), later(front, *second)
+        far_low, far_high = shift(back[:half], 1), shift(front[half:], -1)
+        across = jnp.concatenate([later(far_low, *third), later(far_high, *third)], axis=0)
+        whole = jnp.zeros((n_tp,) + shard.shape, shard.dtype)
+        for hops, piece in ((0, shard), (chips - 1, back), (1, front), (2, across)):
+            place = lax.rem(chip + hops, chips) * CORES
+            other = later(swap(piece), *third)
+            whole = lax.dynamic_update_slice_in_dim(whole, later(piece, *third)[None], place + core, 0)
+            whole = lax.dynamic_update_slice_in_dim(whole, other[None], place + 1 - core, 0)
+        return whole
+
     def per_device(y_one, y_two, dy_one, dy_two, saved_one, saved_two, w_qkv, w_o, w_in, w_out):
         n_layers, width, _, n_heads, size = w_qkv.shape
         n_pairs = saved_one.shape[0]
@@ -329,6 +369,7 @@
         d_shard = d_one.astype(BF16)
         mlp_held = mlp_grads(plan.after(d_shard), parts, dy_two, None, top, n_layers, None)
         g_sum, x_two_out = scatter(later(g_part, d_shard)), own(y_two)
+        wo_all = ring_gather(w_o2[0], (dx,), (g_part,)).reshape(-1, width)
         d_two, attn_held, last = own(dy_two), None, mlp_held[0]
 
         for layer_pair in reversed(range(n_pairs)):
@@ -336,31 +377,38 @@
             mid, low = 2 * layer_pair + 1, 2 * layer_pair
             g_part = mlp_forward(plan.after(last), s_one, w_in, w_out, low)
             d_one_bf = gather(d_shard, g_part)
-            mid_back, attn_held, _ = attn_back(plan, s_two, d_one_bf, w_t, w_o2, mid, n_heads, n_layers, attn_held)
+            finish, chip_sums = ring_scatter(g_part)
+            mid_back, attn_held, _ = attn_back(
+                plan.after(chip_sums), s_two, d_one_bf, w_t, w_o2, mid, n_heads, n_layers, attn_held
+            )
             x_two_shard = x_two_out - later(g_sum, mid_back)
             f_shard = rms_bf(x_two_shard)
             f_in = gather(f_shard)
             mid_sum = scatter(later(mid_back, f_shard))
-            f_back, attn_held, _ = attn_back(plan, f_in, d_one_bf, w_t, w_o2, mid + 1, n_heads, n_layers, attn_held)
-            g_sum, x_two_out = scatter(later(g_part, f_shard)), own(s_two)
+            f_back, attn_held, _ = attn_back(
+                plan, f_in, d_one_bf, w_t, w_o2, mid + 1, n_heads, n_layers, attn_held
+            )
+            low_two = own(s_two) - finish((f_in,), (f_back,))
             mid_two = d_two + rms_pull(x_two_shard, scatter(f_back).astype(F32))
             d_two = mid_two + rms_pull(own(s_two), later(mid_sum, f_back).astype(F32))
             both_d = gather(jnp.stack([mid_two.astype(BF16), d_two.astype(BF16)], axis=1))
-            dx, mid_parts = mlp_back(plan, s_one, both_d, 0, w_in, w_out, mid)
+            dx, mid_parts = mlp_back(plan.after(low_two), s_one, both_d, 0, w_in, w_out, mid)
+            mid_dx = dx
             dx, low_parts = mlp_back(plan, s_one, both_d, 1, w_in, w_out, low, dx)
-            x_two_shard = x_two_out - later(g_sum, dx)
-            d_one = d_one + rms_pull(own(s_one), scatter(dx).astype(F32))
-            heads, x_two = attn_forward(plan, gather(x_two_shard, d_one), w_t, low, n_heads)
+            x_two = ring_gather(low_two[0], (mid_dx,), (dx,))
+            heads, x_two = attn_forward(plan, x_two, w_t, low, n_heads)
+            x_two_shard = low_two
+            d_one = d_one + rms_pull(own(s_one), later(scatter(dx), heads).astype(F32))
             if layer_pair:
                 d_shard, last = d_one.astype(BF16), dx
                 g_sum, x_two_out = jnp.zeros_like(x_two_shard), x_two_shard
                 mlp_held = mlp_grads(plan, mid_parts, both_d, 0, mid, n_layers, mlp_held)
                 mlp_held = mlp_grads(plan, low_parts, both_d, 1, low, n_layers, mlp_held)
         f_back, attn_held, d_one_full = attn_back(
-            plan.after(heads), x_two, gather(d_one), w_t, w_o2, 0, n_heads, n_layers, attn_held, True
+            plan, x_two, gather(d_one), w_t, w_o2, 0, n_heads, n_layers, attn_held, True
         )
-        heads_all, wo_all = gather(heads, f_back), gather(w_o2[0], f_back)
-        d_two = d_two + rms_pull(x_two_shard, scatter(later(f_back, heads_all, wo_all)).astype(F32))
+        heads_all = gather(later(heads, d_one), f_back)
+        d_two = d_two + rms_pull(x_two_shard, scatter(later(f_back, heads_all)).astype(F32))
         tail = plan.after(f_back)
         mlp_held = mlp_grads(tail, mid_parts, both_d, 0, 1, n_layers, mlp_held)
         mlp_held = mlp_grads(tail, low_parts, both_d, 1, 0, n_layers, mlp_held)

time: 773 us -> 806 us (1.043)
  waiting for transfers between devices: 419 us -> 375 us
  starting transfers between devices: 1.42 us -> 37.1 us
  local copies, waits for them, and re-layouts: 11.4 us -> 41.5 us
  other arithmetic: 33.1 us -> 45.5 us
    ppermute x0 -> x23, waiting for transfers between devices: none -> 151 us  [the longest x14 139 us: shift(): return lax.ppermute(value, 'tp', pairs)]
    reduce_scatter x7 -> x6, waiting for transfers between devices: 187 us -> 62.7 us  [scatter(): return lax.psum_scatter(part, 'tp', scatter_dimension=0, tiled=True)]
    all_gather x8 -> x6, waiting for transfers between devices: 229 us -> 158 us  [gather(): return later(lax.all_gather(shard, 'tp', axis=0, tiled=True), *others)]
    ppermute x0 -> x23, starting transfers between devices: none -> 35.4 us  [the longest x14 18 us: shift(): return lax.ppermute(value, 'tp', pairs)]
    dynamic_update_slice x0 -> x16, local copies, waits for them, and re-layouts: none -> 12.7 us  [the longest x8 6.39 us: ring_gather(): lax.dynamic_update_slice_in_dim(whole, later(piece, *third)[None], place...]
    add x2 -> x4, other arithmetic: 5.47 us -> 14.8 us  [the longest x1 7.68 us: ring_scatter(): mine = lax.dynamic_index_in_dim(split, core, 1, False) + far]
  transfers between devices with their start and end apart: 15 -> 35, of which waited for: 13 -> 20; matrix products, arithmetic and copies ran while one was open for 2% -> 6% of each run, Pallas kernels for 35% -> 28%
where the time goes in v4:
time: 806 us; the launch traced here: 800 us
  waiting for transfers between devices  375 us (47%)
  Pallas kernels  287 us (36%)
  other arithmetic  45.5 us (6%)
  local copies, waits for them, and re-layouts  41.5 us (5%)
  starting transfers between devices  37.1 us (5%)
  between operations  14.8 us (2%)
    pallas_call x13, Pallas kernels, call(): pl.pallas_call(body, grid_spec=pltpu.PrefetchScalarGridSpec(num_scalar_pr...  287 us
    all_gather x6, waiting for transfers between devices, gather(): return later(lax.all_gather(shard, 'tp', axis=0, tiled=True), *others)  158 us
    ppermute x14, waiting for transfers between devices, shift(): return lax.ppermute(value, 'tp', pairs)  139 us
    reduce_scatter x6, waiting for transfers between devices, scatter(): return lax.psum_scatter(part, 'tp', scatter_dimension=0, tiled=True)  62.7 us
    ppermute x14, starting transfers between devices, shift(): return lax.ppermute(value, 'tp', pairs)  18 us
    ppermute x9, starting transfers between devices, swap(): lax.ppermute(value, 'tp', [(i, i + 1 - 2 * (i % CORES)) for i in range(n_...  17.4 us
  transfers between devices with their start and end apart: 35, of which 20 were waited for; matrix products, arithmetic and copies ran while one was open for 6% of the time, Pallas kernels for 28%

profile of v4, /device:TPU:113, one launch (start us, length us, event | category | flops | bytes accessed | tf_op | source)
XLA Modules:
  0.0 800.0 jit_solution(1332909667221456321)
XLA Ops:
  7.3 21.3 %shard_map.161 = (bf16[8,256,1408]{2,1,0:T(8,128)(2,1)}, bf16[8,256,1408]{2,1,0:T(8,128)(2,1)}, bf16[8,256,768]{2,1,0:T(8,128)(2,1)}, bf16[8,256,768]{2,1,0:T(8,128)(2,1)}) custom-call(s32[1]{0:T(128)} %bitcast.gate, f32[8,256,1408]{2,1,0:T(8,128)} %x_ref.3, f32[8,256,1408]{2,1,0:T(8,128)} %d_ref.3, bf16[3,1408,768]{2,1,0:T(8,128)(2,1)} %win_ref.9, ...), custom_call_target="tpu_custom_call" | custom-call | flops 13287555072 | bytes 17825792 | tf_op jit(solution)/shard_map/pallas_call | solution.py:59
  30.2 18.2 %shard_map.162 = f32[8,256,1408]{2,1,0:T(8,128)} custom-call(s32[1]{0:T(128)} %bitcast.gate, f32[8,256,1408]{2,1,0:T(8,128)} %x_ref.3, bf16[3,1408,768]{2,1,0:T(8,128)(2,1)} %win_ref.9, bf16[3,768,1408]{2,1,0:T(8,128)(2,1)} %wout_ref.9), custom_call_target="tpu_custom_call" | custom-call | flops 8858370048 | bytes 11534336 | tf_op jit(solution)/shard_map/pallas_call | solution.py:59
  48.5 18.6 %reduce-scatter.7.cloned.1.call-done = bf16[1,256,1408]{2,1,0:T(8,128)(2,1)} async-done(((bf16[8,256,1408]{2,1,0:T(8,128)(2,1)}), bf16[1,256,1408]{2,1,0:T(8,128)(2,1)}) %reduce-scatter.7.cloned.1.call-update) | async-done | bytes 720912 | tf_op jit(solution)/shard_map/reduce_scatter | solution.py:301
  73.3 19.6 %shard_map.163 = (f32[3,1408,768]{2,1,0:T(8,128)}, f32[3,768,1408]{2,1,0:T(8,128)}) custom-call(s32[1]{0:T(128)} %bitcast.gate, bf16[8,256,1408]{2,1,0:T(8,128)(2,1)} %get-tuple-element.87.a_ref, bf16[8,256,768]{2,1,0:T(8,128)(2,1)} %get-tuple-element.88.act_ref, bf16[8,256,768]{2,1,0:T(8,128)(2,1)} %get-tuple-element.89.dh_ref, f32[8,256,1408]{2,1,0:T(8,128)} %d_ref.3), custom_call_target="tpu_custom_call" | custom-call | flops 8858370048 | bytes 25952256 | tf_op jit(solution)/shard_map/pallas_call | solution.py:59
  92.9 18.3 %shard_map.164 = f32[8,256,1408]{2,1,0:T(8,128)} custom-call(s32[1]{0:T(128)} %bitcast.gate, f32[8,256,1408]{2,1,0:T(8,128)} %bitcast.100, bf16[3,1408,768]{2,1,0:T(8,128)(2,1)} %win_ref.9, bf16[3,768,1408]{2,1,0:T(8,128)(2,1)} %wout_ref.9), custom_call_target="tpu_custom_call" | custom-call | flops 8858370048 | bytes 11534336 | tf_op jit(solution)/shard_map/pallas_call | solution.py:59
  111.2 6.0 dynamic-slice_bitcast_fusion
  119.2 10.6 %collective-permute-done = f32[4,256,1408]{2,1,0:T(8,128)} collective-permute-done((f32[4,256,1408]{2,1,0:T(8,128)}, f32[4,256,1408]{2,1,0:T(8,128)}, u32[]{:S(2)}, u32[]{:S(2)}) %collective-permute-start) | collective-permute-done | bytes 5767200 | tf_op jit(solution)/shard_map/ppermute | solution.py:314
  129.9 7.7 bitcast_add_fusion
  137.6 32.0 %shard_map.165 = (bf16[8,256,1408]{2,1,0:T(8,128)(2,1)}, f32[3,528,1408]{2,1,0:T(8,128)}, f32[3,176,1408]{2,1,0:T(8,128)}) custom-call(s32[1]{0:T(128)} %bitcast.gate, f32[8,256,1408]{2,1,0:T(8,128)} %bitcast.119, bf16[8,256,1408]{2,1,0:T(8,128)(2,1)} %all-gather.7.cloned.1.call-done.d_ref, bf16[3,528,1408]{2,1,0:T(8,128)(2,1)} %bitcast.111, ...), custom_call_target="tpu_custom_call" | custom-call | flops 12180258816 | bytes 17661952 | tf_op jit(solution)/shard_map/pallas_call | solution.py:59
  177.8 34.5 %all-gather.9.cloned.1.call-done.x_ref = bf16[8,256,1408]{2,1,0:T(8,128)(2,1)} async-done(((bf16[1,256,1408]{2,1,0:T(8,128)(2,1)}), bf16[8,256,1408]{2,1,0:T(8,128)(2,1)}) %all-gather.9.cloned.1.call-update) | async-done | bytes 5767184 | tf_op jit(solution)/shard_map/all_gather | solution.py:304
  212.4 30.8 %shard_map.166 = (bf16[8,256,1408]{2,1,0:T(8,128)(2,1)}, f32[3,528,1408]{2,1,0:T(8,128)}, f32[3,176,1408]{2,1,0:T(8,128)}) custom-call(s32[1]{0:T(128)} %bitcast.gate, bf16[8,256,1408]{2,1,0:T(8,128)(2,1)} %all-gather.9.cloned.1.call-done.x_ref, ...), custom_call_target="tpu_custom_call", output_to_operand_aliasing={{1}: (5, {}), {2}: (6, {})} | custom-call | flops 12180258816 | bytes 17661952 | tf_op jit(solution)/shard_map/pallas_call | solution.py:59
  248.3 17.4 %collective-permute-done.4 = f32[128,1408]{1,0:T(8,128)S(1)} collective-permute-done((f32[128,1408]{1,0:T(8,128)S(1)}, f32[128,1408]{1,0:T(8,128)S(1)}, u32[]{:S(2)}, u32[]{:S(2)}) %collective-permute-start.4) | collective-permute-done | bytes 720928 | tf_op jit(solution)/shard_map/ppermute | solution.py:311
  274.3 20.1 %collective-permute-done.2 = f32[128,1408]{1,0:T(8,128)} collective-permute-done((f32[128,1408]{1,0:T(8,128)S(1)}, f32[128,1408]{1,0:T(8,128)}, u32[]{:S(2)}, u32[]{:S(2)}) %collective-permute-start.2) | collective-permute-done | bytes 720928 | tf_op jit(solution)/shard_map/ppermute | solution.py:311
  294.3 22.3 %collective-permute-done.3 = f32[128,1408]{1,0:T(8,128)} collective-permute-done((f32[128,1408]{1,0:T(8,128)}, f32[128,1408]{1,0:T(8,128)}, u32[]{:S(2)}, u32[]{:S(2)}) %collective-permute-start.3) | collective-permute-done | bytes 720928 | tf_op jit(solution)/shard_map/ppermute | solution.py:311
  326.6 5.0 convert_bitcast_fusion
  333.0 61.8 %all-gather.11.cloned.1.call-done.d_ref = bf16[8,2,256,1408]{3,2,1,0:T(8,128)(2,1)} async-done(((bf16[1,2,256,1408]{3,2,1,0:T(8,128)(2,1)}), bf16[8,2,256,1408]{3,2,1,0:T(8,128)(2,1)}) %all-gather.11.cloned.1.call-update) | async-done | bytes 11534352 | tf_op jit(solution)/shard_map/all_gather | solution.py:304
  394.8 20.7 %shard_map.167 = (bf16[8,256,1408]{2,1,0:T(8,128)(2,1)}, bf16[8,256,1408]{2,1,0:T(8,128)(2,1)}, bf16[8,256,768]{2,1,0:T(8,128)(2,1)}, bf16[8,256,768]{2,1,0:T(8,128)(2,1)}) custom-call(s32[1]{0:T(128)} %bitcast.gate, f32[8,256,1408]{2,1,0:T(8,128)} %bitcast.101, bf16[8,2,256,1408]{3,2,1,0:T(8,128)(2,1)} %all-gather.11.cloned.1.call-done.d_ref, ...), custom_call_target="tpu_custom_call" | custom-call | flops 13287555072 | bytes 17825792 | tf_op jit(solution)/shard_map/pallas_call | solution.py:59
  415.5 21.2 %shard_map.168 = (bf16[8,256,1408]{2,1,0:T(8,128)(2,1)}, bf16[8,256,1408]{2,1,0:T(8,128)(2,1)}, bf16[8,256,768]{2,1,0:T(8,128)(2,1)}, bf16[8,256,768]{2,1,0:T(8,128)(2,1)}) custom-call(s32[1]{0:T(128)} %bitcast.gate, f32[8,256,1408]{2,1,0:T(8,128)} %bitcast.102, bf16[8,2,256,1408]{3,2,1,0:T(8,128)(2,1)} %all-gather.11.cloned.1.call-done.d_ref, ...), custom_call_target="tpu_custom_call" | custom-call | flops 13287555072 | bytes 17825792 | tf_op jit(solution)/shard_map/pallas_call | solution.py:59
  442.4 42.1 %collective-permute-done.8 = f32[256,1408]{1,0:T(8,128)} collective-permute-done((f32[256,1408]{1,0:T(8,128)S(1)}, f32[256,1408]{1,0:T(8,128)}, u32[]{:S(2)}, u32[]{:S(2)}) %collective-permute-start.8) | collective-permute-done | bytes 1441824 | tf_op jit(solution)/shard_map/ppermute | solution.py:311
  490.4 5.4 broadcast_in_dim.66
  502.1 11.3 %collective-permute-done.13 = f32[128,1408]{1,0:T(8,128)S(1)} collective-permute-done((f32[128,1408]{1,0:T(8,128)S(1)}, f32[128,1408]{1,0:T(8,128)S(1)}, u32[]{:S(2)}, u32[]{:S(2)}) %collective-permute-start.13) | collective-permute-done | bytes 720928 | tf_op jit(solution)/shard_map/ppermute | solution.py:311
  522.0 15.6 %shard_map.169 = (bf16[176,2048]{1,0:T(8,128)(2,1)}, f32[8,256,1408]{2,1,0:T(8,128)}) custom-call(s32[1]{0:T(128)} %bitcast.gate, f32[8,256,1408]{2,1,0:T(8,128)} %bitcast_dynamic-update-slice_fusion.x_ref, bf16[3,528,1408]{2,1,0:T(8,128)(2,1)} %bitcast.113), custom_call_target="tpu_custom_call" | custom-call | flops 3045064704 | bytes 12255232 | tf_op jit(solution)/shard_map/pallas_call | solution.py:59
  544.4 58.2 %all-gather.13.cloned.1.call-done.d_ref = f32[8,256,1408]{2,1,0:T(8,128)} async-done(((f32[1,256,1408]{2,1,0:T(8,128)}), f32[8,256,1408]{2,1,0:T(8,128)}) %all-gather.13.cloned.1.call-update) | async-done | bytes 11534352 | tf_op jit(solution)/shard_map/all_gather | solution.py:304
  602.7 33.0 %shard_map.170 = (bf16[8,256,1408]{2,1,0:T(8,128)(2,1)}, f32[3,528,1408]{2,1,0:T(8,128)}, f32[3,176,1408]{2,1,0:T(8,128)}, f32[8,256,1408]{2,1,0:T(8,128)}) custom-call(s32[1]{0:T(128)} %bitcast.gate, f32[8,256,1408]{2,1,0:T(8,128)} %get-tuple-element.182.x_ref, ...), custom_call_target="tpu_custom_call", output_to_operand_aliasing={{1}: (5, {}), {2}: (6, {})} | custom-call | flops 12180258816 | bytes 29196288 | tf_op jit(solution)/shard_map/pallas_call | solution.py:59
  639.9 37.6 %reduce-scatter.17.cloned.1.call-done = bf16[1,256,1408]{2,1,0:T(8,128)(2,1)} async-done(((bf16[8,256,1408]{2,1,0:T(8,128)(2,1)}), bf16[1,256,1408]{2,1,0:T(8,128)(2,1)}) %reduce-scatter.17.cloned.1.call-update) | async-done | bytes 720912 | tf_op jit(solution)/shard_map/reduce_scatter | solution.py:301
  687.7 9.0 %collective-permute-done.16 = bf16[176,1408]{1,0:T(8,128)(2,1)S(1)} collective-permute-done((bf16[176,1408]{1,0:T(8,128)(2,1)S(1)}, bf16[176,1408]{1,0:T(8,128)(2,1)S(1)}, u32[]{:S(2)}, u32[]{:S(2)}) %collective-permute-start.16) | collective-permute-done | bytes 495648 | tf_op jit(solution)/shard_map/ppermute | solution.py:311
  696.7 7.0 collective-permute-start.17
  708.7 11.0 %collective-permute-done.21 = bf16[88,1408]{1,0:T(8,128)(2,1)S(1)} collective-permute-done((bf16[88,1408]{1,0:T(8,128)(2,1)S(1)}, bf16[88,1408]{1,0:T(8,128)(2,1)S(1)}, u32[]{:S(2)}, u32[]{:S(2)}) %collective-permute-start.21) | collective-permute-done | bytes 247840 | tf_op jit(solution)/shard_map/ppermute | solution.py:311
  727.7 17.3 %shard_map.171 = f32[8,256,1408]{2,1,0:T(8,128)} custom-call(s32[1]{0:T(128)} %bitcast.gate, f32[8,256,1408]{2,1,0:T(8,128)} %bitcast.103, bf16[1408,2048]{1,0:T(8,128)(2,1)} %all-gather.15.cloned.1.call-done.h_ref, bf16[1408,1408]{1,0:T(8,128)(2,1)} %bitcast.110), custom_call_target="tpu_custom_call" | custom-call | flops 8120172544 | bytes 11534336 | tf_op jit(solution)/shard_map/pallas_call | solution.py:59
  745.0 19.2 %shard_map.172 = (f32[3,1408,768]{2,1,0:T(8,128)}, f32[3,768,1408]{2,1,0:T(8,128)}) custom-call(s32[1]{0:T(128)} %bitcast.gate, bf16[8,256,1408]{2,1,0:T(8,128)(2,1)} %get-tuple-element.147.a_ref, bf16[8,256,768]{2,1,0:T(8,128)(2,1)} %get-tuple-element.148.act_ref, ...), custom_call_target="tpu_custom_call", output_to_operand_aliasing={{0}: (5, {}), {1}: (6, {})} | custom-call | flops 8858370048 | bytes 25952256 | tf_op jit(solution)/shard_map/pallas_call | solution.py:59
  764.3 19.1 %shard_map.173 = (f32[3,1408,768]{2,1,0:T(8,128)}, f32[3,768,1408]{2,1,0:T(8,128)}) custom-call(s32[1]{0:T(128)} %bitcast.gate, bf16[8,256,1408]{2,1,0:T(8,128)(2,1)} %get-tuple-element.144.a_ref, bf16[8,256,768]{2,1,0:T(8,128)(2,1)} %get-tuple-element.145.act_ref, ...), custom_call_target="tpu_custom_call", output_to_operand_aliasing={{0}: (5, {}), {1}: (6, {})} | custom-call | flops 8858370048 | bytes 25952256 | tf_op jit(solution)/shard_map/pallas_call | solution.py:59
  783.4 9.5 %copy.59 = f32[8,256,1408]{2,1,0:T(8,128)} copy(f32[8,256,1408]{2,1,0:T(8,128)} %all-gather.17.cloned.1.call-done) | data formatting | bytes 23068672
  (138 shorter events, 103.7 us)
Async XLA Ops:
  7.2 59.9 %reduce-scatter.7.cloned.1.call-start = ((), (), s32[]{:S(2)}) async-start(), calls=%async_computation.6 | async-start | bytes 6488064 | tf_op jit(solution)/shard_map/reduce_scatter | solution.py:301
  28.6 109.0 %all-gather.7.cloned.1.call-start = ((), (), s32[]{:S(2)}) async-start(), calls=%async_computation.8 | async-start | bytes 6488064 | tf_op jit(solution)/shard_map/all_gather | solution.py:304
  72.2 101.8 %reduce-scatter.9.cloned.1.call-start = ((), (), s32[]{:S(2)}) async-start(), calls=%async_computation.7 | async-start | bytes 12976128 | tf_op jit(solution)/shard_map/reduce_scatter | solution.py:301
  73.0 139.4 %all-gather.9.cloned.1.call-start = ((), (), s32[]{:S(2)}) async-start(), calls=%async_computation.9 | async-start | bytes 6488064 | tf_op jit(solution)/shard_map/all_gather | solution.py:304
  177.1 143.8 %reduce-scatter.13.cloned.1.call-start = ((), (), s32[]{:S(2)}) async-start(), calls=%async_computation.11 | async-start | bytes 6488064 | tf_op jit(solution)/shard_map/reduce_scatter | solution.py:301
  177.8 147.3 %reduce-scatter.11.cloned.1.call-start = ((), (), s32[]{:S(2)}) async-start(), calls=%async_computation.10 | async-start | bytes 6488064 | tf_op jit(solution)/shard_map/reduce_scatter | solution.py:301
  243.2 151.5 %all-gather.11.cloned.1.call-start = ((), (), s32[]{:S(2)}) async-start(), calls=%async_computation.12 | async-start | bytes 12976128 | tf_op jit(solution)/shard_map/all_gather | solution.py:304
  246.9 18.9 %collective-permute-start.4 = (f32[128,1408]{1,0:T(8,128)S(1)}, f32[128,1408]{1,0:T(8,128)S(1)}, u32[]{:S(2)}, u32[]{:S(2)}) collective-permute-start(f32[128,1408]{1,0:T(8,128)S(1)} %get-tuple-element.169), channel_id=1, source_target_pairs={{0,6},{1,7},{2,0},{3,1},{4,2},{5,3},{6,4},{7,5},{8,14},{9,15},{10,... | collective-permute-start | bytes 2162696 | tf_op jit(solution)/shard_map/ppermute | solution.py:311
  247.5 19.3 %collective-permute-start.1 = (f32[128,1408]{1,0:T(8,128)S(1)}, f32[128,1408]{1,0:T(8,128)S(1)}, u32[]{:S(2)}, u32[]{:S(2)}) collective-permute-start(f32[128,1408]{1,0:T(8,128)S(1)} %get-tuple-element.168), channel_id=1, source_target_pairs={{0,2},{1,3},{2,4},{3,5},{4,6},{5,7},{6,0},{7,1},{8,10},{9,11},{10,... | collective-permute-start | bytes 2162696 | tf_op jit(solution)/shard_map/ppermute | solution.py:311
  268.3 26.0 %collective-permute-start.2 = (f32[128,1408]{1,0:T(8,128)S(1)}, f32[128,1408]{1,0:T(8,128)}, u32[]{:S(2)}, u32[]{:S(2)}) collective-permute-start(f32[128,1408]{1,0:T(8,128)S(1)} %get-tuple-element.171), channel_id=1, source_target_pairs={{0,2},{1,3},{2,4},{3,5},{4,6},{5,7},{6,0},{7,1},{8,10},{9,11},{10,... | collective-permute-start | bytes 2162696 | tf_op jit(solution)/shard_map/ppermute | solution.py:311
  268.5 25.8 %collective-permute-start.5 = (f32[128,1408]{1,0:T(8,128)S(1)}, f32[128,1408]{1,0:T(8,128)}, u32[]{:S(2)}, u32[]{:S(2)}) collective-permute-start(f32[128,1408]{1,0:T(8,128)S(1)} %get-tuple-element.172), channel_id=1, source_target_pairs={{0,6},{1,7},{2,0},{3,1},{4,2},{5,3},{6,4},{7,5},{8,14},{9,15},{10,... | collective-permute-start | bytes 2162696 | tf_op jit(solution)/shard_map/ppermute | solution.py:311
  271.1 45.5 %collective-permute-start.3 = (f32[128,1408]{1,0:T(8,128)}, f32[128,1408]{1,0:T(8,128)}, u32[]{:S(2)}, u32[]{:S(2)}) collective-permute-start(f32[128,1408]{1,0:T(8,128)} %get-tuple-element.167), channel_id=1, source_target_pairs={{0,6},{1,7},{2,0},{3,1},{4,2},{5,3},{6,4},{7,5},{8,14},{9,15},{10,... | collective-permute-start | bytes 2162696 | tf_op jit(solution)/shard_map/ppermute | solution.py:311
  273.9 45.0 %collective-permute-start.6 = (f32[128,1408]{1,0:T(8,128)S(1)}, f32[128,1408]{1,0:T(8,128)S(1)}, u32[]{:S(2)}, u32[]{:S(2)}) collective-permute-start(f32[128,1408]{1,0:T(8,128)S(1)} %copy-done.7), channel_id=1, source_target_pairs={{0,2},{1,3},{2,4},{3,5},{4,6},{5,7},{6,0},{7,1},{8,10},{9,11},{10,... | collective-permute-start | bytes 2162696 | tf_op jit(solution)/shard_map/ppermute | solution.py:311
  332.9 204.7 %reduce-scatter.15.cloned.1.call-start = ((), (), s32[]{:S(2)}) async-start(), calls=%async_computation.13 | async-start | bytes 6488064 | tf_op jit(solution)/shard_map/reduce_scatter | solution.py:301
  436.8 165.9 %all-gather.13.cloned.1.call-start = ((), (), s32[]{:S(2)}) async-start(), calls=%async_computation.14 | async-start | bytes 12976128 | tf_op jit(solution)/shard_map/all_gather | solution.py:304
  437.0 47.5 %collective-permute-start.8 = (f32[256,1408]{1,0:T(8,128)S(1)}, f32[256,1408]{1,0:T(8,128)}, u32[]{:S(2)}, u32[]{:S(2)}) collective-permute-start(f32[256,1408]{1,0:T(8,128)S(1)} %bitcast.106), channel_id=1, source_target_pairs={{0,2},{1,3},{2,4},{3,5},{4,6},{5,7},{6,0},{7,1},{8,10},{9,11},{10,... | collective-permute-start | bytes 4325384 | tf_op jit(solution)/shard_map/ppermute | solution.py:311
  437.7 50.0 %collective-permute-start.10 = (f32[256,1408]{1,0:T(8,128)S(1)}, f32[256,1408]{1,0:T(8,128)S(1)}, u32[]{:S(2)}, u32[]{:S(2)}) collective-permute-start(f32[256,1408]{1,0:T(8,128)S(1)} %bitcast.107), channel_id=1, source_target_pairs={{0,6},{1,7},{2,0},{3,1},{4,2},{5,3},{6,4},{7,5},{8,14},{9,15},{10,... | collective-permute-start | bytes 4325384 | tf_op jit(solution)/shard_map/ppermute | solution.py:311
  439.8 50.6 %collective-permute-start.7 = (f32[256,1408]{1,0:T(8,128)S(1)}, f32[256,1408]{1,0:T(8,128)}, u32[]{:S(2)}, u32[]{:S(2)}) collective-permute-start(f32[256,1408]{1,0:T(8,128)S(1)} %bitcast.108), channel_id=1, source_target_pairs={{0,1},{1,0},{2,3},{3,2},{4,5},{5,4},{6,7},{7,6},{8,9},{9,8},{10,11... | collective-permute-start | bytes 4325384 | tf_op jit(solution)/shard_map/ppermute | solution.py:314
  485.7 30.4 %collective-permute-start.9 = (f32[256,1408]{1,0:T(8,128)}, f32[256,1408]{1,0:T(8,128)S(1)}, u32[]{:S(2)}, u32[]{:S(2)}) collective-permute-start(f32[256,1408]{1,0:T(8,128)} %collective-permute-done.8), channel_id=1, source_target_pairs={{0,1},{1,0},{2,3},{3,2},{4,5},{5,4},{6,7},{7,6},{8,9},{9,8},{10,11... | collective-permute-start | bytes 4325384 | tf_op jit(solution)/shard_map/ppermute | solution.py:314
  487.7 28.4 %collective-permute-start.11 = (f32[256,1408]{1,0:T(8,128)S(1)}, f32[256,1408]{1,0:T(8,128)S(1)}, u32[]{:S(2)}, u32[]{:S(2)}) collective-permute-start(f32[256,1408]{1,0:T(8,128)S(1)} %collective-permute-done.10), channel_id=1, source_target_pairs={{0,1},{1,0},{2,3},{3,2},{4,5},{5,4},{6,7},{7,6},{8,9},{9,8},{10,11... | collective-permute-start | bytes 4325384 | tf_op jit(solution)/shard_map/ppermute | solution.py:314
  487.8 25.6 %collective-permute-start.13 = (f32[128,1408]{1,0:T(8,128)S(1)}, f32[128,1408]{1,0:T(8,128)S(1)}, u32[]{:S(2)}, u32[]{:S(2)}) collective-permute-start(f32[128,1408]{1,0:T(8,128)S(1)} %slice.65), channel_id=1, source_target_pairs={{0,6},{1,7},{2,0},{3,1},{4,2},{5,3},{6,4},{7,5},{8,14},{9,15},{10,... | collective-permute-start | bytes 2162696 | tf_op jit(solution)/shard_map/ppermute | solution.py:311
  490.4 24.7 %collective-permute-start.12 = (f32[128,1408]{1,0:T(8,128)S(1)}, f32[128,1408]{1,0:T(8,128)S(1)}, u32[]{:S(2)}, u32[]{:S(2)}) collective-permute-start(f32[128,1408]{1,0:T(8,128)S(1)} %slice.64), channel_id=1, source_target_pairs={{0,2},{1,3},{2,4},{3,5},{4,6},{5,7},{6,0},{7,1},{8,10},{9,11},{10,... | collective-permute-start | bytes 2162696 | tf_op jit(solution)/shard_map/ppermute | solution.py:311
  543.7 95.9 %all-gather.15.cloned.1.call-start = ((), (), s32[]{:S(2)}) async-start(), calls=%async_computation.15 | async-start | bytes 6488064 | tf_op jit(solution)/shard_map/all_gather | solution.py:304
  544.4 133.1 %reduce-scatter.17.cloned.1.call-start = ((), (), s32[]{:S(2)}) async-start(), calls=%async_computation.16 | async-start | bytes 6488064 | tf_op jit(solution)/shard_map/reduce_scatter | solution.py:301
  639.6 143.8 %all-gather.17.cloned.1.call-start = ((), (), s32[]{:S(2)}) async-start(), calls=%async_computation.17 | async-start | bytes 12976128 | tf_op jit(solution)/shard_map/all_gather | solution.py:304
  681.7 15.0 %collective-permute-start.16 = (bf16[176,1408]{1,0:T(8,128)(2,1)S(1)}, bf16[176,1408]{1,0:T(8,128)(2,1)S(1)}, u32[]{:S(2)}, u32[]{:S(2)}) collective-permute-start(bf16[176,1408]{1,0:T(8,128)(2,1)S(1)} %bitcast.115), channel_id=1, source_target_pairs={{0,2},{1,3},{2,4},{3,5},{4,6},{5,7},{6,0},{7,1},{8,10},{9,11},{10,... | collective-permute-start | bytes 1486856 | tf_op jit(solution)/shard_map/ppermute | solution.py:311
  682.7 21.0 %collective-permute-start.18 = (bf16[176,1408]{1,0:T(8,128)(2,1)S(1)}, bf16[176,1408]{1,0:T(8,128)(2,1)S(1)}, u32[]{:S(2)}, u32[]{:S(2)}) collective-permute-start(bf16[176,1408]{1,0:T(8,128)(2,1)S(1)} %bitcast.116), channel_id=1, source_target_pairs={{0,6},{1,7},{2,0},{3,1},{4,2},{5,3},{6,4},{7,5},{8,14},{9,15},{10,... | collective-permute-start | bytes 1486856 | tf_op jit(solution)/shard_map/ppermute | solution.py:311
  685.2 23.4 %collective-permute-start.15 = (bf16[176,1408]{1,0:T(8,128)(2,1)S(1)}, bf16[176,1408]{1,0:T(8,128)(2,1)S(1)}, u32[]{:S(2)}, u32[]{:S(2)}) collective-permute-start(bf16[176,1408]{1,0:T(8,128)(2,1)S(1)} %bitcast.117), channel_id=1, source_target_pairs={{0,1},{1,0},{2,3},{3,2},{4,5},{5,4},{6,7},{7,6},{8,9},{9,8},{10,11... | collective-permute-start | bytes 1486856 | tf_op jit(solution)/shard_map/ppermute | solution.py:314
  696.7 27.5 %collective-permute-start.17 = (bf16[176,1408]{1,0:T(8,128)(2,1)S(1)}, bf16[176,1408]{1,0:T(8,128)(2,1)S(1)}, u32[]{:S(2)}, u32[]{:S(2)}) collective-permute-start(bf16[176,1408]{1,0:T(8,128)(2,1)S(1)} %collective-permute-done.16), channel_id=1, source_target_pairs={{0,1},{1,0},{2,3},{3,2},{4,5},{5,4},{6,7},{7,6},{8,9},{9,8},{10,11... | collective-permute-start | bytes 1486856 | tf_op jit(solution)/shard_map/ppermute | solution.py:314
  703.7 20.5 %collective-permute-start.19 = (bf16[176,1408]{1,0:T(8,128)(2,1)S(1)}, bf16[176,1408]{1,0:T(8,128)(2,1)S(1)}, u32[]{:S(2)}, u32[]{:S(2)}) collective-permute-start(bf16[176,1408]{1,0:T(8,128)(2,1)S(1)} %collective-permute-done.18), channel_id=1, source_target_pairs={{0,1},{1,0},{2,3},{3,2},{4,5},{5,4},{6,7},{7,6},{8,9},{9,8},{10,11... | collective-permute-start | bytes 1486856 | tf_op jit(solution)/shard_map/ppermute | solution.py:314
  705.1 14.5 %collective-permute-start.21 = (bf16[88,1408]{1,0:T(8,128)(2,1)S(1)}, bf16[88,1408]{1,0:T(8,128)(2,1)S(1)}, u32[]{:S(2)}, u32[]{:S(2)}) collective-permute-start(bf16[88,1408]{1,0:T(8,128)(2,1)S(1)} %slice.68), channel_id=1, source_target_pairs={{0,6},{1,7},{2,0},{3,1},{4,2},{5,3},{6,4},{7,5},{8,14},{9,15},{10,... | collective-permute-start | bytes 743432 | tf_op jit(solution)/shard_map/ppermute | solution.py:311
  708.5 14.5 %collective-permute-start.20 = (bf16[88,1408]{1,0:T(8,128)(2,1)S(1)}, bf16[88,1408]{1,0:T(8,128)(2,1)S(1)}, u32[]{:S(2)}, u32[]{:S(2)}) collective-permute-start(bf16[88,1408]{1,0:T(8,128)(2,1)S(1)} %slice.67), channel_id=1, source_target_pairs={{0,2},{1,3},{2,4},{3,5},{4,6},{5,7},{6,0},{7,1},{8,10},{9,11},{10,... | collective-permute-start | bytes 743432 | tf_op jit(solution)/shard_map/ppermute | solution.py:311
  (11 other events, 73.0 us)
Sparse Core Ops, SparseCore 0:
  28.7 38.2 reduce-scatter.6
  72.3 36.2 all-gather.6
  111.5 62.4 reduce-scatter.8
  177.2 35.0 all-gather.8
  215.1 34.9 reduce-scatter.12
  252.9 72.1 reduce-scatter.10
  333.0 61.7 all-gather.10
  436.9 77.4 reduce-scatter.14
  543.8 58.7 all-gather.12
  604.7 34.8 all-gather.14
  642.4 34.9 reduce-scatter.16
  680.8 69.8 all-gather.16

commit v5 on v4

--- a/solution.py
+++ b/solution.py
@@ -313,12 +313,20 @@
     def swap(value):
         return lax.ppermute(value, "tp", [(i, i + 1 - 2 * (i % CORES)) for i in range(n_tp)])
 
+    def core_sums(part):
+        core = lax.rem(lax.axis_index("tp"), CORES)
+        split = part.reshape((chips, CORES) + part.shape[1:])
+        far = swap(lax.dynamic_index_in_dim(split, 1 - core, 1, False))
+        return (lax.dynamic_index_in_dim(split, core, 1, False).astype(F32) + far.astype(F32)).astype(part.dtype)
+
+    def like_scatter(sums):
+        alike = [list(range(core, n_tp, CORES)) for core in range(CORES)]
+        return lax.psum_scatter(sums, "tp", scatter_dimension=0, axis_index_groups=alike, tiled=True)
+
     def ring_scatter(part):
-        chip, core = lax.div(lax.axis_index("tp"), CORES), lax.rem(lax.axis_index("tp"), CORES)
-        split = part.reshape((chips, CORES) + part.shape[1:])
+        chip = lax.div(lax.axis_index("tp"), CORES)
         half = part.shape[1] // 2
-        far = swap(lax.dynamic_index_in_dim(split, 1 - core, 1, False))
-        mine = lax.dynamic_index_in_dim(split, core, 1, False) + far
+        mine = core_sums(part)
         ahead, across, behind, here = (
             lax.dynamic_index_in_dim(mine, lax.rem(chip + hops, chips), 0, False) for hops in (1, 2, 3, 0)
         )
@@ -365,10 +373,12 @@
         dx, parts = mlp_back(plan, y_one, dy_two, None, w_in, w_out, top)
         g_back = scatter(dx)
         g_part = mlp_forward(plan.after(dx), y_one, w_in, w_out, top)
-        d_one = own(dy_one) + rms_pull(own(y_one), later(g_back, g_part).astype(F32))
+        g_sums = core_sums(g_part)
+        d_one = own(dy_one) + rms_pull(own(y_one), later(g_back, g_sums).astype(F32))
         d_shard = d_one.astype(BF16)
         mlp_held = mlp_grads(plan.after(d_shard), parts, dy_two, None, top, n_layers, None)
-        g_sum, x_two_out = scatter(later(g_part, d_shard)), own(y_two)
+        g_sum = like_scatter(later(g_sums, d_shard))
+        x_two_out = own(y_two)
         wo_all = ring_gather(w_o2[0], (dx,), (g_part,)).reshape(-1, width)
         d_two, attn_held, last = own(dy_two), None, mlp_held[0]
 
@@ -381,10 +391,11 @@
             mid_back, attn_held, _ = attn_back(
                 plan.after(chip_sums), s_two, d_one_bf, w_t, w_o2, mid, n_heads, n_layers, attn_held
             )
-            x_two_shard = x_two_out - later(g_sum, mid_back)
+            mid_sums = core_sums(mid_back)
+            x_two_shard = x_two_out - later(g_sum, mid_sums)
             f_shard = rms_bf(x_two_shard)
             f_in = gather(f_shard)
-            mid_sum = scatter(later(mid_back, f_shard))
+            mid_sum = like_scatter(later(mid_sums, f_shard))
             f_back, attn_held, _ = attn_back(
                 plan, f_in, d_one_bf, w_t, w_o2, mid + 1, n_heads, n_layers, attn_held
             )
@@ -392,10 +403,10 @@
             mid_two = d_two + rms_pull(x_two_shard, scatter(f_back).astype(F32))
             d_two = mid_two + rms_pull(own(s_two), later(mid_sum, f_back).astype(F32))
             both_d = gather(jnp.stack([mid_two.astype(BF16), d_two.astype(BF16)], axis=1))
-            dx, mid_parts = mlp_back(plan.after(low_two), s_one, both_d, 0, w_in, w_out, mid)
+            dx, mid_parts = mlp_back(plan, s_one, both_d, 0, w_in, w_out, mid)
             mid_dx = dx
             dx, low_parts = mlp_back(plan, s_one, both_d, 1, w_in, w_out, low, dx)
-            x_two = ring_gather(low_two[0], (mid_dx,), (dx,))
+            x_two = ring_gather(later(low_two[0], both_d), (mid_dx,), (dx,))
             heads, x_two = attn_forward(plan, x_two, w_t, low, n_heads)
             x_two_shard = low_two
             d_one = d_one + rms_pull(own(s_one), later(scatter(dx), heads).astype(F32))

time: 806 us -> 817 us (1.014)
  other arithmetic: 45.5 us -> 56.6 us
  waiting for transfers between devices: 375 us -> 366 us
    reduce_scatter x6 -> x4, waiting for transfers between devices: 62.7 us -> 38.1 us  [scatter(): return lax.psum_scatter(part, 'tp', scatter_dimension=0, tiled=True)]
    ppermute x9 -> x11, waiting for transfers between devices: 11.9 us -> 24.7 us  [swap(): lax.ppermute(value, 'tp', [(i, i + 1 - 2 * (i % CORES)) for i in range(n_...]
    ppermute x9 -> x11, starting transfers between devices: 17.4 us -> 16.4 us  [swap(): lax.ppermute(value, 'tp', [(i, i + 1 - 2 * (i % CORES)) for i in range(n_...]
  transfers between devices with their start and end apart: 35 -> 37, of which waited for: 20 -> 20; matrix products, arithmetic and copies ran while one was open for 6% -> 8% of each run, Pallas kernels for 28% -> 28%
where the time goes in v5:
time: 817 us; the launch traced here: 809 us
  waiting for transfers between devices  366 us (45%)
  Pallas kernels  286 us (35%)
  other arithmetic  56.6 us (7%)
  local copies, waits for them, and re-layouts  49 us (6%)
  starting transfers between devices  36.8 us (5%)
  between operations  15 us (2%)
    pallas_call x13, Pallas kernels, call(): pl.pallas_call(body, grid_spec=pltpu.PrefetchScalarGridSpec(num_scalar_pr...  286 us
    all_gather x6, waiting for transfers between devices, gather(): return later(lax.all_gather(shard, 'tp', axis=0, tiled=True), *others)  161 us
    ppermute x14, waiting for transfers between devices, shift(): return lax.ppermute(value, 'tp', pairs)  141 us
    reduce_scatter x4, waiting for transfers between devices, scatter(): return lax.psum_scatter(part, 'tp', scatter_dimension=0, tiled=True)  38.1 us
    ppermute x11, waiting for transfers between devices, swap(): lax.ppermute(value, 'tp', [(i, i + 1 - 2 * (i % CORES)) for i in range(n_...  24.7 us
    ppermute x14, starting transfers between devices, shift(): return lax.ppermute(value, 'tp', pairs)  18 us
    ppermute x11, starting transfers between devices, swap(): lax.ppermute(value, 'tp', [(i, i + 1 - 2 * (i % CORES)) for i in range(n_...  16.4 us
  transfers between devices with their start and end apart: 37, of which 20 were waited for; matrix products, arithmetic and copies ran while one was open for 8% of the time, Pallas kernels for 28%

profile of v5, /device:TPU:113, one launch (start us, length us, event | category | flops | bytes accessed | tf_op | source)
XLA Modules:
  0.0 809.5 jit_solution(8177992245964493468)
XLA Ops:
  7.3 21.3 %shard_map.161 = (bf16[8,256,1408]{2,1,0:T(8,128)(2,1)}, bf16[8,256,1408]{2,1,0:T(8,128)(2,1)}, bf16[8,256,768]{2,1,0:T(8,128)(2,1)}, bf16[8,256,768]{2,1,0:T(8,128)(2,1)}) custom-call(s32[1]{0:T(128)} %bitcast.gate, f32[8,256,1408]{2,1,0:T(8,128)} %x_ref.3, f32[8,256,1408]{2,1,0:T(8,128)} %d_ref.3, bf16[3,1408,768]{2,1,0:T(8,128)(2,1)} %win_ref.9, ...), custom_call_target="tpu_custom_call" | custom-call | flops 13287555072 | bytes 17825792 | tf_op jit(solution)/shard_map/pallas_call | solution.py:59
  28.7 18.2 %shard_map.162 = f32[8,256,1408]{2,1,0:T(8,128)} custom-call(s32[1]{0:T(128)} %bitcast.gate, f32[8,256,1408]{2,1,0:T(8,128)} %x_ref.3, bf16[3,1408,768]{2,1,0:T(8,128)(2,1)} %win_ref.9, bf16[3,768,1408]{2,1,0:T(8,128)(2,1)} %wout_ref.9), custom_call_target="tpu_custom_call" | custom-call | flops 8858370048 | bytes 11534336 | tf_op jit(solution)/shard_map/pallas_call | solution.py:59
  46.9 5.7 dynamic-slice_bitcast_fusion.1
  54.9 9.1 %collective-permute-done = f32[4,256,1408]{2,1,0:T(8,128)} collective-permute-done((f32[4,256,1408]{2,1,0:T(8,128)}, f32[4,256,1408]{2,1,0:T(8,128)}, u32[]{:S(2)}, u32[]{:S(2)}) %collective-permute-start) | collective-permute-done | bytes 5767200 | tf_op jit(solution)/shard_map/ppermute | solution.py:314
  63.9 7.6 bitcast_add_fusion.1
  77.1 19.6 %shard_map.163 = (f32[3,1408,768]{2,1,0:T(8,128)}, f32[3,768,1408]{2,1,0:T(8,128)}) custom-call(s32[1]{0:T(128)} %bitcast.gate, bf16[8,256,1408]{2,1,0:T(8,128)(2,1)} %get-tuple-element.87.a_ref, bf16[8,256,768]{2,1,0:T(8,128)(2,1)} %get-tuple-element.88.act_ref, bf16[8,256,768]{2,1,0:T(8,128)(2,1)} %get-tuple-element.89.dh_ref, f32[8,256,1408]{2,1,0:T(8,128)} %d_ref.3), custom_call_target="tpu_custom_call" | custom-call | flops 8858370048 | bytes 25952256 | tf_op jit(solution)/shard_map/pallas_call | solution.py:59
  96.8 18.4 %shard_map.164 = f32[8,256,1408]{2,1,0:T(8,128)} custom-call(s32[1]{0:T(128)} %bitcast.gate, f32[8,256,1408]{2,1,0:T(8,128)} %bitcast.117, bf16[3,1408,768]{2,1,0:T(8,128)(2,1)} %win_ref.9, bf16[3,768,1408]{2,1,0:T(8,128)(2,1)} %wout_ref.9), custom_call_target="tpu_custom_call" | custom-call | flops 8858370048 | bytes 11534336 | tf_op jit(solution)/shard_map/pallas_call | solution.py:59
  115.2 5.6 dynamic-slice_bitcast_fusion
  121.4 9.1 %collective-permute-done.1 = f32[4,256,1408]{2,1,0:T(8,128)} collective-permute-done((f32[4,256,1408]{2,1,0:T(8,128)}, f32[4,256,1408]{2,1,0:T(8,128)}, u32[]{:S(2)}, u32[]{:S(2)}) %collective-permute-start.1) | collective-permute-done | bytes 5767200 | tf_op jit(solution)/shard_map/ppermute | solution.py:314
  130.5 7.4 bitcast_add_fusion
  137.9 31.8 %shard_map.165 = (bf16[8,256,1408]{2,1,0:T(8,128)(2,1)}, f32[3,528,1408]{2,1,0:T(8,128)}, f32[3,176,1408]{2,1,0:T(8,128)}) custom-call(s32[1]{0:T(128)} %bitcast.gate, f32[8,256,1408]{2,1,0:T(8,128)} %bitcast.140, bf16[8,256,1408]{2,1,0:T(8,128)(2,1)} %all-gather.7.cloned.1.call-done.d_ref, bf16[3,528,1408]{2,1,0:T(8,128)(2,1)} %bitcast.132, ...), custom_call_target="tpu_custom_call" | custom-call | flops 12180258816 | bytes 17661952 | tf_op jit(solution)/shard_map/pallas_call | solution.py:59
  183.9 36.0 %all-gather.9.cloned.1.call-done.x_ref = bf16[8,256,1408]{2,1,0:T(8,128)(2,1)} async-done(((bf16[1,256,1408]{2,1,0:T(8,128)(2,1)}), bf16[8,256,1408]{2,1,0:T(8,128)(2,1)}) %all-gather.9.cloned.1.call-update) | async-done | bytes 5767184 | tf_op jit(solution)/shard_map/all_gather | solution.py:304
  219.9 30.8 %shard_map.166 = (bf16[8,256,1408]{2,1,0:T(8,128)(2,1)}, f32[3,528,1408]{2,1,0:T(8,128)}, f32[3,176,1408]{2,1,0:T(8,128)}) custom-call(s32[1]{0:T(128)} %bitcast.gate, bf16[8,256,1408]{2,1,0:T(8,128)(2,1)} %all-gather.9.cloned.1.call-done.x_ref, ...), custom_call_target="tpu_custom_call", output_to_operand_aliasing={{1}: (5, {}), {2}: (6, {})} | custom-call | flops 12180258816 | bytes 17661952 | tf_op jit(solution)/shard_map/pallas_call | solution.py:59
  255.5 19.9 %collective-permute-done.6 = f32[128,1408]{1,0:T(8,128)S(1)} collective-permute-done((f32[128,1408]{1,0:T(8,128)S(1)}, f32[128,1408]{1,0:T(8,128)S(1)}, u32[]{:S(2)}, u32[]{:S(2)}) %collective-permute-start.6) | collective-permute-done | bytes 720928 | tf_op jit(solution)/shard_map/ppermute | solution.py:311
  286.5 18.2 %collective-permute-done.4 = f32[128,1408]{1,0:T(8,128)} collective-permute-done((f32[128,1408]{1,0:T(8,128)S(1)}, f32[128,1408]{1,0:T(8,128)}, u32[]{:S(2)}, u32[]{:S(2)}) %collective-permute-start.4) | collective-permute-done | bytes 720928 | tf_op jit(solution)/shard_map/ppermute | solution.py:311
  304.8 22.1 %collective-permute-done.5 = f32[128,1408]{1,0:T(8,128)} collective-permute-done((f32[128,1408]{1,0:T(8,128)}, f32[128,1408]{1,0:T(8,128)}, u32[]{:S(2)}, u32[]{:S(2)}) %collective-permute-start.5) | collective-permute-done | bytes 720928 | tf_op jit(solution)/shard_map/ppermute | solution.py:311
  340.2 63.1 %all-gather.11.cloned.1.call-done.d_ref = bf16[8,2,256,1408]{3,2,1,0:T(8,128)(2,1)} async-done(((bf16[1,2,256,1408]{3,2,1,0:T(8,128)(2,1)}), bf16[8,2,256,1408]{3,2,1,0:T(8,128)(2,1)}) %all-gather.11.cloned.1.call-update) | async-done | bytes 11534352 | tf_op jit(solution)/shard_map/all_gather | solution.py:304
  403.3 20.7 %shard_map.167 = (bf16[8,256,1408]{2,1,0:T(8,128)(2,1)}, bf16[8,256,1408]{2,1,0:T(8,128)(2,1)}, bf16[8,256,768]{2,1,0:T(8,128)(2,1)}, bf16[8,256,768]{2,1,0:T(8,128)(2,1)}) custom-call(s32[1]{0:T(128)} %bitcast.gate, f32[8,256,1408]{2,1,0:T(8,128)} %bitcast.118, bf16[8,2,256,1408]{3,2,1,0:T(8,128)(2,1)} %all-gather.11.cloned.1.call-done.d_ref, ...), custom_call_target="tpu_custom_call" | custom-call | flops 13287555072 | bytes 17825792 | tf_op jit(solution)/shard_map/pallas_call | solution.py:59
  424.1 21.2 %shard_map.168 = (bf16[8,256,1408]{2,1,0:T(8,128)(2,1)}, bf16[8,256,1408]{2,1,0:T(8,128)(2,1)}, bf16[8,256,768]{2,1,0:T(8,128)(2,1)}, bf16[8,256,768]{2,1,0:T(8,128)(2,1)}) custom-call(s32[1]{0:T(128)} %bitcast.gate, f32[8,256,1408]{2,1,0:T(8,128)} %bitcast.119, bf16[8,2,256,1408]{3,2,1,0:T(8,128)(2,1)} %all-gather.11.cloned.1.call-done.d_ref, ...), custom_call_target="tpu_custom_call" | custom-call | flops 13287555072 | bytes 17825792 | tf_op jit(solution)/shard_map/pallas_call | solution.py:59
  457.6 35.5 %collective-permute-done.10 = f32[256,1408]{1,0:T(8,128)} collective-permute-done((f32[256,1408]{1,0:T(8,128)S(1)}, f32[256,1408]{1,0:T(8,128)}, u32[]{:S(2)}, u32[]{:S(2)}) %collective-permute-start.10) | collective-permute-done | bytes 1441824 | tf_op jit(solution)/shard_map/ppermute | solution.py:311
  504.2 17.8 %collective-permute-done.15 = f32[128,1408]{1,0:T(8,128)S(1)} collective-permute-done((f32[128,1408]{1,0:T(8,128)S(1)}, f32[128,1408]{1,0:T(8,128)S(1)}, u32[]{:S(2)}, u32[]{:S(2)}) %collective-permute-start.15) | collective-permute-done | bytes 720928 | tf_op jit(solution)/shard_map/ppermute | solution.py:311
  530.7 15.6 %shard_map.169 = (bf16[176,2048]{1,0:T(8,128)(2,1)}, f32[8,256,1408]{2,1,0:T(8,128)}) custom-call(s32[1]{0:T(128)} %bitcast.gate, f32[8,256,1408]{2,1,0:T(8,128)} %bitcast_dynamic-update-slice_fusion.x_ref, bf16[3,528,1408]{2,1,0:T(8,128)(2,1)} %bitcast.134), custom_call_target="tpu_custom_call" | custom-call | flops 3045064704 | bytes 12255232 | tf_op jit(solution)/shard_map/pallas_call | solution.py:59
  553.2 58.2 %all-gather.13.cloned.1.call-done.d_ref = f32[8,256,1408]{2,1,0:T(8,128)} async-done(((f32[1,256,1408]{2,1,0:T(8,128)}), f32[8,256,1408]{2,1,0:T(8,128)}) %all-gather.13.cloned.1.call-update) | async-done | bytes 11534352 | tf_op jit(solution)/shard_map/all_gather | solution.py:304
  611.4 33.0 %shard_map.170 = (bf16[8,256,1408]{2,1,0:T(8,128)(2,1)}, f32[3,528,1408]{2,1,0:T(8,128)}, f32[3,176,1408]{2,1,0:T(8,128)}, f32[8,256,1408]{2,1,0:T(8,128)}) custom-call(s32[1]{0:T(128)} %bitcast.gate, f32[8,256,1408]{2,1,0:T(8,128)} %get-tuple-element.182.x_ref, ...), custom_call_target="tpu_custom_call", output_to_operand_aliasing={{1}: (5, {}), {2}: (6, {})} | custom-call | flops 12180258816 | bytes 29196288 | tf_op jit(solution)/shard_map/pallas_call | solution.py:59
  648.2 37.5 %reduce-scatter.17.cloned.1.call-done = bf16[1,256,1408]{2,1,0:T(8,128)(2,1)} async-done(((bf16[8,256,1408]{2,1,0:T(8,128)(2,1)}), bf16[1,256,1408]{2,1,0:T(8,128)(2,1)}) %reduce-scatter.17.cloned.1.call-update) | async-done | bytes 720912 | tf_op jit(solution)/shard_map/reduce_scatter | solution.py:301
  696.9 9.0 %collective-permute-done.18 = bf16[176,1408]{1,0:T(8,128)(2,1)S(1)} collective-permute-done((bf16[176,1408]{1,0:T(8,128)(2,1)S(1)}, bf16[176,1408]{1,0:T(8,128)(2,1)S(1)}, u32[]{:S(2)}, u32[]{:S(2)}) %collective-permute-start.18) | collective-permute-done | bytes 495648 | tf_op jit(solution)/shard_map/ppermute | solution.py:311
  706.0 6.9 collective-permute-start.19
  717.9 11.0 %collective-permute-done.23 = bf16[88,1408]{1,0:T(8,128)(2,1)S(1)} collective-permute-done((bf16[88,1408]{1,0:T(8,128)(2,1)S(1)}, bf16[88,1408]{1,0:T(8,128)(2,1)S(1)}, u32[]{:S(2)}, u32[]{:S(2)}) %collective-permute-start.23) | collective-permute-done | bytes 247840 | tf_op jit(solution)/shard_map/ppermute | solution.py:311
  736.9 17.3 %shard_map.171 = f32[8,256,1408]{2,1,0:T(8,128)} custom-call(s32[1]{0:T(128)} %bitcast.gate, f32[8,256,1408]{2,1,0:T(8,128)} %bitcast.120, bf16[1408,2048]{1,0:T(8,128)(2,1)} %all-gather.15.cloned.1.call-done.h_ref, bf16[1408,1408]{1,0:T(8,128)(2,1)} %bitcast.129), custom_call_target="tpu_custom_call" | custom-call | flops 8120172544 | bytes 11534336 | tf_op jit(solution)/shard_map/pallas_call | solution.py:59
  754.3 19.2 %shard_map.172 = (f32[3,1408,768]{2,1,0:T(8,128)}, f32[3,768,1408]{2,1,0:T(8,128)}) custom-call(s32[1]{0:T(128)} %bitcast.gate, bf16[8,256,1408]{2,1,0:T(8,128)(2,1)} %get-tuple-element.147.a_ref, bf16[8,256,768]{2,1,0:T(8,128)(2,1)} %get-tuple-element.148.act_ref, ...), custom_call_target="tpu_custom_call", output_to_operand_aliasing={{0}: (5, {}), {1}: (6, {})} | custom-call | flops 8858370048 | bytes 25952256 | tf_op jit(solution)/shard_map/pallas_call | solution.py:59
  773.5 19.1 %shard_map.173 = (f32[3,1408,768]{2,1,0:T(8,128)}, f32[3,768,1408]{2,1,0:T(8,128)}) custom-call(s32[1]{0:T(128)} %bitcast.gate, bf16[8,256,1408]{2,1,0:T(8,128)(2,1)} %get-tuple-element.144.a_ref, bf16[8,256,768]{2,1,0:T(8,128)(2,1)} %get-tuple-element.145.act_ref, ...), custom_call_target="tpu_custom_call", output_to_operand_aliasing={{0}: (5, {}), {1}: (6, {})} | custom-call | flops 8858370048 | bytes 25952256 | tf_op jit(solution)/shard_map/pallas_call | solution.py:59
  792.6 9.5 %copy.72 = f32[8,256,1408]{2,1,0:T(8,128)} copy(f32[8,256,1408]{2,1,0:T(8,128)} %all-gather.17.cloned.1.call-done) | data formatting | bytes 23068672
  (138 shorter events, 118.7 us)
Async XLA Ops:
  7.2 64.4 %reduce-scatter.7.cloned.1.call-start = ((), (), s32[]{:S(2)}) async-start(), calls=%async_computation.6 | async-start | bytes 6488064 | tf_op jit(solution)/shard_map/reduce_scatter | solution.py:301
  28.6 109.3 %all-gather.7.cloned.1.call-start = ((), (), s32[]{:S(2)}) async-start(), calls=%async_computation.8 | async-start | bytes 6488064 | tf_op jit(solution)/shard_map/all_gather | solution.py:304
  76.8 102.7 %reduce-scatter.9.cloned.1.call-start = ((), (), s32[]{:S(2)}) async-start(), calls=%async_computation.7 | async-start | bytes 7208960 | tf_op jit(solution)/shard_map/reduce_scatter | solution.py:324
  121.0 98.9 %all-gather.9.cloned.1.call-start = ((), (), s32[]{:S(2)}) async-start(), calls=%async_computation.9 | async-start | bytes 6488064 | tf_op jit(solution)/shard_map/all_gather | solution.py:304
  182.7 101.9 %reduce-scatter.13.cloned.1.call-start = ((), (), s32[]{:S(2)}) async-start(), calls=%async_computation.11 | async-start | bytes 3604480 | tf_op jit(solution)/shard_map/reduce_scatter | solution.py:324
  183.4 148.7 %reduce-scatter.11.cloned.1.call-start = ((), (), s32[]{:S(2)}) async-start(), calls=%async_computation.10 | async-start | bytes 6488064 | tf_op jit(solution)/shard_map/reduce_scatter | solution.py:301
  250.7 152.6 %all-gather.11.cloned.1.call-start = ((), (), s32[]{:S(2)}) async-start(), calls=%async_computation.12 | async-start | bytes 12976128 | tf_op jit(solution)/shard_map/all_gather | solution.py:304
  254.0 21.3 %collective-permute-start.6 = (f32[128,1408]{1,0:T(8,128)S(1)}, f32[128,1408]{1,0:T(8,128)S(1)}, u32[]{:S(2)}, u32[]{:S(2)}) collective-permute-start(f32[128,1408]{1,0:T(8,128)S(1)} %get-tuple-element.169), channel_id=1, source_target_pairs={{0,6},{1,7},{2,0},{3,1},{4,2},{5,3},{6,4},{7,5},{8,14},{9,15},{10,... | collective-permute-start | bytes 2162696 | tf_op jit(solution)/shard_map/ppermute | solution.py:311
  254.6 22.6 %collective-permute-start.2 = (f32[128,1408]{1,0:T(8,128)S(1)}, f32[128,1408]{1,0:T(8,128)S(1)}, u32[]{:S(2)}, u32[]{:S(2)}) collective-permute-start(f32[128,1408]{1,0:T(8,128)S(1)} %get-tuple-element.168), channel_id=1, source_target_pairs={{0,2},{1,3},{2,4},{3,5},{4,6},{5,7},{6,0},{7,1},{8,10},{9,11},{10,... | collective-permute-start | bytes 2162696 | tf_op jit(solution)/shard_map/ppermute | solution.py:311
  278.8 26.0 %collective-permute-start.4 = (f32[128,1408]{1,0:T(8,128)S(1)}, f32[128,1408]{1,0:T(8,128)}, u32[]{:S(2)}, u32[]{:S(2)}) collective-permute-start(f32[128,1408]{1,0:T(8,128)S(1)} %get-tuple-element.171), channel_id=1, source_target_pairs={{0,2},{1,3},{2,4},{3,5},{4,6},{5,7},{6,0},{7,1},{8,10},{9,11},{10,... | collective-permute-start | bytes 2162696 | tf_op jit(solution)/shard_map/ppermute | solution.py:311
  278.9 25.8 %collective-permute-start.7 = (f32[128,1408]{1,0:T(8,128)S(1)}, f32[128,1408]{1,0:T(8,128)}, u32[]{:S(2)}, u32[]{:S(2)}) collective-permute-start(f32[128,1408]{1,0:T(8,128)S(1)} %get-tuple-element.172), channel_id=1, source_target_pairs={{0,6},{1,7},{2,0},{3,1},{4,2},{5,3},{6,4},{7,5},{8,14},{9,15},{10,... | collective-permute-start | bytes 2162696 | tf_op jit(solution)/shard_map/ppermute | solution.py:311
  281.5 45.4 %collective-permute-start.5 = (f32[128,1408]{1,0:T(8,128)}, f32[128,1408]{1,0:T(8,128)}, u32[]{:S(2)}, u32[]{:S(2)}) collective-permute-start(f32[128,1408]{1,0:T(8,128)} %get-tuple-element.167), channel_id=1, source_target_pairs={{0,6},{1,7},{2,0},{3,1},{4,2},{5,3},{6,4},{7,5},{8,14},{9,15},{10,... | collective-permute-start | bytes 2162696 | tf_op jit(solution)/shard_map/ppermute | solution.py:311
  283.1 46.1 %collective-permute-start.8 = (f32[128,1408]{1,0:T(8,128)}, f32[128,1408]{1,0:T(8,128)}, u32[]{:S(2)}, u32[]{:S(2)}) collective-permute-start(f32[128,1408]{1,0:T(8,128)} %get-tuple-element.170), channel_id=1, source_target_pairs={{0,2},{1,3},{2,4},{3,5},{4,6},{5,7},{6,0},{7,1},{8,10},{9,11},{10,... | collective-permute-start | bytes 2162696 | tf_op jit(solution)/shard_map/ppermute | solution.py:311
  340.0 206.4 %reduce-scatter.15.cloned.1.call-start = ((), (), s32[]{:S(2)}) async-start(), calls=%async_computation.13 | async-start | bytes 6488064 | tf_op jit(solution)/shard_map/reduce_scatter | solution.py:301
  445.3 166.1 %all-gather.13.cloned.1.call-start = ((), (), s32[]{:S(2)}) async-start(), calls=%async_computation.14 | async-start | bytes 12976128 | tf_op jit(solution)/shard_map/all_gather | solution.py:304
  445.6 47.5 %collective-permute-start.10 = (f32[256,1408]{1,0:T(8,128)S(1)}, f32[256,1408]{1,0:T(8,128)}, u32[]{:S(2)}, u32[]{:S(2)}) collective-permute-start(f32[256,1408]{1,0:T(8,128)S(1)} %bitcast.125), channel_id=1, source_target_pairs={{0,2},{1,3},{2,4},{3,5},{4,6},{5,7},{6,0},{7,1},{8,10},{9,11},{10,... | collective-permute-start | bytes 4325384 | tf_op jit(solution)/shard_map/ppermute | solution.py:311
  446.3 50.0 %collective-permute-start.12 = (f32[256,1408]{1,0:T(8,128)S(1)}, f32[256,1408]{1,0:T(8,128)S(1)}, u32[]{:S(2)}, u32[]{:S(2)}) collective-permute-start(f32[256,1408]{1,0:T(8,128)S(1)} %bitcast.126), channel_id=1, source_target_pairs={{0,6},{1,7},{2,0},{3,1},{4,2},{5,3},{6,4},{7,5},{8,14},{9,15},{10,... | collective-permute-start | bytes 4325384 | tf_op jit(solution)/shard_map/ppermute | solution.py:311
  448.4 50.7 %collective-permute-start.9 = (f32[256,1408]{1,0:T(8,128)S(1)}, f32[256,1408]{1,0:T(8,128)}, u32[]{:S(2)}, u32[]{:S(2)}) collective-permute-start(f32[256,1408]{1,0:T(8,128)S(1)} %bitcast.127), channel_id=1, source_target_pairs={{0,1},{1,0},{2,3},{3,2},{4,5},{5,4},{6,7},{7,6},{8,9},{9,8},{10,11... | collective-permute-start | bytes 4325384 | tf_op jit(solution)/shard_map/ppermute | solution.py:314
  494.3 30.4 %collective-permute-start.11 = (f32[256,1408]{1,0:T(8,128)}, f32[256,1408]{1,0:T(8,128)S(1)}, u32[]{:S(2)}, u32[]{:S(2)}) collective-permute-start(f32[256,1408]{1,0:T(8,128)} %collective-permute-done.10), channel_id=1, source_target_pairs={{0,1},{1,0},{2,3},{3,2},{4,5},{5,4},{6,7},{7,6},{8,9},{9,8},{10,11... | collective-permute-start | bytes 4325384 | tf_op jit(solution)/shard_map/ppermute | solution.py:314
  496.3 28.4 %collective-permute-start.13 = (f32[256,1408]{1,0:T(8,128)S(1)}, f32[256,1408]{1,0:T(8,128)S(1)}, u32[]{:S(2)}, u32[]{:S(2)}) collective-permute-start(f32[256,1408]{1,0:T(8,128)S(1)} %collective-permute-done.12), channel_id=1, source_target_pairs={{0,1},{1,0},{2,3},{3,2},{4,5},{5,4},{6,7},{7,6},{8,9},{9,8},{10,11... | collective-permute-start | bytes 4325384 | tf_op jit(solution)/shard_map/ppermute | solution.py:314
  496.4 25.6 %collective-permute-start.15 = (f32[128,1408]{1,0:T(8,128)S(1)}, f32[128,1408]{1,0:T(8,128)S(1)}, u32[]{:S(2)}, u32[]{:S(2)}) collective-permute-start(f32[128,1408]{1,0:T(8,128)S(1)} %slice.65), channel_id=1, source_target_pairs={{0,6},{1,7},{2,0},{3,1},{4,2},{5,3},{6,4},{7,5},{8,14},{9,15},{10,... | collective-permute-start | bytes 2162696 | tf_op jit(solution)/shard_map/ppermute | solution.py:311
  499.0 24.7 %collective-permute-start.14 = (f32[128,1408]{1,0:T(8,128)S(1)}, f32[128,1408]{1,0:T(8,128)S(1)}, u32[]{:S(2)}, u32[]{:S(2)}) collective-permute-start(f32[128,1408]{1,0:T(8,128)S(1)} %slice.64), channel_id=1, source_target_pairs={{0,2},{1,3},{2,4},{3,5},{4,6},{5,7},{6,0},{7,1},{8,10},{9,11},{10,... | collective-permute-start | bytes 2162696 | tf_op jit(solution)/shard_map/ppermute | solution.py:311
  552.5 95.3 %all-gather.15.cloned.1.call-start = ((), (), s32[]{:S(2)}) async-start(), calls=%async_computation.15 | async-start | bytes 6488064 | tf_op jit(solution)/shard_map/all_gather | solution.py:304
  553.2 132.5 %reduce-scatter.17.cloned.1.call-start = ((), (), s32[]{:S(2)}) async-start(), calls=%async_computation.16 | async-start | bytes 6488064 | tf_op jit(solution)/shard_map/reduce_scatter | solution.py:301
  647.8 144.8 %all-gather.17.cloned.1.call-start = ((), (), s32[]{:S(2)}) async-start(), calls=%async_computation.17 | async-start | bytes 12976128 | tf_op jit(solution)/shard_map/all_gather | solution.py:304
  690.9 15.0 %collective-permute-start.18 = (bf16[176,1408]{1,0:T(8,128)(2,1)S(1)}, bf16[176,1408]{1,0:T(8,128)(2,1)S(1)}, u32[]{:S(2)}, u32[]{:S(2)}) collective-permute-start(bf16[176,1408]{1,0:T(8,128)(2,1)S(1)} %bitcast.136), channel_id=1, source_target_pairs={{0,2},{1,3},{2,4},{3,5},{4,6},{5,7},{6,0},{7,1},{8,10},{9,11},{10,... | collective-permute-start | bytes 1486856 | tf_op jit(solution)/shard_map/ppermute | solution.py:311
  691.9 21.0 %collective-permute-start.20 = (bf16[176,1408]{1,0:T(8,128)(2,1)S(1)}, bf16[176,1408]{1,0:T(8,128)(2,1)S(1)}, u32[]{:S(2)}, u32[]{:S(2)}) collective-permute-start(bf16[176,1408]{1,0:T(8,128)(2,1)S(1)} %bitcast.137), channel_id=1, source_target_pairs={{0,6},{1,7},{2,0},{3,1},{4,2},{5,3},{6,4},{7,5},{8,14},{9,15},{10,... | collective-permute-start | bytes 1486856 | tf_op jit(solution)/shard_map/ppermute | solution.py:311
  694.4 23.4 %collective-permute-start.17 = (bf16[176,1408]{1,0:T(8,128)(2,1)S(1)}, bf16[176,1408]{1,0:T(8,128)(2,1)S(1)}, u32[]{:S(2)}, u32[]{:S(2)}) collective-permute-start(bf16[176,1408]{1,0:T(8,128)(2,1)S(1)} %bitcast.138), channel_id=1, source_target_pairs={{0,1},{1,0},{2,3},{3,2},{4,5},{5,4},{6,7},{7,6},{8,9},{9,8},{10,11... | collective-permute-start | bytes 1486856 | tf_op jit(solution)/shard_map/ppermute | solution.py:314
  706.0 27.5 %collective-permute-start.19 = (bf16[176,1408]{1,0:T(8,128)(2,1)S(1)}, bf16[176,1408]{1,0:T(8,128)(2,1)S(1)}, u32[]{:S(2)}, u32[]{:S(2)}) collective-permute-start(bf16[176,1408]{1,0:T(8,128)(2,1)S(1)} %collective-permute-done.18), channel_id=1, source_target_pairs={{0,1},{1,0},{2,3},{3,2},{4,5},{5,4},{6,7},{7,6},{8,9},{9,8},{10,11... | collective-permute-start | bytes 1486856 | tf_op jit(solution)/shard_map/ppermute | solution.py:314
  712.9 20.5 %collective-permute-start.21 = (bf16[176,1408]{1,0:T(8,128)(2,1)S(1)}, bf16[176,1408]{1,0:T(8,128)(2,1)S(1)}, u32[]{:S(2)}, u32[]{:S(2)}) collective-permute-start(bf16[176,1408]{1,0:T(8,128)(2,1)S(1)} %collective-permute-done.20), channel_id=1, source_target_pairs={{0,1},{1,0},{2,3},{3,2},{4,5},{5,4},{6,7},{7,6},{8,9},{9,8},{10,11... | collective-permute-start | bytes 1486856 | tf_op jit(solution)/shard_map/ppermute | solution.py:314
  714.4 14.5 %collective-permute-start.23 = (bf16[88,1408]{1,0:T(8,128)(2,1)S(1)}, bf16[88,1408]{1,0:T(8,128)(2,1)S(1)}, u32[]{:S(2)}, u32[]{:S(2)}) collective-permute-start(bf16[88,1408]{1,0:T(8,128)(2,1)S(1)} %slice.68), channel_id=1, source_target_pairs={{0,6},{1,7},{2,0},{3,1},{4,2},{5,3},{6,4},{7,5},{8,14},{9,15},{10,... | collective-permute-start | bytes 743432 | tf_op jit(solution)/shard_map/ppermute | solution.py:311
  717.8 14.5 %collective-permute-start.22 = (bf16[88,1408]{1,0:T(8,128)(2,1)S(1)}, bf16[88,1408]{1,0:T(8,128)(2,1)S(1)}, u32[]{:S(2)}, u32[]{:S(2)}) collective-permute-start(bf16[88,1408]{1,0:T(8,128)(2,1)S(1)} %slice.67), channel_id=1, source_target_pairs={{0,2},{1,3},{2,4},{3,5},{4,6},{5,7},{6,0},{7,1},{8,10},{9,11},{10,... | collective-permute-start | bytes 743432 | tf_op jit(solution)/shard_map/ppermute | solution.py:311
  (9 other events, 101.2 us)
Sparse Core Ops, SparseCore 0:
  28.7 38.3 reduce-scatter.6
  77.0 37.1 all-gather.6
  121.1 57.6 reduce-scatter.8
  182.8 37.0 all-gather.8
  222.6 31.5 reduce-scatter.12
  257.0 75.0 reduce-scatter.10
  340.1 63.2 all-gather.10
  445.5 77.4 reduce-scatter.14
  552.6 58.7 all-gather.12
  612.9 34.8 all-gather.14
  650.7 34.9 reduce-scatter.16
  690.0 69.8 all-gather.16

commit v6 on v5

--- a/solution.py
+++ b/solution.py
@@ -96,22 +96,62 @@
     return hidden * cdf, bent, cdf, root, square
 
 
-def mlp_forward(plan, state, w_in, w_out, layer):
+def gelu_slope(hidden):
+    act, bent, cdf, root, square = gelu_parts(hidden)
+    return act.astype(BF16), cdf + 0.5 * hidden * (1.0 - bent * bent) * (root * (1.0 + 3.0 * 0.044715 * square))
+
+
+def mlp_forward(plan, state, w_in, w_out, layer, want_out=True, keep=False):
     n_seq, rows, width = state.shape
     ff = w_in.shape[-1]
 
-    def body(gate, x_ref, win_ref, wout_ref, out_ref):
-        act = gelu_parts(dot(rms_bf(flat(x_ref)), win_ref[...], 1, 0))[0].astype(BF16)
-        put(out_ref, dot(act, wout_ref[...], 1, 0))
-
+    def body(gate, x_ref, win_ref, *refs):
+        normed = rms_bf(flat(x_ref))
+        hidden = dot(normed, win_ref[...], 1, 0)
+        if keep:
+            act, slope = gelu_slope(hidden)
+            for ref, value in zip(refs[-3:], (normed, act, slope)):
+                put(ref, value)
+        else:
+            act = gelu_parts(hidden)[0].astype(BF16)
+        if want_out:
+            put(refs[1], dot(act, refs[0][...], 1, 0))
+
+    out_shape = [jax.ShapeDtypeStruct(state.shape, F32)] if want_out else []
+    if keep:
+        out_shape += [jax.ShapeDtypeStruct((n_seq, rows, n), t) for n, t in ((width, BF16), (ff, BF16), (ff, F32))]
+    in_specs = [plan.seqs(state), plan.layer(layer, width, ff)] + [plan.layer(layer, ff, width)] * want_out
     return plan.call(
         body,
-        [plan.seqs(state), plan.layer(layer, width, ff), plan.layer(layer, ff, width)],
-        [plan.seqs(state)],
-        [jax.ShapeDtypeStruct(state.shape, F32)],
-        (state, w_in, w_out),
-        4 * n_seq * rows * width * ff,
-    )[0]
+        in_specs,
+        [plan.seqs(x) for x in out_shape],
+        out_shape,
+        [state, w_in] + [w_out] * want_out,
+        (2 + 2 * want_out) * n_seq * rows * width * ff,
+    )
+
+
+def mlp_back_kept(plan, slope, d_out, slot, w_in, w_out, layer, extra=None):
+    n_seq, rows, ff = slope.shape
+    width = w_in.shape[1]
+    n_e = 0 if extra is None else 1
+
+    def body(gate, slope_ref, d_ref, win_ref, wout_ref, *refs):
+        dx_ref, dh_ref = refs[n_e:]
+        d_hidden = (flat(slope_ref) * dot(flat(d_ref), wout_ref[...], 1, 1)).astype(BF16)
+        d_x = dot(d_hidden, win_ref[...], 1, 1)
+        if n_e:
+            d_x = d_x + flat(refs[0]).astype(F32)
+        put(dx_ref, d_x)
+        put(dh_ref, d_hidden)
+
+    in_specs = [plan.seqs(slope), plan.seqs(d_out, slot), plan.layer(layer, width, ff), plan.layer(layer, ff, width)]
+    args = [slope, d_out, w_in, w_out]
+    if n_e:
+        in_specs.append(plan.seqs(extra))
+        args.append(extra)
+    out_shape = [jax.ShapeDtypeStruct((n_seq, rows, width), BF16), jax.ShapeDtypeStruct((n_seq, rows, ff), BF16)]
+    return plan.call(body, in_specs, [plan.seqs(x) for x in out_shape], out_shape, args, 4 * n_seq * rows * width * ff)
 
 
 def mlp_back(plan, state, d_out, slot, w_in, w_out, layer, extra=None):
@@ -372,9 +412,9 @@
         top = n_layers - 1
         dx, parts = mlp_back(plan, y_one, dy_two, None, w_in, w_out, top)
         g_back = scatter(dx)
-        g_part = mlp_forward(plan.after(dx), y_one, w_in, w_out, top)
+        (g_part,) = mlp_forward(plan.after(dx), y_one, w_in, w_out, top)
         g_sums = core_sums(g_part)
-        d_one = own(dy_one) + rms_pull(own(y_one), later(g_back, g_sums).astype(F32))
+        d_one = own(dy_one) + rms_pull(own(y_one), later(g_back, g_part).astype(F32))
         d_shard = d_one.astype(BF16)
         mlp_held = mlp_grads(plan.after(d_shard), parts, dy_two, None, top, n_layers, None)
         g_sum = like_scatter(later(g_sums, d_shard))
@@ -385,7 +425,7 @@
         for layer_pair in reversed(range(n_pairs)):
             s_one, s_two = saved_one[layer_pair], saved_two[layer_pair]
             mid, low = 2 * layer_pair + 1, 2 * layer_pair
-            g_part = mlp_forward(plan.after(last), s_one, w_in, w_out, low)
+            g_part, normed, low_act, low_slope = mlp_forward(plan.after(last), s_one, w_in, w_out, low, keep=True)
             d_one_bf = gather(d_shard, g_part)
             finish, chip_sums = ring_scatter(g_part)
             mid_back, attn_held, _ = attn_back(
@@ -396,6 +436,8 @@
             f_shard = rms_bf(x_two_shard)
             f_in = gather(f_shard)
             mid_sum = like_scatter(later(mid_sums, f_shard))
+            _, mid_act, mid_slope = mlp_forward(plan.after(f_shard), s_one, w_in, w_out, mid, want_out=False, keep=True)
+            f_in = later(f_in, mid_slope)
             f_back, attn_held, _ = attn_back(
                 plan, f_in, d_one_bf, w_t, w_o2, mid + 1, n_heads, n_layers, attn_held
             )
@@ -403,25 +445,25 @@
             mid_two = d_two + rms_pull(x_two_shard, scatter(f_back).astype(F32))
             d_two = mid_two + rms_pull(own(s_two), later(mid_sum, f_back).astype(F32))
             both_d = gather(jnp.stack([mid_two.astype(BF16), d_two.astype(BF16)], axis=1))
-            dx, mid_parts = mlp_back(plan, s_one, both_d, 0, w_in, w_out, mid)
-            mid_dx = dx
-            dx, low_parts = mlp_back(plan, s_one, both_d, 1, w_in, w_out, low, dx)
-            x_two = ring_gather(later(low_two[0], both_d), (mid_dx,), (dx,))
-            heads, x_two = attn_forward(plan, x_two, w_t, low, n_heads)
+            dx, mid_dh = mlp_back_kept(plan, mid_slope, both_d, 0, w_in, w_out, mid)
+            dx, low_dh = mlp_back_kept(plan, low_slope, both_d, 1, w_in, w_out, low, dx)
+            dx_sum = scatter(dx)
+            mid_parts, low_parts = (normed, mid_act, mid_dh), (normed, low_act, low_dh)
+            mlp_held = mlp_grads(plan.after(dx), mid_parts, both_d, 0, mid, n_layers, mlp_held)
+            x_two = ring_gather(later(low_two[0], both_d), (dx,), (mlp_held[0],))
             x_two_shard = low_two
-            d_one = d_one + rms_pull(own(s_one), later(scatter(dx), heads).astype(F32))
+            d_one = d_one + rms_pull(own(s_one), later(dx_sum, mlp_held[0]).astype(F32))
+            heads, x_two = attn_forward(plan.after(d_one), x_two, w_t, low, n_heads)
             if layer_pair:
                 d_shard, last = d_one.astype(BF16), dx
                 g_sum, x_two_out = jnp.zeros_like(x_two_shard), x_two_shard
-                mlp_held = mlp_grads(plan, mid_parts, both_d, 0, mid, n_layers, mlp_held)
                 mlp_held = mlp_grads(plan, low_parts, both_d, 1, low, n_layers, mlp_held)
         f_back, attn_held, d_one_full = attn_back(
-            plan, x_two, gather(d_one), w_t, w_o2, 0, n_heads, n_layers, attn_held, True
+            plan, x_two, gather(d_one, heads), w_t, w_o2, 0, n_heads, n_layers, attn_held, True
         )
         heads_all = gather(later(heads, d_one), f_back)
         d_two = d_two + rms_pull(x_two_shard, scatter(later(f_back, heads_all)).astype(F32))
         tail = plan.after(f_back)
-        mlp_held = mlp_grads(tail, mid_parts, both_d, 0, 1, n_layers, mlp_held)
         mlp_held = mlp_grads(tail, low_parts, both_d, 1, 0, n_layers, mlp_held)
         x_one = project_out(tail, s_one, heads_all, wo_all)
         d_two_full = gather(d_two, x_one, mlp_held[0])

time: 817 us -> 792 us (0.969)
  waiting for transfers between devices: 366 us -> 322 us
  starting transfers between devices: 36.8 us -> 46.5 us
  Pallas kernels: 286 us -> 295 us
    all_gather x6, waiting for transfers between devices: 161 us -> 86.1 us  [gather(): return later(lax.all_gather(shard, 'tp', axis=0, tiled=True), *others)]
    reduce_scatter x4, waiting for transfers between devices: 38.1 us -> 70.8 us  [scatter(): return lax.psum_scatter(part, 'tp', scatter_dimension=0, tiled=True)]
    ppermute x11, waiting for transfers between devices: 24.7 us -> 8.26 us  [swap(): lax.ppermute(value, 'tp', [(i, i + 1 - 2 * (i % CORES)) for i in range(n_...]
    ppermute x14, waiting for transfers between devices: 141 us -> 153 us  [shift(): return lax.ppermute(value, 'tp', pairs)]
    pallas_call x13 -> x14, Pallas kernels: 286 us -> 295 us  [call(): pl.pallas_call(body, grid_spec=pltpu.PrefetchScalarGridSpec(num_scalar_pr...]
  transfers between devices with their start and end apart: 37 -> 37, of which waited for: 20 -> 20; matrix products, arithmetic and copies ran while one was open for 8% -> 9% of each run, Pallas kernels for 28% -> 30%
where the time goes in v6:
time: 792 us; the launch traced here: 786 us
  waiting for transfers between devices  322 us (41%)
  Pallas kernels  295 us (37%)
  other arithmetic  57.2 us (7%)
  local copies, waits for them, and re-layouts  49.8 us (6%)
  starting transfers between devices  46.5 us (6%)
  between operations  15 us (2%)
    pallas_call x14, Pallas kernels, call(): pl.pallas_call(body, grid_spec=pltpu.PrefetchScalarGridSpec(num_scalar_pr...  295 us
    ppermute x14, waiting for transfers between devices, shift(): return lax.ppermute(value, 'tp', pairs)  153 us
    all_gather x6, waiting for transfers between devices, gather(): return later(lax.all_gather(shard, 'tp', axis=0, tiled=True), *others)  86.1 us
    reduce_scatter x4, waiting for transfers between devices, scatter(): return lax.psum_scatter(part, 'tp', scatter_dimension=0, tiled=True)  70.8 us
    ppermute x11, starting transfers between devices, swap(): lax.ppermute(value, 'tp', [(i, i + 1 - 2 * (i % CORES)) for i in range(n_...  24.5 us
    ppermute x14, starting transfers between devices, shift(): return lax.ppermute(value, 'tp', pairs)  19.6 us
    add x2, other arithmetic, core_sums(): lax.dynamic_index_in_dim(split, core, 1, False).astype(F32)  15.9 us
  transfers between devices with their start and end apart: 37, of which 20 were waited for; matrix products, arithmetic and copies ran while one was open for 9% of the time, Pallas kernels for 30%

profile of v6, /device:TPU:113, one launch (start us, length us, event | category | flops | bytes accessed | tf_op | source)
XLA Modules:
  0.0 785.7 jit_solution(8638593317211836105)
XLA Ops:
  7.3 21.3 %shard_map.161 = (bf16[8,256,1408]{2,1,0:T(8,128)(2,1)}, bf16[8,256,1408]{2,1,0:T(8,128)(2,1)}, bf16[8,256,768]{2,1,0:T(8,128)(2,1)}, bf16[8,256,768]{2,1,0:T(8,128)(2,1)}) custom-call(s32[1]{0:T(128)} %bitcast.gate, f32[8,256,1408]{2,1,0:T(8,128)} %x_ref.3, f32[8,256,1408]{2,1,0:T(8,128)} %d_ref.3, bf16[3,1408,768]{2,1,0:T(8,128)(2,1)} %win_ref.11, ...), custom_call_target="tpu_custom_call" | custom-call | flops 13287555072 | bytes 17825792 | tf_op jit(solution)/shard_map/pallas_call | solution.py:59
  30.2 18.2 %shard_map.162 = f32[8,256,1408]{2,1,0:T(8,128)} custom-call(s32[1]{0:T(128)} %bitcast.gate, f32[8,256,1408]{2,1,0:T(8,128)} %x_ref.3, bf16[3,1408,768]{2,1,0:T(8,128)(2,1)} %win_ref.11, bf16[3,768,1408]{2,1,0:T(8,128)(2,1)} %wout_ref.5), custom_call_target="tpu_custom_call" | custom-call | flops 8858370048 | bytes 11534336 | tf_op jit(solution)/shard_map/pallas_call | solution.py:59
  48.5 18.6 %reduce-scatter.7.cloned.1.call-done = bf16[1,256,1408]{2,1,0:T(8,128)(2,1)} async-done(((bf16[8,256,1408]{2,1,0:T(8,128)(2,1)}), bf16[1,256,1408]{2,1,0:T(8,128)(2,1)}) %reduce-scatter.7.cloned.1.call-update) | async-done | bytes 720912 | tf_op jit(solution)/shard_map/reduce_scatter | solution.py:341
  80.6 19.8 %shard_map.163 = (f32[3,1408,768]{2,1,0:T(8,128)}, f32[3,768,1408]{2,1,0:T(8,128)}) custom-call(s32[1]{0:T(128)} %bitcast.gate, bf16[8,256,1408]{2,1,0:T(8,128)(2,1)} %get-tuple-element.94.a_ref, bf16[8,256,768]{2,1,0:T(8,128)(2,1)} %get-tuple-element.95.act_ref, bf16[8,256,768]{2,1,0:T(8,128)(2,1)} %get-tuple-element.96.dh_ref, f32[8,256,1408]{2,1,0:T(8,128)} %d_ref.3), custom_call_target="tpu_custom_call" | custom-call | flops 8858370048 | bytes 25952256 | tf_op jit(solution)/shard_map/pallas_call | solution.py:59
  100.4 20.2 %shard_map.164 = (f32[8,256,1408]{2,1,0:T(8,128)}, bf16[8,256,1408]{2,1,0:T(8,128)(2,1)}, bf16[8,256,768]{2,1,0:T(8,128)(2,1)}, f32[8,256,768]{2,1,0:T(8,128)}) custom-call(s32[1]{0:T(128)} %bitcast.gate, f32[8,256,1408]{2,1,0:T(8,128)} %bitcast.117, bf16[3,1408,768]{2,1,0:T(8,128)(2,1)} %win_ref.11, bf16[3,768,1408]{2,1,0:T(8,128)(2,1)} %wout_ref.5), custom_call_target="tpu_custom_call" | custom-call | flops 8858370048 | bytes 26738688 | tf_op jit(solution)/shard_map/pallas_call | solution.py:59
  126.4 7.4 bitcast_add_fusion
  135.9 8.5 %bitcast_add_fusion.1 = f32[4,256,1408]{2,1,0:T(8,128)} fusion(f32[4,256,1408]{2,1,0:T(8,128)} %collective-permute-done.1, f32[4,2,256,1408]{3,2,1,0:T(8,128)} %bitcast.128, s32[]{:T(128)S(6)} %select_n.67), kind=kLoop, calls=%fused_computation.1 | loop fusion | flops 1441792 | bytes 17301508 | tf_op jit(solution)/shard_map/add | solution.py:360
  144.4 31.8 %shard_map.165 = (bf16[8,256,1408]{2,1,0:T(8,128)(2,1)}, f32[3,528,1408]{2,1,0:T(8,128)}, f32[3,176,1408]{2,1,0:T(8,128)}) custom-call(s32[1]{0:T(128)} %bitcast.gate, f32[8,256,1408]{2,1,0:T(8,128)} %bitcast.139, bf16[8,256,1408]{2,1,0:T(8,128)(2,1)} %all-gather.7.cloned.1.call-done.d_ref, bf16[3,528,1408]{2,1,0:T(8,128)(2,1)} %bitcast.131, ...), custom_call_target="tpu_custom_call" | custom-call | flops 12180258816 | bytes 17661952 | tf_op jit(solution)/shard_map/pallas_call | solution.py:59
  193.6 14.0 %shard_map.166 = (bf16[8,256,1408]{2,1,0:T(8,128)(2,1)}, bf16[8,256,768]{2,1,0:T(8,128)(2,1)}, f32[8,256,768]{2,1,0:T(8,128)}) custom-call(s32[1]{0:T(128)} %bitcast.gate, f32[8,256,1408]{2,1,0:T(8,128)} %bitcast.118, bf16[3,1408,768]{2,1,0:T(8,128)(2,1)} %win_ref.11), custom_call_target="tpu_custom_call" | custom-call | flops 4429185024 | bytes 15204352 | tf_op jit(solution)/shard_map/pallas_call | solution.py:59
  207.6 19.7 %all-gather.9.cloned.1.call-done.x_ref = bf16[8,256,1408]{2,1,0:T(8,128)(2,1)} async-done(((bf16[1,256,1408]{2,1,0:T(8,128)(2,1)}), bf16[8,256,1408]{2,1,0:T(8,128)(2,1)}) %all-gather.9.cloned.1.call-update) | async-done | bytes 5767184 | tf_op jit(solution)/shard_map/all_gather | solution.py:344
  227.3 30.8 %shard_map.167 = (bf16[8,256,1408]{2,1,0:T(8,128)(2,1)}, f32[3,528,1408]{2,1,0:T(8,128)}, f32[3,176,1408]{2,1,0:T(8,128)}) custom-call(s32[1]{0:T(128)} %bitcast.gate, bf16[8,256,1408]{2,1,0:T(8,128)(2,1)} %all-gather.9.cloned.1.call-done.x_ref, ...), custom_call_target="tpu_custom_call", output_to_operand_aliasing={{1}: (5, {}), {2}: (6, {})} | custom-call | flops 12180258816 | bytes 17661952 | tf_op jit(solution)/shard_map/pallas_call | solution.py:59
  262.9 20.2 %collective-permute-done.6 = f32[128,1408]{1,0:T(8,128)S(1)} collective-permute-done((f32[128,1408]{1,0:T(8,128)S(1)}, f32[128,1408]{1,0:T(8,128)S(1)}, u32[]{:S(2)}, u32[]{:S(2)}) %collective-permute-start.6) | collective-permute-done | bytes 720928 | tf_op jit(solution)/shard_map/ppermute | solution.py:351
  294.5 18.2 %collective-permute-done.4 = f32[128,1408]{1,0:T(8,128)} collective-permute-done((f32[128,1408]{1,0:T(8,128)S(1)}, f32[128,1408]{1,0:T(8,128)}, u32[]{:S(2)}, u32[]{:S(2)}) %collective-permute-start.4) | collective-permute-done | bytes 720928 | tf_op jit(solution)/shard_map/ppermute | solution.py:351
  312.6 22.2 %collective-permute-done.5 = f32[128,1408]{1,0:T(8,128)} collective-permute-done((f32[128,1408]{1,0:T(8,128)}, f32[128,1408]{1,0:T(8,128)}, u32[]{:S(2)}, u32[]{:S(2)}) %collective-permute-start.5) | collective-permute-done | bytes 720928 | tf_op jit(solution)/shard_map/ppermute | solution.py:351
  347.7 63.6 %all-gather.11.cloned.1.call-done.d_ref = bf16[8,2,256,1408]{3,2,1,0:T(8,128)(2,1)} async-done(((bf16[1,2,256,1408]{3,2,1,0:T(8,128)(2,1)}), bf16[8,2,256,1408]{3,2,1,0:T(8,128)(2,1)}) %all-gather.11.cloned.1.call-update) | async-done | bytes 11534352 | tf_op jit(solution)/shard_map/all_gather | solution.py:344
  411.3 17.0 %shard_map.168 = (bf16[8,256,1408]{2,1,0:T(8,128)(2,1)}, bf16[8,256,768]{2,1,0:T(8,128)(2,1)}) custom-call(s32[1]{0:T(128)} %bitcast.gate, f32[8,256,768]{2,1,0:T(8,128)} %get-tuple-element.107.slope_ref, bf16[8,2,256,1408]{3,2,1,0:T(8,128)(2,1)} %all-gather.11.cloned.1.call-done.d_ref, bf16[3,1408,768]{2,1,0:T(8,128)(2,1)} %win_ref.11, ...), custom_call_target="tpu_custom_call" | custom-call | flops 8858370048 | bytes 8912896 | tf_op jit(solution)/shard_map/pallas_call | solution.py:59
  428.3 17.5 %shard_map.169 = (bf16[8,256,1408]{2,1,0:T(8,128)(2,1)}, bf16[8,256,768]{2,1,0:T(8,128)(2,1)}) custom-call(s32[1]{0:T(128)} %bitcast.gate, f32[8,256,768]{2,1,0:T(8,128)} %get-tuple-element.99.slope_ref, bf16[8,2,256,1408]{3,2,1,0:T(8,128)(2,1)} %all-gather.11.cloned.1.call-done.d_ref, bf16[3,1408,768]{2,1,0:T(8,128)(2,1)} %win_ref.11, ...), custom_call_target="tpu_custom_call" | custom-call | flops 8858370048 | bytes 8912896 | tf_op jit(solution)/shard_map/pallas_call | solution.py:59
  447.5 19.2 %shard_map.170 = (f32[3,1408,768]{2,1,0:T(8,128)}, f32[3,768,1408]{2,1,0:T(8,128)}) custom-call(s32[1]{0:T(128)} %bitcast.gate, bf16[8,256,1408]{2,1,0:T(8,128)(2,1)} %get-tuple-element.117.a_ref, bf16[8,256,768]{2,1,0:T(8,128)(2,1)} %get-tuple-element.118.act_ref, ...), custom_call_target="tpu_custom_call", output_to_operand_aliasing={{0}: (5, {}), {1}: (6, {})} | custom-call | flops 8858370048 | bytes 25952256 | tf_op jit(solution)/shard_map/pallas_call | solution.py:59
  466.7 14.6 %reduce-scatter.15.cloned.1.call-done = bf16[1,256,1408]{2,1,0:T(8,128)(2,1)} async-done(((bf16[8,256,1408]{2,1,0:T(8,128)(2,1)}), bf16[1,256,1408]{2,1,0:T(8,128)(2,1)}) %reduce-scatter.15.cloned.1.call-update) | async-done | bytes 720912 | tf_op jit(solution)/shard_map/reduce_scatter | solution.py:341
  493.4 6.2 broadcast_in_dim.66
  500.9 41.6 %collective-permute-done.10 = f32[256,1408]{1,0:T(8,128)} collective-permute-done((f32[256,1408]{1,0:T(8,128)S(1)}, f32[256,1408]{1,0:T(8,128)}, u32[]{:S(2)}, u32[]{:S(2)}) %collective-permute-start.10) | collective-permute-done | bytes 1441824 | tf_op jit(solution)/shard_map/ppermute | solution.py:351
  543.7 7.1 collective-permute-start.11
  559.7 24.6 %collective-permute-done.15 = f32[128,1408]{1,0:T(8,128)S(1)} collective-permute-done((f32[128,1408]{1,0:T(8,128)S(1)}, f32[128,1408]{1,0:T(8,128)S(1)}, u32[]{:S(2)}, u32[]{:S(2)}) %collective-permute-start.15) | collective-permute-done | bytes 720928 | tf_op jit(solution)/shard_map/ppermute | solution.py:351
  591.6 15.6 %shard_map.171 = (bf16[176,2048]{1,0:T(8,128)(2,1)}, f32[8,256,1408]{2,1,0:T(8,128)}) custom-call(s32[1]{0:T(128)} %bitcast.gate, f32[8,256,1408]{2,1,0:T(8,128)} %bitcast_dynamic-update-slice_fusion.x_ref, bf16[3,528,1408]{2,1,0:T(8,128)(2,1)} %bitcast.133), custom_call_target="tpu_custom_call" | custom-call | flops 3045064704 | bytes 12255232 | tf_op jit(solution)/shard_map/pallas_call | solution.py:59
  607.4 33.0 %shard_map.172 = (bf16[8,256,1408]{2,1,0:T(8,128)(2,1)}, f32[3,528,1408]{2,1,0:T(8,128)}, f32[3,176,1408]{2,1,0:T(8,128)}, f32[8,256,1408]{2,1,0:T(8,128)}) custom-call(s32[1]{0:T(128)} %bitcast.gate, f32[8,256,1408]{2,1,0:T(8,128)} %get-tuple-element.196.x_ref, ...), custom_call_target="tpu_custom_call", output_to_operand_aliasing={{1}: (5, {}), {2}: (6, {})} | custom-call | flops 12180258816 | bytes 29196288 | tf_op jit(solution)/shard_map/pallas_call | solution.py:59
  643.6 37.5 %reduce-scatter.17.cloned.1.call-done = bf16[1,256,1408]{2,1,0:T(8,128)(2,1)} async-done(((bf16[8,256,1408]{2,1,0:T(8,128)(2,1)}), bf16[1,256,1408]{2,1,0:T(8,128)(2,1)}) %reduce-scatter.17.cloned.1.call-update) | async-done | bytes 720912 | tf_op jit(solution)/shard_map/reduce_scatter | solution.py:341
  692.3 9.0 %collective-permute-done.18 = bf16[176,1408]{1,0:T(8,128)(2,1)S(1)} collective-permute-done((bf16[176,1408]{1,0:T(8,128)(2,1)S(1)}, bf16[176,1408]{1,0:T(8,128)(2,1)S(1)}, u32[]{:S(2)}, u32[]{:S(2)}) %collective-permute-start.18) | collective-permute-done | bytes 495648 | tf_op jit(solution)/shard_map/ppermute | solution.py:351
  701.3 7.0 collective-permute-start.19
  713.3 11.0 %collective-permute-done.23 = bf16[88,1408]{1,0:T(8,128)(2,1)S(1)} collective-permute-done((bf16[88,1408]{1,0:T(8,128)(2,1)S(1)}, bf16[88,1408]{1,0:T(8,128)(2,1)S(1)}, u32[]{:S(2)}, u32[]{:S(2)}) %collective-permute-start.23) | collective-permute-done | bytes 247840 | tf_op jit(solution)/shard_map/ppermute | solution.py:351
  732.3 17.3 %shard_map.173 = f32[8,256,1408]{2,1,0:T(8,128)} custom-call(s32[1]{0:T(128)} %bitcast.gate, f32[8,256,1408]{2,1,0:T(8,128)} %bitcast.119, bf16[1408,2048]{1,0:T(8,128)(2,1)} %all-gather.15.cloned.1.call-done.h_ref, bf16[1408,1408]{1,0:T(8,128)(2,1)} %bitcast.126), custom_call_target="tpu_custom_call" | custom-call | flops 8120172544 | bytes 11534336 | tf_op jit(solution)/shard_map/pallas_call | solution.py:59
  749.6 19.2 %shard_map.174 = (f32[3,1408,768]{2,1,0:T(8,128)}, f32[3,768,1408]{2,1,0:T(8,128)}) custom-call(s32[1]{0:T(128)} %bitcast.gate, bf16[8,256,1408]{2,1,0:T(8,128)(2,1)} %get-tuple-element.117.a_ref, bf16[8,256,768]{2,1,0:T(8,128)(2,1)} %get-tuple-element.164.act_ref, ...), custom_call_target="tpu_custom_call", output_to_operand_aliasing={{0}: (5, {}), {1}: (6, {})} | custom-call | flops 8858370048 | bytes 25952256 | tf_op jit(solution)/shard_map/pallas_call | solution.py:59
  768.8 9.5 %copy.72 = f32[8,256,1408]{2,1,0:T(8,128)} copy(f32[8,256,1408]{2,1,0:T(8,128)} %all-gather.17.cloned.1.call-done) | data formatting | bytes 23068672
  (139 shorter events, 129.1 us)
Async XLA Ops:
  7.2 59.9 %reduce-scatter.7.cloned.1.call-start = ((), (), s32[]{:S(2)}) async-start(), calls=%async_computation.6 | async-start | bytes 6488064 | tf_op jit(solution)/shard_map/reduce_scatter | solution.py:341
  28.6 115.8 %all-gather.7.cloned.1.call-start = ((), (), s32[]{:S(2)}) async-start(), calls=%async_computation.8 | async-start | bytes 6488064 | tf_op jit(solution)/shard_map/all_gather | solution.py:344
  72.4 116.9 %reduce-scatter.9.cloned.1.call-start = ((), (), s32[]{:S(2)}) async-start(), calls=%async_computation.7 | async-start | bytes 7208960 | tf_op jit(solution)/shard_map/reduce_scatter | solution.py:364
  78.2 48.2 %collective-permute-start = (f32[4,256,1408]{2,1,0:T(8,128)}, f32[4,256,1408]{2,1,0:T(8,128)}, u32[]{:S(2)}, u32[]{:S(2)}) collective-permute-start(f32[4,256,1408]{2,1,0:T(8,128)} %dynamic-slice_bitcast_fusion.1), channel_id=1, source_target_pairs={{0,1},{1,0},{2,3},{3,2},{4,5},{5,4},{6,7},{7,6},{8,9},{9,8},{10,11... | collective-permute-start | bytes 17301512 | tf_op jit(solution)/shard_map/ppermute | solution.py:354
  133.8 93.4 %all-gather.9.cloned.1.call-start = ((), (), s32[]{:S(2)}) async-start(), calls=%async_computation.9 | async-start | bytes 6488064 | tf_op jit(solution)/shard_map/all_gather | solution.py:344
  192.4 100.1 %reduce-scatter.13.cloned.1.call-start = ((), (), s32[]{:S(2)}) async-start(), calls=%async_computation.11 | async-start | bytes 3604480 | tf_op jit(solution)/shard_map/reduce_scatter | solution.py:364
  193.0 146.4 %reduce-scatter.11.cloned.1.call-start = ((), (), s32[]{:S(2)}) async-start(), calls=%async_computation.10 | async-start | bytes 6488064 | tf_op jit(solution)/shard_map/reduce_scatter | solution.py:341
  258.1 153.1 %all-gather.11.cloned.1.call-start = ((), (), s32[]{:S(2)}) async-start(), calls=%async_computation.12 | async-start | bytes 12976128 | tf_op jit(solution)/shard_map/all_gather | solution.py:344
  261.5 21.7 %collective-permute-start.6 = (f32[128,1408]{1,0:T(8,128)S(1)}, f32[128,1408]{1,0:T(8,128)S(1)}, u32[]{:S(2)}, u32[]{:S(2)}) collective-permute-start(f32[128,1408]{1,0:T(8,128)S(1)} %get-tuple-element.183), channel_id=1, source_target_pairs={{0,6},{1,7},{2,0},{3,1},{4,2},{5,3},{6,4},{7,5},{8,14},{9,15},{10,... | collective-permute-start | bytes 2162696 | tf_op jit(solution)/shard_map/ppermute | solution.py:351
  262.0 23.0 %collective-permute-start.3 = (f32[128,1408]{1,0:T(8,128)S(1)}, f32[128,1408]{1,0:T(8,128)S(1)}, u32[]{:S(2)}, u32[]{:S(2)}) collective-permute-start(f32[128,1408]{1,0:T(8,128)S(1)} %get-tuple-element.182), channel_id=1, source_target_pairs={{0,2},{1,3},{2,4},{3,5},{4,6},{5,7},{6,0},{7,1},{8,10},{9,11},{10,... | collective-permute-start | bytes 2162696 | tf_op jit(solution)/shard_map/ppermute | solution.py:351
  286.6 26.0 %collective-permute-start.4 = (f32[128,1408]{1,0:T(8,128)S(1)}, f32[128,1408]{1,0:T(8,128)}, u32[]{:S(2)}, u32[]{:S(2)}) collective-permute-start(f32[128,1408]{1,0:T(8,128)S(1)} %get-tuple-element.185), channel_id=1, source_target_pairs={{0,2},{1,3},{2,4},{3,5},{4,6},{5,7},{6,0},{7,1},{8,10},{9,11},{10,... | collective-permute-start | bytes 2162696 | tf_op jit(solution)/shard_map/ppermute | solution.py:351
  286.8 25.9 %collective-permute-start.7 = (f32[128,1408]{1,0:T(8,128)S(1)}, f32[128,1408]{1,0:T(8,128)}, u32[]{:S(2)}, u32[]{:S(2)}) collective-permute-start(f32[128,1408]{1,0:T(8,128)S(1)} %get-tuple-element.186), channel_id=1, source_target_pairs={{0,6},{1,7},{2,0},{3,1},{4,2},{5,3},{6,4},{7,5},{8,14},{9,15},{10,... | collective-permute-start | bytes 2162696 | tf_op jit(solution)/shard_map/ppermute | solution.py:351
  289.3 45.5 %collective-permute-start.5 = (f32[128,1408]{1,0:T(8,128)}, f32[128,1408]{1,0:T(8,128)}, u32[]{:S(2)}, u32[]{:S(2)}) collective-permute-start(f32[128,1408]{1,0:T(8,128)} %get-tuple-element.181), channel_id=1, source_target_pairs={{0,6},{1,7},{2,0},{3,1},{4,2},{5,3},{6,4},{7,5},{8,14},{9,15},{10,... | collective-permute-start | bytes 2162696 | tf_op jit(solution)/shard_map/ppermute | solution.py:351
  290.9 46.3 %collective-permute-start.8 = (f32[128,1408]{1,0:T(8,128)}, f32[128,1408]{1,0:T(8,128)}, u32[]{:S(2)}, u32[]{:S(2)}) collective-permute-start(f32[128,1408]{1,0:T(8,128)} %get-tuple-element.184), channel_id=1, source_target_pairs={{0,2},{1,3},{2,4},{3,5},{4,6},{5,7},{6,0},{7,1},{8,10},{9,11},{10,... | collective-permute-start | bytes 2162696 | tf_op jit(solution)/shard_map/ppermute | solution.py:351
  347.4 133.9 %reduce-scatter.15.cloned.1.call-start = ((), (), s32[]{:S(2)}) async-start(), calls=%async_computation.13 | async-start | bytes 6488064 | tf_op jit(solution)/shard_map/reduce_scatter | solution.py:341
  445.8 161.5 %all-gather.13.cloned.1.call-start = ((), (), s32[]{:S(2)}) async-start(), calls=%async_computation.14 | async-start | bytes 12976128 | tf_op jit(solution)/shard_map/all_gather | solution.py:344
  487.5 155.7 %all-gather.15.cloned.1.call-start = ((), (), s32[]{:S(2)}) async-start(), calls=%async_computation.15 | async-start | bytes 6488064 | tf_op jit(solution)/shard_map/all_gather | solution.py:344
  487.7 54.8 %collective-permute-start.10 = (f32[256,1408]{1,0:T(8,128)S(1)}, f32[256,1408]{1,0:T(8,128)}, u32[]{:S(2)}, u32[]{:S(2)}) collective-permute-start(f32[256,1408]{1,0:T(8,128)S(1)} %bitcast.122), channel_id=1, source_target_pairs={{0,2},{1,3},{2,4},{3,5},{4,6},{5,7},{6,0},{7,1},{8,10},{9,11},{10,... | collective-permute-start | bytes 4325384 | tf_op jit(solution)/shard_map/ppermute | solution.py:351
  488.7 62.0 %collective-permute-start.12 = (f32[256,1408]{1,0:T(8,128)S(1)}, f32[256,1408]{1,0:T(8,128)S(1)}, u32[]{:S(2)}, u32[]{:S(2)}) collective-permute-start(f32[256,1408]{1,0:T(8,128)S(1)} %bitcast.123), channel_id=1, source_target_pairs={{0,6},{1,7},{2,0},{3,1},{4,2},{5,3},{6,4},{7,5},{8,14},{9,15},{10,... | collective-permute-start | bytes 4325384 | tf_op jit(solution)/shard_map/ppermute | solution.py:351
  491.2 59.8 %collective-permute-start.9 = (f32[256,1408]{1,0:T(8,128)S(1)}, f32[256,1408]{1,0:T(8,128)}, u32[]{:S(2)}, u32[]{:S(2)}) collective-permute-start(f32[256,1408]{1,0:T(8,128)S(1)} %bitcast.124), channel_id=1, source_target_pairs={{0,1},{1,0},{2,3},{3,2},{4,5},{5,4},{6,7},{7,6},{8,9},{9,8},{10,11... | collective-permute-start | bytes 4325384 | tf_op jit(solution)/shard_map/ppermute | solution.py:354
  543.7 42.0 %collective-permute-start.11 = (f32[256,1408]{1,0:T(8,128)}, f32[256,1408]{1,0:T(8,128)S(1)}, u32[]{:S(2)}, u32[]{:S(2)}) collective-permute-start(f32[256,1408]{1,0:T(8,128)} %collective-permute-done.10), channel_id=1, source_target_pairs={{0,1},{1,0},{2,3},{3,2},{4,5},{5,4},{6,7},{7,6},{8,9},{9,8},{10,11... | collective-permute-start | bytes 4325384 | tf_op jit(solution)/shard_map/ppermute | solution.py:354
  550.8 34.8 %collective-permute-start.13 = (f32[256,1408]{1,0:T(8,128)S(1)}, f32[256,1408]{1,0:T(8,128)S(1)}, u32[]{:S(2)}, u32[]{:S(2)}) collective-permute-start(f32[256,1408]{1,0:T(8,128)S(1)} %collective-permute-done.12), channel_id=1, source_target_pairs={{0,1},{1,0},{2,3},{3,2},{4,5},{5,4},{6,7},{7,6},{8,9},{9,8},{10,11... | collective-permute-start | bytes 4325384 | tf_op jit(solution)/shard_map/ppermute | solution.py:354
  551.0 33.3 %collective-permute-start.15 = (f32[128,1408]{1,0:T(8,128)S(1)}, f32[128,1408]{1,0:T(8,128)S(1)}, u32[]{:S(2)}, u32[]{:S(2)}) collective-permute-start(f32[128,1408]{1,0:T(8,128)S(1)} %slice.65), channel_id=1, source_target_pairs={{0,6},{1,7},{2,0},{3,1},{4,2},{5,3},{6,4},{7,5},{8,14},{9,15},{10,... | collective-permute-start | bytes 2162696 | tf_op jit(solution)/shard_map/ppermute | solution.py:351
  554.4 30.4 %collective-permute-start.14 = (f32[128,1408]{1,0:T(8,128)S(1)}, f32[128,1408]{1,0:T(8,128)S(1)}, u32[]{:S(2)}, u32[]{:S(2)}) collective-permute-start(f32[128,1408]{1,0:T(8,128)S(1)} %slice.64), channel_id=1, source_target_pairs={{0,2},{1,3},{2,4},{3,5},{4,6},{5,7},{6,0},{7,1},{8,10},{9,11},{10,... | collective-permute-start | bytes 2162696 | tf_op jit(solution)/shard_map/ppermute | solution.py:351
  607.3 73.8 %reduce-scatter.17.cloned.1.call-start = ((), (), s32[]{:S(2)}) async-start(), calls=%async_computation.16 | async-start | bytes 6488064 | tf_op jit(solution)/shard_map/reduce_scatter | solution.py:341
  643.2 125.6 %all-gather.17.cloned.1.call-start = ((), (), s32[]{:S(2)}) async-start(), calls=%async_computation.17 | async-start | bytes 12976128 | tf_op jit(solution)/shard_map/all_gather | solution.py:344
  686.3 15.0 %collective-permute-start.18 = (bf16[176,1408]{1,0:T(8,128)(2,1)S(1)}, bf16[176,1408]{1,0:T(8,128)(2,1)S(1)}, u32[]{:S(2)}, u32[]{:S(2)}) collective-permute-start(bf16[176,1408]{1,0:T(8,128)(2,1)S(1)} %bitcast.135), channel_id=1, source_target_pairs={{0,2},{1,3},{2,4},{3,5},{4,6},{5,7},{6,0},{7,1},{8,10},{9,11},{10,... | collective-permute-start | bytes 1486856 | tf_op jit(solution)/shard_map/ppermute | solution.py:351
  687.3 21.0 %collective-permute-start.20 = (bf16[176,1408]{1,0:T(8,128)(2,1)S(1)}, bf16[176,1408]{1,0:T(8,128)(2,1)S(1)}, u32[]{:S(2)}, u32[]{:S(2)}) collective-permute-start(bf16[176,1408]{1,0:T(8,128)(2,1)S(1)} %bitcast.136), channel_id=1, source_target_pairs={{0,6},{1,7},{2,0},{3,1},{4,2},{5,3},{6,4},{7,5},{8,14},{9,15},{10,... | collective-permute-start | bytes 1486856 | tf_op jit(solution)/shard_map/ppermute | solution.py:351
  689.8 23.4 %collective-permute-start.17 = (bf16[176,1408]{1,0:T(8,128)(2,1)S(1)}, bf16[176,1408]{1,0:T(8,128)(2,1)S(1)}, u32[]{:S(2)}, u32[]{:S(2)}) collective-permute-start(bf16[176,1408]{1,0:T(8,128)(2,1)S(1)} %bitcast.137), channel_id=1, source_target_pairs={{0,1},{1,0},{2,3},{3,2},{4,5},{5,4},{6,7},{7,6},{8,9},{9,8},{10,11... | collective-permute-start | bytes 1486856 | tf_op jit(solution)/shard_map/ppermute | solution.py:354
  701.3 27.5 %collective-permute-start.19 = (bf16[176,1408]{1,0:T(8,128)(2,1)S(1)}, bf16[176,1408]{1,0:T(8,128)(2,1)S(1)}, u32[]{:S(2)}, u32[]{:S(2)}) collective-permute-start(bf16[176,1408]{1,0:T(8,128)(2,1)S(1)} %collective-permute-done.18), channel_id=1, source_target_pairs={{0,1},{1,0},{2,3},{3,2},{4,5},{5,4},{6,7},{7,6},{8,9},{9,8},{10,11... | collective-permute-start | bytes 1486856 | tf_op jit(solution)/shard_map/ppermute | solution.py:354
  708.3 20.5 %collective-permute-start.21 = (bf16[176,1408]{1,0:T(8,128)(2,1)S(1)}, bf16[176,1408]{1,0:T(8,128)(2,1)S(1)}, u32[]{:S(2)}, u32[]{:S(2)}) collective-permute-start(bf16[176,1408]{1,0:T(8,128)(2,1)S(1)} %collective-permute-done.20), channel_id=1, source_target_pairs={{0,1},{1,0},{2,3},{3,2},{4,5},{5,4},{6,7},{7,6},{8,9},{9,8},{10,11... | collective-permute-start | bytes 1486856 | tf_op jit(solution)/shard_map/ppermute | solution.py:354
  713.1 14.5 %collective-permute-start.22 = (bf16[88,1408]{1,0:T(8,128)(2,1)S(1)}, bf16[88,1408]{1,0:T(8,128)(2,1)S(1)}, u32[]{:S(2)}, u32[]{:S(2)}) collective-permute-start(bf16[88,1408]{1,0:T(8,128)(2,1)S(1)} %slice.67), channel_id=1, source_target_pairs={{0,2},{1,3},{2,4},{3,5},{4,6},{5,7},{6,0},{7,1},{8,10},{9,11},{10,... | collective-permute-start | bytes 743432 | tf_op jit(solution)/shard_map/ppermute | solution.py:351
  (9 other events, 122.4 us)
Sparse Core Ops, SparseCore 0:
  28.7 38.3 reduce-scatter.6
  72.5 36.2 all-gather.6
  134.0 55.2 reduce-scatter.8
  192.5 34.7 all-gather.8
  229.4 31.5 reduce-scatter.12
  263.8 75.6 reduce-scatter.10
  347.5 63.6 all-gather.10
  445.9 35.2 reduce-scatter.14
  487.6 97.5 all-gather.12
  607.4 35.7 all-gather.14
  646.0 34.9 reduce-scatter.16
  685.3 69.8 all-gather.16

commit v7 on v6

--- a/solution.py
+++ b/solution.py
@@ -416,16 +416,17 @@
         g_sums = core_sums(g_part)
         d_one = own(dy_one) + rms_pull(own(y_one), later(g_back, g_part).astype(F32))
         d_shard = d_one.astype(BF16)
-        mlp_held = mlp_grads(plan.after(d_shard), parts, dy_two, None, top, n_layers, None)
         g_sum = like_scatter(later(g_sums, d_shard))
         x_two_out = own(y_two)
         wo_all = ring_gather(w_o2[0], (dx,), (g_part,)).reshape(-1, width)
-        d_two, attn_held, last = own(dy_two), None, mlp_held[0]
+        d_two, attn_held, last, mlp_held = own(dy_two), None, g_sums, None
 
         for layer_pair in reversed(range(n_pairs)):
             s_one, s_two = saved_one[layer_pair], saved_two[layer_pair]
             mid, low = 2 * layer_pair + 1, 2 * layer_pair
-            g_part, normed, low_act, low_slope = mlp_forward(plan.after(last), s_one, w_in, w_out, low, keep=True)
+            g_part, normed, low_act, low_slope = mlp_forward(
+                plan.after(last, d_shard), s_one, w_in, w_out, low, keep=True
+            )
             d_one_bf = gather(d_shard, g_part)
             finish, chip_sums = ring_scatter(g_part)
             mid_back, attn_held, _ = attn_back(
@@ -437,7 +438,9 @@
             f_in = gather(f_shard)
             mid_sum = like_scatter(later(mid_sums, f_shard))
             _, mid_act, mid_slope = mlp_forward(plan.after(f_shard), s_one, w_in, w_out, mid, want_out=False, keep=True)
-            f_in = later(f_in, mid_slope)
+            if mlp_held is None:
+                mlp_held = mlp_grads(plan.after(mid_slope), parts, dy_two, None, top, n_layers, None)
+            f_in = later(f_in, mid_slope, mlp_held[0])
             f_back, attn_held, _ = attn_back(
                 plan, f_in, d_one_bf, w_t, w_o2, mid + 1, n_heads, n_layers, attn_held
             )

time: 792 us -> 788 us (level)
    all_gather x6, waiting for transfers between devices: 86.1 us -> 65.8 us  [gather(): return later(lax.all_gather(shard, 'tp', axis=0, tiled=True), *others)]
    ppermute x11, waiting for transfers between devices: 8.26 us -> 25.8 us  [swap(): lax.ppermute(value, 'tp', [(i, i + 1 - 2 * (i % CORES)) for i in range(n_...]
  transfers between devices with their start and end apart: 37 -> 37, of which waited for: 20 -> 20; matrix products, arithmetic and copies ran while one was open for 9% -> 9% of each run, Pallas kernels for 30% -> 31%
where the time goes in v7:
time: 788 us; the launch traced here: 782 us
  waiting for transfers between devices  318 us (40%)
  Pallas kernels  295 us (37%)
  other arithmetic  56.4 us (7%)
  local copies, waits for them, and re-layouts  49.8 us (6%)
  starting transfers between devices  48 us (6%)
  between operations  15.1 us (2%)
    pallas_call x14, Pallas kernels, call(): pl.pallas_call(body, grid_spec=pltpu.PrefetchScalarGridSpec(num_scalar_pr...  295 us
    ppermute x14, waiting for transfers between devices, shift(): return lax.ppermute(value, 'tp', pairs)  154 us
    reduce_scatter x4, waiting for transfers between devices, scatter(): return lax.psum_scatter(part, 'tp', scatter_dimension=0, tiled=True)  70.5 us
    all_gather x6, waiting for transfers between devices, gather(): return later(lax.all_gather(shard, 'tp', axis=0, tiled=True), *others)  65.8 us
    ppermute x11, waiting for transfers between devices, swap(): lax.ppermute(value, 'tp', [(i, i + 1 - 2 * (i % CORES)) for i in range(n_...  25.8 us
    ppermute x11, starting transfers between devices, swap(): lax.ppermute(value, 'tp', [(i, i + 1 - 2 * (i % CORES)) for i in range(n_...  25 us
    ppermute x14, starting transfers between devices, shift(): return lax.ppermute(value, 'tp', pairs)  20.3 us
  transfers between devices with their start and end apart: 37, of which 20 were waited for; matrix products, arithmetic and copies ran while one was open for 9% of the time, Pallas kernels for 31%

profile of v7, /device:TPU:113, one launch (start us, length us, event | category | flops | bytes accessed | tf_op | source)
XLA Modules:
  0.0 781.9 jit_solution(13132843666636247523)
XLA Ops:
  7.3 21.3 %shard_map.161 = (bf16[8,256,1408]{2,1,0:T(8,128)(2,1)}, bf16[8,256,1408]{2,1,0:T(8,128)(2,1)}, bf16[8,256,768]{2,1,0:T(8,128)(2,1)}, bf16[8,256,768]{2,1,0:T(8,128)(2,1)}) custom-call(s32[1]{0:T(128)} %bitcast.gate, f32[8,256,1408]{2,1,0:T(8,128)} %x_ref.3, f32[8,256,1408]{2,1,0:T(8,128)} %d_ref.3, bf16[3,1408,768]{2,1,0:T(8,128)(2,1)} %win_ref.11, ...), custom_call_target="tpu_custom_call" | custom-call | flops 13287555072 | bytes 17825792 | tf_op jit(solution)/shard_map/pallas_call | solution.py:59
  30.2 18.2 %shard_map.162 = f32[8,256,1408]{2,1,0:T(8,128)} custom-call(s32[1]{0:T(128)} %bitcast.gate, f32[8,256,1408]{2,1,0:T(8,128)} %x_ref.3, bf16[3,1408,768]{2,1,0:T(8,128)(2,1)} %win_ref.11, bf16[3,768,1408]{2,1,0:T(8,128)(2,1)} %wout_ref.5), custom_call_target="tpu_custom_call" | custom-call | flops 8858370048 | bytes 11534336 | tf_op jit(solution)/shard_map/pallas_call | solution.py:59
  48.5 18.6 %reduce-scatter.7.cloned.1.call-done = bf16[1,256,1408]{2,1,0:T(8,128)(2,1)} async-done(((bf16[8,256,1408]{2,1,0:T(8,128)(2,1)}), bf16[1,256,1408]{2,1,0:T(8,128)(2,1)}) %reduce-scatter.7.cloned.1.call-update) | async-done | bytes 720912 | tf_op jit(solution)/shard_map/reduce_scatter | solution.py:341
  80.6 10.6 %collective-permute-done = f32[4,256,1408]{2,1,0:T(8,128)} collective-permute-done((f32[4,256,1408]{2,1,0:T(8,128)}, f32[4,256,1408]{2,1,0:T(8,128)}, u32[]{:S(2)}, u32[]{:S(2)}) %collective-permute-start) | collective-permute-done | bytes 5767200 | tf_op jit(solution)/shard_map/ppermute | solution.py:354
  91.2 7.7 bitcast_add_fusion.1
  98.9 20.3 %shard_map.163 = (f32[8,256,1408]{2,1,0:T(8,128)}, bf16[8,256,1408]{2,1,0:T(8,128)(2,1)}, bf16[8,256,768]{2,1,0:T(8,128)(2,1)}, f32[8,256,768]{2,1,0:T(8,128)}) custom-call(s32[1]{0:T(128)} %bitcast.gate, f32[8,256,1408]{2,1,0:T(8,128)} %bitcast.117, bf16[3,1408,768]{2,1,0:T(8,128)(2,1)} %win_ref.11, bf16[3,768,1408]{2,1,0:T(8,128)(2,1)} %wout_ref.5), custom_call_target="tpu_custom_call" | custom-call | flops 8858370048 | bytes 26738688 | tf_op jit(solution)/shard_map/pallas_call | solution.py:59
  125.4 9.0 %collective-permute-done.1 = f32[4,256,1408]{2,1,0:T(8,128)} collective-permute-done((f32[4,256,1408]{2,1,0:T(8,128)}, f32[4,256,1408]{2,1,0:T(8,128)}, u32[]{:S(2)}, u32[]{:S(2)}) %collective-permute-start.1) | collective-permute-done | bytes 5767200 | tf_op jit(solution)/shard_map/ppermute | solution.py:354
  134.4 7.5 bitcast_add_fusion
  141.9 31.7 %shard_map.164 = (bf16[8,256,1408]{2,1,0:T(8,128)(2,1)}, f32[3,528,1408]{2,1,0:T(8,128)}, f32[3,176,1408]{2,1,0:T(8,128)}) custom-call(s32[1]{0:T(128)} %bitcast.gate, f32[8,256,1408]{2,1,0:T(8,128)} %bitcast.139, bf16[8,256,1408]{2,1,0:T(8,128)(2,1)} %all-gather.7.cloned.1.call-done.d_ref, bf16[3,528,1408]{2,1,0:T(8,128)(2,1)} %bitcast.131, ...), custom_call_target="tpu_custom_call" | custom-call | flops 12180258816 | bytes 17661952 | tf_op jit(solution)/shard_map/pallas_call | solution.py:59
  187.8 14.0 %shard_map.165 = (bf16[8,256,1408]{2,1,0:T(8,128)(2,1)}, bf16[8,256,768]{2,1,0:T(8,128)(2,1)}, f32[8,256,768]{2,1,0:T(8,128)}) custom-call(s32[1]{0:T(128)} %bitcast.gate, f32[8,256,1408]{2,1,0:T(8,128)} %bitcast.118, bf16[3,1408,768]{2,1,0:T(8,128)(2,1)} %win_ref.11), custom_call_target="tpu_custom_call" | custom-call | flops 4429185024 | bytes 15204352 | tf_op jit(solution)/shard_map/pallas_call | solution.py:59
  201.9 19.7 %shard_map.166 = (f32[3,1408,768]{2,1,0:T(8,128)}, f32[3,768,1408]{2,1,0:T(8,128)}) custom-call(s32[1]{0:T(128)} %bitcast.gate, bf16[8,256,1408]{2,1,0:T(8,128)(2,1)} %get-tuple-element.104.a_ref, bf16[8,256,768]{2,1,0:T(8,128)(2,1)} %get-tuple-element.105.act_ref, bf16[8,256,768]{2,1,0:T(8,128)(2,1)} %get-tuple-element.106.dh_ref, f32[8,256,1408]{2,1,0:T(8,128)} %d_ref.3), custom_call_target="tpu_custom_call" | custom-call | flops 8858370048 | bytes 25952256 | tf_op jit(solution)/shard_map/pallas_call | solution.py:59
  221.7 30.8 %shard_map.167 = (bf16[8,256,1408]{2,1,0:T(8,128)(2,1)}, f32[3,528,1408]{2,1,0:T(8,128)}, f32[3,176,1408]{2,1,0:T(8,128)}) custom-call(s32[1]{0:T(128)} %bitcast.gate, bf16[8,256,1408]{2,1,0:T(8,128)(2,1)} %all-gather.9.cloned.1.call-done.x_ref, ...), custom_call_target="tpu_custom_call", output_to_operand_aliasing={{1}: (5, {}), {2}: (6, {})} | custom-call | flops 12180258816 | bytes 17661952 | tf_op jit(solution)/shard_map/pallas_call | solution.py:59
  258.2 20.6 %collective-permute-done.6 = f32[128,1408]{1,0:T(8,128)S(1)} collective-permute-done((f32[128,1408]{1,0:T(8,128)S(1)}, f32[128,1408]{1,0:T(8,128)S(1)}, u32[]{:S(2)}, u32[]{:S(2)}) %collective-permute-start.6) | collective-permute-done | bytes 720928 | tf_op jit(solution)/shard_map/ppermute | solution.py:351
  291.5 18.2 %collective-permute-done.4 = f32[128,1408]{1,0:T(8,128)} collective-permute-done((f32[128,1408]{1,0:T(8,128)S(1)}, f32[128,1408]{1,0:T(8,128)}, u32[]{:S(2)}, u32[]{:S(2)}) %collective-permute-start.4) | collective-permute-done | bytes 720928 | tf_op jit(solution)/shard_map/ppermute | solution.py:351
  309.7 22.2 %collective-permute-done.5 = f32[128,1408]{1,0:T(8,128)} collective-permute-done((f32[128,1408]{1,0:T(8,128)}, f32[128,1408]{1,0:T(8,128)}, u32[]{:S(2)}, u32[]{:S(2)}) %collective-permute-start.5) | collective-permute-done | bytes 720928 | tf_op jit(solution)/shard_map/ppermute | solution.py:351
  344.4 63.2 %all-gather.11.cloned.1.call-done.d_ref = bf16[8,2,256,1408]{3,2,1,0:T(8,128)(2,1)} async-done(((bf16[1,2,256,1408]{3,2,1,0:T(8,128)(2,1)}), bf16[8,2,256,1408]{3,2,1,0:T(8,128)(2,1)}) %all-gather.11.cloned.1.call-update) | async-done | bytes 11534352 | tf_op jit(solution)/shard_map/all_gather | solution.py:344
  407.7 17.0 %shard_map.168 = (bf16[8,256,1408]{2,1,0:T(8,128)(2,1)}, bf16[8,256,768]{2,1,0:T(8,128)(2,1)}) custom-call(s32[1]{0:T(128)} %bitcast.gate, f32[8,256,768]{2,1,0:T(8,128)} %get-tuple-element.102.slope_ref, bf16[8,2,256,1408]{3,2,1,0:T(8,128)(2,1)} %all-gather.11.cloned.1.call-done.d_ref, bf16[3,1408,768]{2,1,0:T(8,128)(2,1)} %win_ref.11, ...), custom_call_target="tpu_custom_call" | custom-call | flops 8858370048 | bytes 8912896 | tf_op jit(solution)/shard_map/pallas_call | solution.py:59
  424.7 17.5 %shard_map.169 = (bf16[8,256,1408]{2,1,0:T(8,128)(2,1)}, bf16[8,256,768]{2,1,0:T(8,128)(2,1)}) custom-call(s32[1]{0:T(128)} %bitcast.gate, f32[8,256,768]{2,1,0:T(8,128)} %get-tuple-element.94.slope_ref, bf16[8,2,256,1408]{3,2,1,0:T(8,128)(2,1)} %all-gather.11.cloned.1.call-done.d_ref, bf16[3,1408,768]{2,1,0:T(8,128)(2,1)} %win_ref.11, ...), custom_call_target="tpu_custom_call" | custom-call | flops 8858370048 | bytes 8912896 | tf_op jit(solution)/shard_map/pallas_call | solution.py:59
  444.1 19.2 %shard_map.170 = (f32[3,1408,768]{2,1,0:T(8,128)}, f32[3,768,1408]{2,1,0:T(8,128)}) custom-call(s32[1]{0:T(128)} %bitcast.gate, bf16[8,256,1408]{2,1,0:T(8,128)(2,1)} %get-tuple-element.117.a_ref, bf16[8,256,768]{2,1,0:T(8,128)(2,1)} %get-tuple-element.118.act_ref, ...), custom_call_target="tpu_custom_call", output_to_operand_aliasing={{0}: (5, {}), {1}: (6, {})} | custom-call | flops 8858370048 | bytes 25952256 | tf_op jit(solution)/shard_map/pallas_call | solution.py:59
  463.3 14.4 %reduce-scatter.15.cloned.1.call-done = bf16[1,256,1408]{2,1,0:T(8,128)(2,1)} async-done(((bf16[8,256,1408]{2,1,0:T(8,128)(2,1)}), bf16[1,256,1408]{2,1,0:T(8,128)(2,1)}) %reduce-scatter.15.cloned.1.call-update) | async-done | bytes 720912 | tf_op jit(solution)/shard_map/reduce_scatter | solution.py:341
  497.1 41.4 %collective-permute-done.10 = f32[256,1408]{1,0:T(8,128)} collective-permute-done((f32[256,1408]{1,0:T(8,128)S(1)}, f32[256,1408]{1,0:T(8,128)}, u32[]{:S(2)}, u32[]{:S(2)}) %collective-permute-start.10) | collective-permute-done | bytes 1441824 | tf_op jit(solution)/shard_map/ppermute | solution.py:351
  539.7 7.0 collective-permute-start.11
  555.7 24.8 %collective-permute-done.15 = f32[128,1408]{1,0:T(8,128)S(1)} collective-permute-done((f32[128,1408]{1,0:T(8,128)S(1)}, f32[128,1408]{1,0:T(8,128)S(1)}, u32[]{:S(2)}, u32[]{:S(2)}) %collective-permute-start.15) | collective-permute-done | bytes 720928 | tf_op jit(solution)/shard_map/ppermute | solution.py:351
  587.8 15.6 %shard_map.171 = (bf16[176,2048]{1,0:T(8,128)(2,1)}, f32[8,256,1408]{2,1,0:T(8,128)}) custom-call(s32[1]{0:T(128)} %bitcast.gate, f32[8,256,1408]{2,1,0:T(8,128)} %bitcast_dynamic-update-slice_fusion.x_ref, bf16[3,528,1408]{2,1,0:T(8,128)(2,1)} %bitcast.133), custom_call_target="tpu_custom_call" | custom-call | flops 3045064704 | bytes 12255232 | tf_op jit(solution)/shard_map/pallas_call | solution.py:59
  603.8 33.0 %shard_map.172 = (bf16[8,256,1408]{2,1,0:T(8,128)(2,1)}, f32[3,528,1408]{2,1,0:T(8,128)}, f32[3,176,1408]{2,1,0:T(8,128)}, f32[8,256,1408]{2,1,0:T(8,128)}) custom-call(s32[1]{0:T(128)} %bitcast.gate, f32[8,256,1408]{2,1,0:T(8,128)} %get-tuple-element.196.x_ref, ...), custom_call_target="tpu_custom_call", output_to_operand_aliasing={{1}: (5, {}), {2}: (6, {})} | custom-call | flops 12180258816 | bytes 29196288 | tf_op jit(solution)/shard_map/pallas_call | solution.py:59
  639.7 37.5 %reduce-scatter.17.cloned.1.call-done = bf16[1,256,1408]{2,1,0:T(8,128)(2,1)} async-done(((bf16[8,256,1408]{2,1,0:T(8,128)(2,1)}), bf16[1,256,1408]{2,1,0:T(8,128)(2,1)}) %reduce-scatter.17.cloned.1.call-update) | async-done | bytes 720912 | tf_op jit(solution)/shard_map/reduce_scatter | solution.py:341
  688.5 9.0 %collective-permute-done.18 = bf16[176,1408]{1,0:T(8,128)(2,1)S(1)} collective-permute-done((bf16[176,1408]{1,0:T(8,128)(2,1)S(1)}, bf16[176,1408]{1,0:T(8,128)(2,1)S(1)}, u32[]{:S(2)}, u32[]{:S(2)}) %collective-permute-start.18) | collective-permute-done | bytes 495648 | tf_op jit(solution)/shard_map/ppermute | solution.py:351
  697.5 7.0 collective-permute-start.19
  709.4 11.0 %collective-permute-done.23 = bf16[88,1408]{1,0:T(8,128)(2,1)S(1)} collective-permute-done((bf16[88,1408]{1,0:T(8,128)(2,1)S(1)}, bf16[88,1408]{1,0:T(8,128)(2,1)S(1)}, u32[]{:S(2)}, u32[]{:S(2)}) %collective-permute-start.23) | collective-permute-done | bytes 247840 | tf_op jit(solution)/shard_map/ppermute | solution.py:351
  728.4 17.3 %shard_map.173 = f32[8,256,1408]{2,1,0:T(8,128)} custom-call(s32[1]{0:T(128)} %bitcast.gate, f32[8,256,1408]{2,1,0:T(8,128)} %bitcast.119, bf16[1408,2048]{1,0:T(8,128)(2,1)} %all-gather.15.cloned.1.call-done.h_ref, bf16[1408,1408]{1,0:T(8,128)(2,1)} %bitcast.126), custom_call_target="tpu_custom_call" | custom-call | flops 8120172544 | bytes 11534336 | tf_op jit(solution)/shard_map/pallas_call | solution.py:59
  745.8 19.2 %shard_map.174 = (f32[3,1408,768]{2,1,0:T(8,128)}, f32[3,768,1408]{2,1,0:T(8,128)}) custom-call(s32[1]{0:T(128)} %bitcast.gate, bf16[8,256,1408]{2,1,0:T(8,128)(2,1)} %get-tuple-element.117.a_ref, bf16[8,256,768]{2,1,0:T(8,128)(2,1)} %get-tuple-element.164.act_ref, ...), custom_call_target="tpu_custom_call", output_to_operand_aliasing={{0}: (5, {}), {1}: (6, {})} | custom-call | flops 8858370048 | bytes 25952256 | tf_op jit(solution)/shard_map/pallas_call | solution.py:59
  765.0 9.5 %copy.72 = f32[8,256,1408]{2,1,0:T(8,128)} copy(f32[8,256,1408]{2,1,0:T(8,128)} %all-gather.17.cloned.1.call-done) | data formatting | bytes 23068672
  (139 shorter events, 132.6 us)
Async XLA Ops:
  7.2 59.9 %reduce-scatter.7.cloned.1.call-start = ((), (), s32[]{:S(2)}) async-start(), calls=%async_computation.6 | async-start | bytes 6488064 | tf_op jit(solution)/shard_map/reduce_scatter | solution.py:341
  28.6 113.3 %all-gather.7.cloned.1.call-start = ((), (), s32[]{:S(2)}) async-start(), calls=%async_computation.8 | async-start | bytes 6488064 | tf_op jit(solution)/shard_map/all_gather | solution.py:344
  72.4 111.1 %reduce-scatter.9.cloned.1.call-start = ((), (), s32[]{:S(2)}) async-start(), calls=%async_computation.7 | async-start | bytes 7208960 | tf_op jit(solution)/shard_map/reduce_scatter | solution.py:364
  125.1 96.6 %all-gather.9.cloned.1.call-start = ((), (), s32[]{:S(2)}) async-start(), calls=%async_computation.9 | async-start | bytes 6488064 | tf_op jit(solution)/shard_map/all_gather | solution.py:344
  186.6 102.9 %reduce-scatter.13.cloned.1.call-start = ((), (), s32[]{:S(2)}) async-start(), calls=%async_computation.11 | async-start | bytes 3604480 | tf_op jit(solution)/shard_map/reduce_scatter | solution.py:364
  187.3 149.1 %reduce-scatter.11.cloned.1.call-start = ((), (), s32[]{:S(2)}) async-start(), calls=%async_computation.10 | async-start | bytes 6488064 | tf_op jit(solution)/shard_map/reduce_scatter | solution.py:341
  252.6 155.1 %all-gather.11.cloned.1.call-start = ((), (), s32[]{:S(2)}) async-start(), calls=%async_computation.12 | async-start | bytes 12976128 | tf_op jit(solution)/shard_map/all_gather | solution.py:344
  256.0 22.8 %collective-permute-start.6 = (f32[128,1408]{1,0:T(8,128)S(1)}, f32[128,1408]{1,0:T(8,128)S(1)}, u32[]{:S(2)}, u32[]{:S(2)}) collective-permute-start(f32[128,1408]{1,0:T(8,128)S(1)} %get-tuple-element.183), channel_id=1, source_target_pairs={{0,6},{1,7},{2,0},{3,1},{4,2},{5,3},{6,4},{7,5},{8,14},{9,15},{10,... | collective-permute-start | bytes 2162696 | tf_op jit(solution)/shard_map/ppermute | solution.py:351
  258.2 23.9 %collective-permute-start.3 = (f32[128,1408]{1,0:T(8,128)S(1)}, f32[128,1408]{1,0:T(8,128)S(1)}, u32[]{:S(2)}, u32[]{:S(2)}) collective-permute-start(f32[128,1408]{1,0:T(8,128)S(1)} %get-tuple-element.182), channel_id=1, source_target_pairs={{0,2},{1,3},{2,4},{3,5},{4,6},{5,7},{6,0},{7,1},{8,10},{9,11},{10,... | collective-permute-start | bytes 2162696 | tf_op jit(solution)/shard_map/ppermute | solution.py:351
  283.6 26.0 %collective-permute-start.4 = (f32[128,1408]{1,0:T(8,128)S(1)}, f32[128,1408]{1,0:T(8,128)}, u32[]{:S(2)}, u32[]{:S(2)}) collective-permute-start(f32[128,1408]{1,0:T(8,128)S(1)} %get-tuple-element.185), channel_id=1, source_target_pairs={{0,2},{1,3},{2,4},{3,5},{4,6},{5,7},{6,0},{7,1},{8,10},{9,11},{10,... | collective-permute-start | bytes 2162696 | tf_op jit(solution)/shard_map/ppermute | solution.py:351
  283.7 25.9 %collective-permute-start.7 = (f32[128,1408]{1,0:T(8,128)S(1)}, f32[128,1408]{1,0:T(8,128)}, u32[]{:S(2)}, u32[]{:S(2)}) collective-permute-start(f32[128,1408]{1,0:T(8,128)S(1)} %get-tuple-element.186), channel_id=1, source_target_pairs={{0,6},{1,7},{2,0},{3,1},{4,2},{5,3},{6,4},{7,5},{8,14},{9,15},{10,... | collective-permute-start | bytes 2162696 | tf_op jit(solution)/shard_map/ppermute | solution.py:351
  286.4 45.5 %collective-permute-start.5 = (f32[128,1408]{1,0:T(8,128)}, f32[128,1408]{1,0:T(8,128)}, u32[]{:S(2)}, u32[]{:S(2)}) collective-permute-start(f32[128,1408]{1,0:T(8,128)} %get-tuple-element.181), channel_id=1, source_target_pairs={{0,6},{1,7},{2,0},{3,1},{4,2},{5,3},{6,4},{7,5},{8,14},{9,15},{10,... | collective-permute-start | bytes 2162696 | tf_op jit(solution)/shard_map/ppermute | solution.py:351
  288.0 46.2 %collective-permute-start.8 = (f32[128,1408]{1,0:T(8,128)}, f32[128,1408]{1,0:T(8,128)}, u32[]{:S(2)}, u32[]{:S(2)}) collective-permute-start(f32[128,1408]{1,0:T(8,128)} %get-tuple-element.184), channel_id=1, source_target_pairs={{0,2},{1,3},{2,4},{3,5},{4,6},{5,7},{6,0},{7,1},{8,10},{9,11},{10,... | collective-permute-start | bytes 2162696 | tf_op jit(solution)/shard_map/ppermute | solution.py:351
  344.4 133.3 %reduce-scatter.15.cloned.1.call-start = ((), (), s32[]{:S(2)}) async-start(), calls=%async_computation.13 | async-start | bytes 6488064 | tf_op jit(solution)/shard_map/reduce_scatter | solution.py:341
  442.2 161.6 %all-gather.13.cloned.1.call-start = ((), (), s32[]{:S(2)}) async-start(), calls=%async_computation.14 | async-start | bytes 12976128 | tf_op jit(solution)/shard_map/all_gather | solution.py:344
  483.8 155.5 %all-gather.15.cloned.1.call-start = ((), (), s32[]{:S(2)}) async-start(), calls=%async_computation.15 | async-start | bytes 6488064 | tf_op jit(solution)/shard_map/all_gather | solution.py:344
  483.9 54.6 %collective-permute-start.10 = (f32[256,1408]{1,0:T(8,128)S(1)}, f32[256,1408]{1,0:T(8,128)}, u32[]{:S(2)}, u32[]{:S(2)}) collective-permute-start(f32[256,1408]{1,0:T(8,128)S(1)} %bitcast.122), channel_id=1, source_target_pairs={{0,2},{1,3},{2,4},{3,5},{4,6},{5,7},{6,0},{7,1},{8,10},{9,11},{10,... | collective-permute-start | bytes 4325384 | tf_op jit(solution)/shard_map/ppermute | solution.py:351
  484.9 61.9 %collective-permute-start.12 = (f32[256,1408]{1,0:T(8,128)S(1)}, f32[256,1408]{1,0:T(8,128)S(1)}, u32[]{:S(2)}, u32[]{:S(2)}) collective-permute-start(f32[256,1408]{1,0:T(8,128)S(1)} %bitcast.123), channel_id=1, source_target_pairs={{0,6},{1,7},{2,0},{3,1},{4,2},{5,3},{6,4},{7,5},{8,14},{9,15},{10,... | collective-permute-start | bytes 4325384 | tf_op jit(solution)/shard_map/ppermute | solution.py:351
  487.4 59.6 %collective-permute-start.9 = (f32[256,1408]{1,0:T(8,128)S(1)}, f32[256,1408]{1,0:T(8,128)}, u32[]{:S(2)}, u32[]{:S(2)}) collective-permute-start(f32[256,1408]{1,0:T(8,128)S(1)} %bitcast.124), channel_id=1, source_target_pairs={{0,1},{1,0},{2,3},{3,2},{4,5},{5,4},{6,7},{7,6},{8,9},{9,8},{10,11... | collective-permute-start | bytes 4325384 | tf_op jit(solution)/shard_map/ppermute | solution.py:354
  539.7 42.1 %collective-permute-start.11 = (f32[256,1408]{1,0:T(8,128)}, f32[256,1408]{1,0:T(8,128)S(1)}, u32[]{:S(2)}, u32[]{:S(2)}) collective-permute-start(f32[256,1408]{1,0:T(8,128)} %collective-permute-done.10), channel_id=1, source_target_pairs={{0,1},{1,0},{2,3},{3,2},{4,5},{5,4},{6,7},{7,6},{8,9},{9,8},{10,11... | collective-permute-start | bytes 4325384 | tf_op jit(solution)/shard_map/ppermute | solution.py:354
  546.8 35.0 %collective-permute-start.13 = (f32[256,1408]{1,0:T(8,128)S(1)}, f32[256,1408]{1,0:T(8,128)S(1)}, u32[]{:S(2)}, u32[]{:S(2)}) collective-permute-start(f32[256,1408]{1,0:T(8,128)S(1)} %collective-permute-done.12), channel_id=1, source_target_pairs={{0,1},{1,0},{2,3},{3,2},{4,5},{5,4},{6,7},{7,6},{8,9},{9,8},{10,11... | collective-permute-start | bytes 4325384 | tf_op jit(solution)/shard_map/ppermute | solution.py:354
  547.0 33.5 %collective-permute-start.15 = (f32[128,1408]{1,0:T(8,128)S(1)}, f32[128,1408]{1,0:T(8,128)S(1)}, u32[]{:S(2)}, u32[]{:S(2)}) collective-permute-start(f32[128,1408]{1,0:T(8,128)S(1)} %slice.65), channel_id=1, source_target_pairs={{0,6},{1,7},{2,0},{3,1},{4,2},{5,3},{6,4},{7,5},{8,14},{9,15},{10,... | collective-permute-start | bytes 2162696 | tf_op jit(solution)/shard_map/ppermute | solution.py:351
  550.4 30.6 %collective-permute-start.14 = (f32[128,1408]{1,0:T(8,128)S(1)}, f32[128,1408]{1,0:T(8,128)S(1)}, u32[]{:S(2)}, u32[]{:S(2)}) collective-permute-start(f32[128,1408]{1,0:T(8,128)S(1)} %slice.64), channel_id=1, source_target_pairs={{0,2},{1,3},{2,4},{3,5},{4,6},{5,7},{6,0},{7,1},{8,10},{9,11},{10,... | collective-permute-start | bytes 2162696 | tf_op jit(solution)/shard_map/ppermute | solution.py:351
  603.4 73.8 %reduce-scatter.17.cloned.1.call-start = ((), (), s32[]{:S(2)}) async-start(), calls=%async_computation.16 | async-start | bytes 6488064 | tf_op jit(solution)/shard_map/reduce_scatter | solution.py:341
  639.4 125.6 %all-gather.17.cloned.1.call-start = ((), (), s32[]{:S(2)}) async-start(), calls=%async_computation.17 | async-start | bytes 12976128 | tf_op jit(solution)/shard_map/all_gather | solution.py:344
  682.4 15.0 %collective-permute-start.18 = (bf16[176,1408]{1,0:T(8,128)(2,1)S(1)}, bf16[176,1408]{1,0:T(8,128)(2,1)S(1)}, u32[]{:S(2)}, u32[]{:S(2)}) collective-permute-start(bf16[176,1408]{1,0:T(8,128)(2,1)S(1)} %bitcast.135), channel_id=1, source_target_pairs={{0,2},{1,3},{2,4},{3,5},{4,6},{5,7},{6,0},{7,1},{8,10},{9,11},{10,... | collective-permute-start | bytes 1486856 | tf_op jit(solution)/shard_map/ppermute | solution.py:351
  683.4 21.0 %collective-permute-start.20 = (bf16[176,1408]{1,0:T(8,128)(2,1)S(1)}, bf16[176,1408]{1,0:T(8,128)(2,1)S(1)}, u32[]{:S(2)}, u32[]{:S(2)}) collective-permute-start(bf16[176,1408]{1,0:T(8,128)(2,1)S(1)} %bitcast.136), channel_id=1, source_target_pairs={{0,6},{1,7},{2,0},{3,1},{4,2},{5,3},{6,4},{7,5},{8,14},{9,15},{10,... | collective-permute-start | bytes 1486856 | tf_op jit(solution)/shard_map/ppermute | solution.py:351
  685.9 23.4 %collective-permute-start.17 = (bf16[176,1408]{1,0:T(8,128)(2,1)S(1)}, bf16[176,1408]{1,0:T(8,128)(2,1)S(1)}, u32[]{:S(2)}, u32[]{:S(2)}) collective-permute-start(bf16[176,1408]{1,0:T(8,128)(2,1)S(1)} %bitcast.137), channel_id=1, source_target_pairs={{0,1},{1,0},{2,3},{3,2},{4,5},{5,4},{6,7},{7,6},{8,9},{9,8},{10,11... | collective-permute-start | bytes 1486856 | tf_op jit(solution)/shard_map/ppermute | solution.py:354
  697.5 27.5 %collective-permute-start.19 = (bf16[176,1408]{1,0:T(8,128)(2,1)S(1)}, bf16[176,1408]{1,0:T(8,128)(2,1)S(1)}, u32[]{:S(2)}, u32[]{:S(2)}) collective-permute-start(bf16[176,1408]{1,0:T(8,128)(2,1)S(1)} %collective-permute-done.18), channel_id=1, source_target_pairs={{0,1},{1,0},{2,3},{3,2},{4,5},{5,4},{6,7},{7,6},{8,9},{9,8},{10,11... | collective-permute-start | bytes 1486856 | tf_op jit(solution)/shard_map/ppermute | solution.py:354
  704.4 20.5 %collective-permute-start.21 = (bf16[176,1408]{1,0:T(8,128)(2,1)S(1)}, bf16[176,1408]{1,0:T(8,128)(2,1)S(1)}, u32[]{:S(2)}, u32[]{:S(2)}) collective-permute-start(bf16[176,1408]{1,0:T(8,128)(2,1)S(1)} %collective-permute-done.20), channel_id=1, source_target_pairs={{0,1},{1,0},{2,3},{3,2},{4,5},{5,4},{6,7},{7,6},{8,9},{9,8},{10,11... | collective-permute-start | bytes 1486856 | tf_op jit(solution)/shard_map/ppermute | solution.py:354
  705.9 14.5 %collective-permute-start.23 = (bf16[88,1408]{1,0:T(8,128)(2,1)S(1)}, bf16[88,1408]{1,0:T(8,128)(2,1)S(1)}, u32[]{:S(2)}, u32[]{:S(2)}) collective-permute-start(bf16[88,1408]{1,0:T(8,128)(2,1)S(1)} %slice.68), channel_id=1, source_target_pairs={{0,6},{1,7},{2,0},{3,1},{4,2},{5,3},{6,4},{7,5},{8,14},{9,15},{10,... | collective-permute-start | bytes 743432 | tf_op jit(solution)/shard_map/ppermute | solution.py:351
  709.3 14.5 %collective-permute-start.22 = (bf16[88,1408]{1,0:T(8,128)(2,1)S(1)}, bf16[88,1408]{1,0:T(8,128)(2,1)S(1)}, u32[]{:S(2)}, u32[]{:S(2)}) collective-permute-start(bf16[88,1408]{1,0:T(8,128)(2,1)S(1)} %slice.67), channel_id=1, source_target_pairs={{0,2},{1,3},{2,4},{3,5},{4,6},{5,7},{6,0},{7,1},{8,10},{9,11},{10,... | collective-permute-start | bytes 743432 | tf_op jit(solution)/shard_map/ppermute | solution.py:351
  (9 other events, 120.6 us)
Sparse Core Ops, SparseCore 0:
  28.7 38.3 reduce-scatter.6
  72.5 36.2 all-gather.6
  125.2 55.3 reduce-scatter.8
  186.8 34.8 all-gather.8
  223.8 31.6 reduce-scatter.12
  258.2 75.8 reduce-scatter.10
  344.5 63.1 all-gather.10
  442.3 35.2 reduce-scatter.14
  484.0 97.4 all-gather.12
  603.6 35.6 all-gather.14
  642.2 34.9 reduce-scatter.16
  681.5 69.8 all-gather.16
